TPU v7x, 512 devices: a 4x2x32 block of a 4x16x32 slice. The times are simulated.
512 devices in a mesh: ens: 2 (over y), lon: 32 (over z), lat: 4 (over x), ch: 2 (over core).
Axes of the slice: x: 4, y: 2, z: 32, core: 2. Of those that a mesh axis runs over, the one named last changes fastest.
The devices are a block of a 4x16x32 slice.
Arguments:
- input_field: bfloat16 [512, 1024, 128], P(('ens', 'lat', 'ch'), 'lon'), parts along dimension 0, may hold values from -6 to 6
- encoder_filter: bfloat16 [256, 4, 5], P(('lat', 'ch')), may hold values from -2.6875 to 2.6875
- row_owner: int32 [512], P(('ens', 'lat', 'ch')), parts along dimension 0, may hold values from 0 to 127, as said below
- encoder_weight: bfloat16 [512, 256], replicated, may hold values from -0.25 to 0.25
- disco_basis: bfloat16 [128, 4, 3, 17], P(('lat', 'ch')), may hold values from -1.5 to 1.5
- row_widths: int32 [128], P(('lat', 'ch')), may hold values from 1 to 8, as said below
- block_weights: bfloat16 [2, 1024, 256], replicated, may hold values from -0.1875 to 0.1875
- cotangent: bfloat16 [256, 512, 256], P(('ens', 'lat', 'ch'), 'lon'), parts along dimension 0, may hold values from -6 to 6
Outputs:
- state_out: bfloat16 [256, 512, 256], P(('ens', 'lat', 'ch'), 'lon'), parts along dimension 0
- latent_grad: bfloat16 [256, 512, 256], P(('ens', 'lat', 'ch'), 'lon'), parts along dimension 0
- block_grads: float32 [4, 1024, 256], P('ens', None, 'ch'), parts along dimension 0
- encoder_grad: float32 [1024, 256], P('ens', 'ch'), parts along dimension 0
There are 2 independent parts, one for each index of `ens`. A program takes and returns all parts, laid end to end along the dimension named above; an argument that names none is the same for every part. Nothing has to cross between parts.
Inputs may be any that keep to these rules, and one draw needn't show every extreme that they name: `row_owner`: input row p feeds latent row (p - 1) // 2, p // 2 or (p + 1) // 2, and every latent row is fed by 1 to 3 input rows. `row_widths`: the first and last rows have 8.
All inputs are finite; a program needn't handle non-finite values.
Results may differ from a plain program's by a relative error of at most 0.014.
Values may be sent and summed in bfloat16 or wider, within the bound.
No kernel may reach another device: no remote copies, remote signals or barrier semaphores. Data moves between devices by JAX's collectives and lax.ppermute only.
A program may use at most 64 MiB of HBM per device.

v0:
```python
import math

import jax
import jax.numpy as jnp
from jax import lax
from jax.sharding import PartitionSpec as P

REACH = 8
TAP_REACH = 2


def passed_along(value, axis, steps):
    count = lax.axis_size(axis)
    pairs = [(source, (source + steps) % count) for source in range(count)]
    return lax.ppermute(value, axis, pairs)


def from_behind(block, axis, distance):
    devices = range(lax.axis_size(axis))
    route = [(i - distance, i) for i in devices if i - distance in devices]
    return lax.ppermute(block, axis, route)


def padded(block, sides, width, periodic):
    for axis, dim in sides:
        count = lax.axis_size(axis)
        forward = [(i, i + 1) for i in range(count - 1)]
        if periodic:
            forward.append((count - 1, 0))
        backward = [(target, source) for source, target in forward]
        low = lax.ppermute(
            lax.slice_in_dim(block, block.shape[dim] - width, None, axis=dim), axis, forward
        )
        high = lax.ppermute(lax.slice_in_dim(block, 0, width, axis=dim), axis, backward)
        block = jnp.concatenate([low, block, high], axis=dim)
    return block


def with_halo(value, sides, width):
    edges = {}
    for axis, dim in sides:
        peers, length = (lax.axis_size(axis), value.shape[dim])
        up = [(i, (i + 1) % peers) for i in range(peers - 1)]
        last = lax.slice_in_dim(value, length - width, length, axis=dim)
        initial = lax.slice_in_dim(value, 0, width, axis=dim)
        edges[dim] = (
            lax.ppermute(last, axis, up),
            lax.ppermute(initial, axis, [(b, a) for a, b in up]),
        )
    done = []
    for _, dim in sides:
        low, high = edges[dim]
        around = [(width, width) if d in done else (0, 0) for d in range(value.ndim)]
        value = jnp.concatenate([jnp.pad(low, around), value, jnp.pad(high, around)], axis=dim)
        done.append(dim)
    return value


def rows_for(lines, peers):
    spare = -lines.shape[0] % peers
    if not spare:
        return lines
    return jnp.concatenate([lines, jnp.zeros((spare, *lines.shape[1:]), lines.dtype)])


def from_everyone(value, axis):
    peers = lax.axis_size(axis)
    return lax.all_to_all(
        jnp.broadcast_to(value[None], (peers, *value.shape)), axis, 0, 0, tiled=True
    )


def laid_out(tiles, dim):
    tiles = jnp.moveaxis(tiles, 0, dim)
    lengths = tiles.shape
    return tiles.reshape(*lengths[:dim], lengths[dim] * lengths[dim + 1], *lengths[dim + 2 :])


def whole_of(value, axes, dim):
    far, near = axes
    initial = from_everyone(value, far)
    tiles = jnp.swapaxes(from_everyone(initial, near), 0, 1)
    return laid_out(tiles.reshape(-1, *value.shape), dim)


def in_blocks(value, dim, peers):
    lengths = value.shape
    tiles = value.reshape(*lengths[:dim], peers, lengths[dim] // peers, *lengths[dim + 1 :])
    return jnp.moveaxis(tiles, dim, 0)


def sum_at_owner(value, axis, dim):
    tiles = in_blocks(value, dim, lax.axis_size(axis))
    arrived = lax.all_to_all(tiles, axis, split_axis=0, concat_axis=0, tiled=True)
    return arrived.astype(jnp.float32).sum(axis=0)


def sum_in_two_steps(value, axes, dim):
    far, near = axes
    own = sum_at_owner(in_blocks(value, dim, lax.axis_size(far)), near, dim + 1)
    return jnp.sum(
        lax.all_to_all(own.astype(jnp.bfloat16), far, 0, 0, tiled=True).astype(jnp.float32), axis=0
    )


def sum_by_parts(value, axes):
    lines = value.reshape(-1, value.shape[-1])
    padded = rows_for(lines, lax.axis_size(axes[0]) * lax.axis_size(axes[1]))
    whole = whole_of(sum_in_two_steps(padded, axes, 0).astype(jnp.bfloat16), axes, 0)
    return lax.slice_in_dim(whole, 0, len(lines)).reshape(value.shape).astype(jnp.float32)


def add_edges(middle, to_first, to_last):
    row_count = middle.shape[0]
    rest_pads = [(0, 0)] * (middle.ndim - 1)
    lower = jnp.pad(to_first, [(0, row_count - 1)] + rest_pads)
    upper = jnp.pad(to_last, [(row_count - 1, 0)] + rest_pads)
    return middle + lower + upper


def apply_basis(banded, extended, rows_dev):
    accumulated = None
    for shift_row in range(3):
        term = jnp.einsum(
            "ikjq,iqc->ijkc",
            banded[:, :, shift_row],
            extended[shift_row : shift_row + rows_dev],
            preferred_element_type=jnp.float32,
        )
        accumulated = term if accumulated is None else accumulated + term
    return accumulated


def spread_basis(banded, errors):
    pieces = [
        jnp.einsum(
            "ikjq,ijkc->iqc", banded[:, :, shift_row], errors, preferred_element_type=jnp.float32
        )
        for shift_row in range(3)
    ]
    first = jnp.pad(pieces[0], ((0, 2), (0, 0), (0, 0)))
    second = jnp.pad(pieces[1], ((1, 1), (0, 0), (0, 0)))
    third = jnp.pad(pieces[2], ((2, 0), (0, 0), (0, 0)))
    return first + second + third


def return_rims(spread, cols_dev):
    left_rim = spread[:, :REACH]
    right_rim = spread[:, REACH + cols_dev :]
    interior = spread[:, REACH : REACH + cols_dev]
    from_east = passed_along(left_rim.astype(jnp.bfloat16), "lon", -1).astype(left_rim.dtype)
    from_west = passed_along(right_rim.astype(jnp.bfloat16), "lon", 1).astype(right_rim.dtype)
    interior = interior + jnp.pad(from_west, ((0, 0), (0, cols_dev - REACH), (0, 0)))
    interior = interior + jnp.pad(from_east, ((0, 0), (cols_dev - REACH, 0), (0, 0)))
    row_total = interior.shape[0]
    from_above = from_behind(interior[0:1], ("lat", "ch"), -1)
    from_below = from_behind(interior[row_total - 1 :], ("lat", "ch"), 1)
    return add_edges(interior[1 : row_total - 1], from_below, from_above)


def per_device(
    input_field,
    encoder_filter,
    row_owner,
    encoder_weight,
    disco_basis,
    row_widths,
    block_weights,
    cotangent,
):
    rows_in, cols_in, in_width = input_field.shape
    rows_dev = rows_in // 2
    cols_dev = cols_in // 2
    basis_count = encoder_filter.shape[1]
    tap_count = encoder_filter.shape[2]
    channels = block_weights.shape[2]
    layers = block_weights.shape[0]
    cell_count = rows_dev * cols_dev
    extended_in = padded(input_field, (("lon", 1),), TAP_REACH, True)
    filter_values = encoder_filter.astype(jnp.float32)
    accumulated = jnp.zeros((rows_in, cols_dev, basis_count, in_width), jnp.float32)
    for tap_index in range(tap_count):
        sampled = extended_in[:, tap_index : tap_index + cols_in : 2, :]
        accumulated = (
            accumulated
            + sampled[:, :, None, :].astype(jnp.float32)
            * filter_values[:, None, :, tap_index, None]
        )
    filtered_in = accumulated.astype(jnp.bfloat16).reshape(
        rows_in, cols_dev * basis_count * in_width
    )
    first_row = lax.axis_index(("lat", "ch")) * rows_dev
    relative = row_owner - first_row + 1
    selector = (relative[None, :] == jnp.arange(rows_dev + 2, dtype=jnp.int32)[:, None]).astype(
        jnp.bfloat16
    )
    summed = jnp.dot(selector, filtered_in, preferred_element_type=jnp.float32)
    from_above = from_behind(summed[0:1].astype(jnp.bfloat16), ("lat", "ch"), -1).astype(
        jnp.float32
    )
    from_below = from_behind(summed[rows_dev + 1 :].astype(jnp.bfloat16), ("lat", "ch"), 1).astype(
        jnp.float32
    )
    regridded = add_edges(summed[1 : rows_dev + 1], from_below, from_above)
    latent_in = regridded.astype(jnp.bfloat16).reshape(cell_count, basis_count * in_width)
    current = jnp.dot(latent_in, encoder_weight, preferred_element_type=jnp.float32).astype(
        jnp.bfloat16
    )
    current = current.reshape(rows_dev, cols_dev, channels)
    offsets = jnp.abs(jnp.arange(2 * REACH + 1, dtype=jnp.int32) - REACH)
    keep = offsets[None, :] <= row_widths[:, None]
    masked = jnp.where(keep[:, None, None, :], disco_basis, jnp.zeros_like(disco_basis))
    ext_cols = cols_dev + 2 * REACH
    differences = (
        jnp.arange(ext_cols, dtype=jnp.int32)[None, :]
        - jnp.arange(cols_dev, dtype=jnp.int32)[:, None]
    )
    placement = (
        differences[:, :, None] == jnp.arange(2 * REACH + 1, dtype=jnp.int32)[None, None, :]
    ).astype(jnp.bfloat16)
    banded = jnp.einsum(
        "ikrt,jqt->ikrjq", masked, placement, preferred_element_type=jnp.float32
    ).astype(jnp.bfloat16)
    saved = []
    for layer_index in range(layers):
        rows_ext = with_halo(current, ((("lat", "ch"), 0),), 1)
        extended = padded(rows_ext, (("lon", 1),), REACH, True)
        features = (
            apply_basis(banded, extended, rows_dev)
            .astype(jnp.bfloat16)
            .reshape(cell_count, basis_count * channels)
        )
        preact = jnp.dot(features, block_weights[layer_index], preferred_element_type=jnp.float32)
        current = (
            current.astype(jnp.float32) + jax.nn.silu(preact).reshape(rows_dev, cols_dev, channels)
        ).astype(jnp.bfloat16)
        saved.append((features, preact))
    gradient = cotangent
    weight_terms = [None] * layers
    for layer_index in reversed(range(layers)):
        features, preact = saved[layer_index]
        sigma = jax.nn.sigmoid(preact)
        upstream = gradient.reshape(cell_count, channels).astype(jnp.float32)
        act_grad = (upstream * sigma * (1.0 + preact * (1.0 - sigma))).astype(jnp.bfloat16)
        weight_terms[layer_index] = lax.dot_general(
            features, act_grad, (((0,), (0,)), ((), ())), preferred_element_type=jnp.float32
        )
        errors = lax.dot_general(
            act_grad,
            block_weights[layer_index],
            (((1,), (1,)), ((), ())),
            preferred_element_type=jnp.float32,
        )
        errors = errors.astype(jnp.bfloat16).reshape(rows_dev, cols_dev, basis_count, channels)
        spread = spread_basis(banded, errors)
        returned = return_rims(spread, cols_dev)
        gradient = (gradient.astype(jnp.float32) + returned).astype(jnp.bfloat16)
    encoder_term = lax.dot_general(
        latent_in,
        gradient.reshape(cell_count, channels),
        (((0,), (0,)), ((), ())),
        preferred_element_type=jnp.float32,
    )
    block_stack = jnp.concatenate(weight_terms, axis=0)
    own_width = channels // lax.axis_size("ch")
    block_sum, encoder_sum = (
        sum_by_parts(block_stack.astype(jnp.bfloat16), ("lon", ("lat", "ch"))),
        sum_by_parts(encoder_term.astype(jnp.bfloat16), ("lon", ("lat", "ch"))),
    )
    first_col = lax.axis_index("ch") * own_width
    block_sum = lax.dynamic_slice_in_dim(block_sum, first_col, own_width, 1)
    encoder_sum = lax.dynamic_slice_in_dim(encoder_sum, first_col, own_width, 1)
    cells_total = cell_count * lax.axis_size("lon") * lax.axis_size(("lat", "ch"))
    normalizer = 1.0 / math.sqrt(cells_total)
    block_grads = (block_sum * normalizer).reshape(layers, basis_count * channels, own_width)
    encoder_grad = encoder_sum * normalizer
    return (current, gradient, block_grads, encoder_grad)


def solution(mesh):
    placed = (
        P(("ens", "lat", "ch"), "lon", None),
        P(("lat", "ch"), None, None),
        P(("ens", "lat", "ch")),
        P(),
        P(("lat", "ch"), None, None, None),
        P(("lat", "ch")),
        P(),
        P(("ens", "lat", "ch"), "lon", None),
    )
    return jax.shard_map(
        per_device,
        mesh=mesh,
        in_specs=placed,
        out_specs=(
            P(("ens", "lat", "ch"), "lon", None),
            P(("ens", "lat", "ch"), "lon", None),
            P("ens", None, "ch"),
            P("ens", "ch"),
        ),
        check_vma=False,
    )
```

profile of v0, /device:TPU:40, one launch (start us, length us, event | category | flops | bytes accessed | tf_op | source)
XLA Modules:
  0.0 341.4 jit_solution(5924152707104150749)
XLA Ops:
  0.6 0.9 fusion.64
  1.6 4.7 %collective-permute-start = (bf16[32,2,128]{2,1,0:T(2,128)(2,1)S(1)}, bf16[32,2,128]{2,1,0:T(2,128)(2,1)S(1)}, u32[]{:S(2)}, u32[]{:S(2)}) collective-permute-start(bf16[32,2,128]{2,1,0:T(2,128)(2,1)S(1)} %get-tuple-element.23), channel_id=1, source_target_pairs={{0,8},{8,16},{16,24},{24,32},{32,40},{40,48},{48,56},{56,64},{64,7... | collective-permute-start | bytes 49160 | tf_op jit(solution)/shard_map/ppermute | solution.py:31
  6.3 42.6 %collective-permute-start.1 = (bf16[32,2,128]{2,1,0:T(2,128)(2,1)S(1)}, bf16[32,2,128]{2,1,0:T(2,128)(2,1)S(1)}, u32[]{:S(2)}, u32[]{:S(2)}) collective-permute-start(bf16[32,2,128]{2,1,0:T(2,128)(2,1)S(1)} %get-tuple-element.24), channel_id=1, source_target_pairs={{8,0},{16,8},{24,16},{32,24},{40,32},{48,40},{56,48},{64,56},{72,6... | collective-permute-start | bytes 49160 | tf_op jit(solution)/shard_map/ppermute | solution.py:34
  48.9 0.7 convert_element_type.170
  49.6 0.7 broadcast_compare_fusion
  50.3 0.8 select_bitcast_fusion
  51.2 0.7 subtract_add_fusion
  51.8 1.8 slice.167
  54.2 1.1 pad_maximum_fusion.1
  57.2 1.0 add_convert_fusion
  59.0 1.6 collective-permute-start.2
  60.6 1.3 collective-permute-start.3
  61.9 3.4 %collective-permute-done.3 = bf16[1,8192]{1,0:T(2,128)(2,1)S(1)} collective-permute-done((bf16[1,8192]{1,0:T(2,128)(2,1)S(1)}, bf16[1,8192]{1,0:T(2,128)(2,1)S(1)}, u32[]{:S(2)}, u32[]{:S(2)}) %collective-permute-start.3) | collective-permute-done | bytes 16416 | tf_op jit(solution)/shard_map/ppermute | solution.py:21
  65.8 4.6 %collective-permute-start.4 = (bf16[1,16,256]{2,1,0:T(8,128)(2,1)S(1)}, bf16[1,16,256]{2,1,0:T(8,128)(2,1)S(1)}, u32[]{:S(2)}, u32[]{:S(2)}) collective-permute-start(bf16[1,16,256]{2,1,0:T(8,128)(2,1)S(1)} %get-tuple-element.31), channel_id=1, source_target_pairs={{0,1},{1,2},{2,3},{3,4},{4,5},{5,6},{6,7},{8,9},{9,10},{10,11},{11... | collective-permute-start | bytes 24584 | tf_op jit(solution)/shard_map/ppermute | solution.py:47
  70.4 1.3 collective-permute-start.5
  72.1 1.4 collective-permute-done.5
  73.6 2.0 collective-permute-start.6
  75.5 5.2 %collective-permute-start.7 = (bf16[18,8,256]{2,1,0:T(8,128)(2,1)S(1)}, bf16[18,8,256]{2,1,0:T(8,128)(2,1)S(1)}, u32[]{:S(2)}, u32[]{:S(2)}) collective-permute-start(bf16[18,8,256]{2,1,0:T(8,128)(2,1)S(1)} %get-tuple-element.28), channel_id=1, source_target_pairs={{8,0},{16,8},{24,16},{32,24},{40,32},{48,40},{56,48},{64,56},{72,6... | collective-permute-start | bytes 221192 | tf_op jit(solution)/shard_map/ppermute | solution.py:34
  81.0 1.6 collective-permute-done.7
  84.5 1.0 fusion.37
  85.5 2.7 collective-permute-start.8
  88.3 1.3 collective-permute-start.9
  89.6 2.7 collective-permute-done.9
  92.3 2.0 collective-permute-start.10
  94.3 5.6 %collective-permute-start.11 = (bf16[18,8,256]{2,1,0:T(8,128)(2,1)S(1)}, bf16[18,8,256]{2,1,0:T(8,128)(2,1)S(1)}, u32[]{:S(2)}, u32[]{:S(2)}) collective-permute-start(bf16[18,8,256]{2,1,0:T(8,128)(2,1)S(1)} %get-tuple-element.26), channel_id=1, source_target_pairs={{8,0},{16,8},{24,16},{32,24},{40,32},{48,40},{56,48},{64,56},{72,6... | collective-permute-start | bytes 221192 | tf_op jit(solution)/shard_map/ppermute | solution.py:34
  100.3 1.6 collective-permute-done.11
  103.4 1.1 fusion.35
  104.5 0.7 copy-done.3
  106.9 2.1 collective-permute-start.12
  109.0 5.5 %collective-permute-start.13 = (bf16[18,8,256]{2,1,0:T(8,128)(2,1)S(1)}, bf16[18,8,256]{2,1,0:T(8,128)(2,1)S(1)}, u32[]{:S(2)}, u32[]{:S(2)}) collective-permute-start(bf16[18,8,256]{2,1,0:T(8,128)(2,1)S(1)} %get-tuple-element.20), channel_id=1, source_target_pairs={{0,248},{8,0},{16,8},{24,16},{32,24},{40,32},{48,40},{56,48},{64,5... | collective-permute-start | bytes 221192 | tf_op jit(solution)/shard_map/ppermute | solution.py:15
  115.1 1.8 collective-permute-done.13
  116.9 2.3 collective-permute-start.14
  119.3 1.3 collective-permute-start.15
  120.6 3.5 %collective-permute-done.15 = f32[1,16,256]{2,1,0:T(8,128)S(1)} collective-permute-done((f32[1,16,256]{2,1,0:T(8,128)S(1)}, f32[1,16,256]{2,1,0:T(8,128)S(1)}, u32[]{:S(2)}, u32[]{:S(2)}) %collective-permute-start.15) | collective-permute-done | bytes 16416 | tf_op jit(solution)/shard_map/ppermute | solution.py:21
  124.2 1.1 convolution_convert_fusion.3
  125.4 1.4 reshape.138
  127.9 2.1 collective-permute-start.16
  129.9 5.6 %collective-permute-start.17 = (bf16[18,8,256]{2,1,0:T(8,128)(2,1)S(1)}, bf16[18,8,256]{2,1,0:T(8,128)(2,1)S(1)}, u32[]{:S(2)}, u32[]{:S(2)}) collective-permute-start(bf16[18,8,256]{2,1,0:T(8,128)(2,1)S(1)} %get-tuple-element.16), channel_id=1, source_target_pairs={{0,248},{8,0},{16,8},{24,16},{32,24},{40,32},{48,40},{56,48},{64,5... | collective-permute-start | bytes 221192 | tf_op jit(solution)/shard_map/ppermute | solution.py:15
  135.9 1.6 collective-permute-done.17
  137.6 3.6 %collective-permute-start.18 = (f32[1,16,256]{2,1,0:T(8,128)S(1)}, f32[1,16,256]{2,1,0:T(8,128)S(1)}, u32[]{:S(2)}, u32[]{:S(2)}) collective-permute-start(f32[1,16,256]{2,1,0:T(8,128)S(1)} %get-tuple-element.13), channel_id=1, source_target_pairs={{0,1},{1,2},{2,3},{3,4},{4,5},{5,6},{6,7},{8,9},{9,10},{10,11},{11... | collective-permute-start | bytes 49160 | tf_op jit(solution)/shard_map/ppermute | solution.py:21
  141.2 1.3 collective-permute-start.19
  142.5 2.2 collective-permute-done.19
  145.1 0.9 copy.242
  146.0 5.6 %all-to-all-start.4 = ((bf16[8,32,2,256]{3,2,1,0:T(2,128)(2,1)}), bf16[8,32,2,256]{3,2,1,0:T(2,128)(2,1)S(1)}, u32[]{:S(2)}, u32[]{:S(2)}) async-start(bf16[8,32,2,256]{3,2,1,0:T(2,128)(2,1)} %bitcast.140), calls=%async_computation.4 | async-start | bytes 524288 | tf_op jit(solution)/shard_map/all_to_all | solution.py:94
  151.9 7.1 %all-to-all-done.4 = bf16[8,32,2,256]{3,2,1,0:T(2,128)(2,1)S(1)} async-done(((bf16[8,32,2,256]{3,2,1,0:T(2,128)(2,1)}), bf16[8,32,2,256]{3,2,1,0:T(2,128)(2,1)S(1)}, u32[]{:S(2)}, u32[]{:S(2)}) %all-to-all-start.4) | async-done | bytes 262176 | tf_op jit(solution)/shard_map/all_to_all | solution.py:94
  159.1 0.9 reduce_sum.50
  159.9 9.9 %all-to-all-start.5 = ((bf16[32,2,256]{2,1,0:T(2,128)(2,1)}), bf16[32,2,256]{2,1,0:T(2,128)(2,1)S(1)}, u32[]{:S(2)}, u32[]{:S(2)}) async-start(bf16[32,2,256]{2,1,0:T(2,128)(2,1)} %reduce_sum.50), calls=%async_computation.5 | async-start | bytes 65536 | tf_op jit(solution)/shard_map/all_to_all | solution.py:102
  170.3 1.0 copy.241
  171.4 21.0 %all-to-all-done.5 = bf16[32,2,256]{2,1,0:T(2,128)(2,1)S(1)} async-done(((bf16[32,2,256]{2,1,0:T(2,128)(2,1)}), bf16[32,2,256]{2,1,0:T(2,128)(2,1)S(1)}, u32[]{:S(2)}, u32[]{:S(2)}) %all-to-all-start.5) | async-done | bytes 32800 | tf_op jit(solution)/shard_map/all_to_all | solution.py:102
  192.3 3.8 %all-to-all-start = ((bf16[8,32,8,256]{3,2,1,0:T(8,128)(2,1)}), bf16[8,32,8,256]{3,2,1,0:T(8,128)(2,1)S(1)}, u32[]{:S(2)}, u32[]{:S(2)}) async-start(bf16[8,32,8,256]{3,2,1,0:T(8,128)(2,1)} %bitcast.139), calls=%async_computation | async-start | bytes 2097152 | tf_op jit(solution)/shard_map/all_to_all | solution.py:94
  196.2 15.7 %all-to-all-done = bf16[8,32,8,256]{3,2,1,0:T(8,128)(2,1)S(1)} async-done(((bf16[8,32,8,256]{3,2,1,0:T(8,128)(2,1)}), bf16[8,32,8,256]{3,2,1,0:T(8,128)(2,1)S(1)}, u32[]{:S(2)}, u32[]{:S(2)}) %all-to-all-start) | async-done | bytes 1048608 | tf_op jit(solution)/shard_map/all_to_all | solution.py:94
  212.5 4.8 %all-to-all-start.6 = ((bf16[32,2,256]{2,1,0:T(2,128)(2,1)}), bf16[32,2,256]{2,1,0:T(2,128)(2,1)S(1)}, u32[]{:S(2)}, u32[]{:S(2)}) async-start(bf16[32,2,256]{2,1,0:T(2,128)(2,1)} %broadcast_in_dim.22), calls=%async_computation.6 | async-start | bytes 65536 | tf_op jit(solution)/shard_map/all_to_all | solution.py:68
  217.4 22.2 %all-to-all-done.6 = bf16[32,2,256]{2,1,0:T(2,128)(2,1)S(1)} async-done(((bf16[32,2,256]{2,1,0:T(2,128)(2,1)}), bf16[32,2,256]{2,1,0:T(2,128)(2,1)S(1)}, u32[]{:S(2)}, u32[]{:S(2)}) %all-to-all-start.6) | async-done | bytes 32800 | tf_op jit(solution)/shard_map/all_to_all | solution.py:68
  239.6 33.5 %all_to_all.40 = bf16[32,8,256]{2,1,0:T(8,128)(2,1)S(1)} all-to-all(bf16[32,8,256]{2,1,0:T(8,128)(2,1)S(1)} %reduce_sum.48), channel_id=1, replica_groups=mesh['ens'=2,'lon'=32,'lat'=4,'ch'=2] {'lon'}, dimensions={0} | all-to-all | bytes 262144 | tf_op jit(solution)/shard_map/all_to_all | solution.py:102
  273.1 0.8 broadcast_in_dim.23
  273.9 3.7 %all-to-all-start.7 = ((bf16[8,32,2,256]{3,2,1,0:T(2,128)(2,1)}), bf16[8,32,2,256]{3,2,1,0:T(2,128)(2,1)S(1)}, u32[]{:S(2)}, u32[]{:S(2)}) async-start(bf16[8,32,2,256]{3,2,1,0:T(2,128)(2,1)} %broadcast_in_dim.23), calls=%async_computation.7 | async-start | bytes 524288 | tf_op jit(solution)/shard_map/all_to_all | solution.py:68
  277.7 7.2 %all-to-all-done.7 = bf16[8,32,2,256]{3,2,1,0:T(2,128)(2,1)S(1)} async-done(((bf16[8,32,2,256]{3,2,1,0:T(2,128)(2,1)}), bf16[8,32,2,256]{3,2,1,0:T(2,128)(2,1)S(1)}, u32[]{:S(2)}, u32[]{:S(2)}) %all-to-all-start.7) | async-done | bytes 262176 | tf_op jit(solution)/shard_map/all_to_all | solution.py:68
  285.0 34.6 %all_to_all.41 = bf16[32,8,256]{2,1,0:T(8,128)(2,1)S(1)} all-to-all(bf16[32,8,256]{2,1,0:T(8,128)(2,1)S(1)} %broadcast_in_dim.20), channel_id=1, replica_groups=mesh['ens'=2,'lon'=32,'lat'=4,'ch'=2] {'lon'}, dimensions={0} | all-to-all | bytes 262144 | tf_op jit(solution)/shard_map/all_to_all | solution.py:68
  319.6 1.0 broadcast_in_dim.21
  320.6 3.8 %all-to-all-start.3 = ((bf16[8,32,8,256]{3,2,1,0:T(8,128)(2,1)}), bf16[8,32,8,256]{3,2,1,0:T(8,128)(2,1)S(1)}, u32[]{:S(2)}, u32[]{:S(2)}) async-start(bf16[8,32,8,256]{3,2,1,0:T(8,128)(2,1)} %broadcast_in_dim.21), calls=%async_computation.3 | async-start | bytes 2097152 | tf_op jit(solution)/shard_map/all_to_all | solution.py:68
  324.4 0.7 add_convert_fusion.1
  325.9 0.7 dynamic-slice_multiply_fusion.1
  326.6 13.4 %all-to-all-done.3 = bf16[8,32,8,256]{3,2,1,0:T(8,128)(2,1)S(1)} async-done(((bf16[8,32,8,256]{3,2,1,0:T(8,128)(2,1)}), bf16[8,32,8,256]{3,2,1,0:T(8,128)(2,1)S(1)}, u32[]{:S(2)}, u32[]{:S(2)}) %all-to-all-start.3) | async-done | bytes 1048608 | tf_op jit(solution)/shard_map/all_to_all | solution.py:68
  340.3 1.0 dynamic-slice_multiply_fusion
  (107 shorter events, 15.1 us)
Async XLA Ops:
  0.6 65.0 %copy-start = (bf16[512,256]{1,0:T(8,128)(2,1)S(1)}, bf16[512,256]{1,0:T(8,128)(2,1)}, u32[]{:S(2)}) copy-start(bf16[512,256]{1,0:T(8,128)(2,1)} %param.11) | copy-start | bytes 786436
  1.6 52.5 %collective-permute-start = (bf16[32,2,128]{2,1,0:T(2,128)(2,1)S(1)}, bf16[32,2,128]{2,1,0:T(2,128)(2,1)S(1)}, u32[]{:S(2)}, u32[]{:S(2)}) collective-permute-start(bf16[32,2,128]{2,1,0:T(2,128)(2,1)S(1)} %get-tuple-element.23), channel_id=1, source_target_pairs={{0,8},{8,16},{16,24},{24,32},{32,40},{40,48},{48,56},{56,64},{64,7... | collective-permute-start | bytes 49160 | tf_op jit(solution)/shard_map/ppermute | solution.py:31
  6.3 47.8 %collective-permute-start.1 = (bf16[32,2,128]{2,1,0:T(2,128)(2,1)S(1)}, bf16[32,2,128]{2,1,0:T(2,128)(2,1)S(1)}, u32[]{:S(2)}, u32[]{:S(2)}) collective-permute-start(bf16[32,2,128]{2,1,0:T(2,128)(2,1)S(1)} %get-tuple-element.24), channel_id=1, source_target_pairs={{8,0},{16,8},{24,16},{32,24},{40,32},{48,40},{56,48},{64,56},{72,6... | collective-permute-start | bytes 49160 | tf_op jit(solution)/shard_map/ppermute | solution.py:34
  59.0 2.9 collective-permute-start.2
  60.6 4.8 %collective-permute-start.3 = (bf16[1,8192]{1,0:T(2,128)(2,1)S(1)}, bf16[1,8192]{1,0:T(2,128)(2,1)S(1)}, u32[]{:S(2)}, u32[]{:S(2)}) collective-permute-start(bf16[1,8192]{1,0:T(2,128)(2,1)S(1)} %get-tuple-element.12), channel_id=1, source_target_pairs={{1,0},{2,1},{3,2},{4,3},{5,4},{6,5},{7,6},{9,8},{10,9},{11,10},{12... | collective-permute-start | bytes 49160 | tf_op jit(solution)/shard_map/ppermute | solution.py:21
  65.8 6.2 %collective-permute-start.4 = (bf16[1,16,256]{2,1,0:T(8,128)(2,1)S(1)}, bf16[1,16,256]{2,1,0:T(8,128)(2,1)S(1)}, u32[]{:S(2)}, u32[]{:S(2)}) collective-permute-start(bf16[1,16,256]{2,1,0:T(8,128)(2,1)S(1)} %get-tuple-element.31), channel_id=1, source_target_pairs={{0,1},{1,2},{2,3},{3,4},{4,5},{5,6},{6,7},{8,9},{9,10},{10,11},{11... | collective-permute-start | bytes 24584 | tf_op jit(solution)/shard_map/ppermute | solution.py:47
  70.4 3.1 collective-permute-start.5
  73.6 7.5 %collective-permute-start.6 = (bf16[18,8,256]{2,1,0:T(8,128)(2,1)S(1)}, bf16[18,8,256]{2,1,0:T(8,128)(2,1)S(1)}, u32[]{:S(2)}, u32[]{:S(2)}) collective-permute-start(bf16[18,8,256]{2,1,0:T(8,128)(2,1)S(1)} %get-tuple-element.27), channel_id=1, source_target_pairs={{0,8},{8,16},{16,24},{24,32},{32,40},{40,48},{48,56},{56,64},{64,7... | collective-permute-start | bytes 221192 | tf_op jit(solution)/shard_map/ppermute | solution.py:31
  75.5 7.1 %collective-permute-start.7 = (bf16[18,8,256]{2,1,0:T(8,128)(2,1)S(1)}, bf16[18,8,256]{2,1,0:T(8,128)(2,1)S(1)}, u32[]{:S(2)}, u32[]{:S(2)}) collective-permute-start(bf16[18,8,256]{2,1,0:T(8,128)(2,1)S(1)} %get-tuple-element.28), channel_id=1, source_target_pairs={{8,0},{16,8},{24,16},{32,24},{40,32},{48,40},{56,48},{64,56},{72,6... | collective-permute-start | bytes 221192 | tf_op jit(solution)/shard_map/ppermute | solution.py:34
  83.3 1.2 copy-start.1
  85.5 4.1 %collective-permute-start.8 = (bf16[1,16,256]{2,1,0:T(8,128)(2,1)S(1)}, bf16[1,16,256]{2,1,0:T(8,128)(2,1)S(1)}, u32[]{:S(2)}, u32[]{:S(2)}) collective-permute-start(bf16[1,16,256]{2,1,0:T(8,128)(2,1)S(1)} %get-tuple-element.29), channel_id=1, source_target_pairs={{0,1},{1,2},{2,3},{3,4},{4,5},{5,6},{6,7},{8,9},{9,10},{10,11},{11... | collective-permute-start | bytes 24584 | tf_op jit(solution)/shard_map/ppermute | solution.py:47
  88.3 4.0 %collective-permute-start.9 = (bf16[1,16,256]{2,1,0:T(8,128)(2,1)S(1)}, bf16[1,16,256]{2,1,0:T(8,128)(2,1)S(1)}, u32[]{:S(2)}, u32[]{:S(2)}) collective-permute-start(bf16[1,16,256]{2,1,0:T(8,128)(2,1)S(1)} %get-tuple-element.30), channel_id=1, source_target_pairs={{1,0},{2,1},{3,2},{4,3},{5,4},{6,5},{7,6},{9,8},{10,9},{11,10},{12... | collective-permute-start | bytes 24584 | tf_op jit(solution)/shard_map/ppermute | solution.py:48
  92.3 8.0 %collective-permute-start.10 = (bf16[18,8,256]{2,1,0:T(8,128)(2,1)S(1)}, bf16[18,8,256]{2,1,0:T(8,128)(2,1)S(1)}, u32[]{:S(2)}, u32[]{:S(2)}) collective-permute-start(bf16[18,8,256]{2,1,0:T(8,128)(2,1)S(1)} %get-tuple-element.25), channel_id=1, source_target_pairs={{0,8},{8,16},{16,24},{24,32},{32,40},{40,48},{48,56},{56,64},{64,7... | collective-permute-start | bytes 221192 | tf_op jit(solution)/shard_map/ppermute | solution.py:31
  94.3 7.6 %collective-permute-start.11 = (bf16[18,8,256]{2,1,0:T(8,128)(2,1)S(1)}, bf16[18,8,256]{2,1,0:T(8,128)(2,1)S(1)}, u32[]{:S(2)}, u32[]{:S(2)}) collective-permute-start(bf16[18,8,256]{2,1,0:T(8,128)(2,1)S(1)} %get-tuple-element.26), channel_id=1, source_target_pairs={{8,0},{16,8},{24,16},{32,24},{40,32},{48,40},{56,48},{64,56},{72,6... | collective-permute-start | bytes 221192 | tf_op jit(solution)/shard_map/ppermute | solution.py:34
  102.5 0.9 copy-start.8
  104.5 0.7 copy-start.3
  106.7 17.4 %copy-start.9 = (bf16[16,16,256]{2,1,0:T(8,128)(2,1)S(1)}, bf16[16,16,256]{2,1,0:T(8,128)(2,1)}, u32[]{:S(2)}) copy-start(bf16[16,16,256]{2,1,0:T(8,128)(2,1)} %param.15) | copy-start | bytes 393220
  106.7 17.5 %copy-start.7 = (f32[256,256]{1,0:T(8,128)S(1)}, f32[256,256]{1,0:T(8,128)}, u32[]{:S(2)}) copy-start(f32[256,256]{1,0:T(8,128)} %get-tuple-element.41) | copy-start | bytes 786436
  106.7 17.6 %copy-start.2 = (bf16[2,1024,256]{2,1,0:T(8,128)(2,1)S(1)}, bf16[2,1024,256]{2,1,0:T(8,128)(2,1)}, u32[]{:S(2)}) copy-start(bf16[2,1024,256]{2,1,0:T(8,128)(2,1)} %param.14) | copy-start | bytes 3145732
  106.9 8.2 %collective-permute-start.12 = (bf16[18,8,256]{2,1,0:T(8,128)(2,1)S(1)}, bf16[18,8,256]{2,1,0:T(8,128)(2,1)S(1)}, u32[]{:S(2)}, u32[]{:S(2)}) collective-permute-start(bf16[18,8,256]{2,1,0:T(8,128)(2,1)S(1)} %get-tuple-element.19), channel_id=1, source_target_pairs={{0,8},{8,16},{16,24},{24,32},{32,40},{40,48},{48,56},{56,64},{64,7... | collective-permute-start | bytes 221192 | tf_op jit(solution)/shard_map/ppermute | solution.py:15
  109.0 7.9 %collective-permute-start.13 = (bf16[18,8,256]{2,1,0:T(8,128)(2,1)S(1)}, bf16[18,8,256]{2,1,0:T(8,128)(2,1)S(1)}, u32[]{:S(2)}, u32[]{:S(2)}) collective-permute-start(bf16[18,8,256]{2,1,0:T(8,128)(2,1)S(1)} %get-tuple-element.20), channel_id=1, source_target_pairs={{0,248},{8,0},{16,8},{24,16},{32,24},{40,32},{48,40},{56,48},{64,5... | collective-permute-start | bytes 221192 | tf_op jit(solution)/shard_map/ppermute | solution.py:15
  116.9 3.7 %collective-permute-start.14 = (f32[1,16,256]{2,1,0:T(8,128)S(1)}, f32[1,16,256]{2,1,0:T(8,128)S(1)}, u32[]{:S(2)}, u32[]{:S(2)}) collective-permute-start(f32[1,16,256]{2,1,0:T(8,128)S(1)} %get-tuple-element.17), channel_id=1, source_target_pairs={{0,1},{1,2},{2,3},{3,4},{4,5},{5,6},{6,7},{8,9},{9,10},{10,11},{11... | collective-permute-start | bytes 49160 | tf_op jit(solution)/shard_map/ppermute | solution.py:21
  119.3 4.8 %collective-permute-start.15 = (f32[1,16,256]{2,1,0:T(8,128)S(1)}, f32[1,16,256]{2,1,0:T(8,128)S(1)}, u32[]{:S(2)}, u32[]{:S(2)}) collective-permute-start(f32[1,16,256]{2,1,0:T(8,128)S(1)} %get-tuple-element.18), channel_id=1, source_target_pairs={{1,0},{2,1},{3,2},{4,3},{5,4},{6,5},{7,6},{9,8},{10,9},{11,10},{12... | collective-permute-start | bytes 49160 | tf_op jit(solution)/shard_map/ppermute | solution.py:21
  127.8 23.7 %copy-start.4 = (bf16[256,256]{1,0:T(8,128)(2,1)S(1)}, bf16[256,256]{1,0:T(8,128)(2,1)}, u32[]{:S(2)}) copy-start(bf16[256,256]{1,0:T(8,128)(2,1)} %copy-done.3) | copy-start | bytes 393220
  127.9 8.1 %collective-permute-start.16 = (bf16[18,8,256]{2,1,0:T(8,128)(2,1)S(1)}, bf16[18,8,256]{2,1,0:T(8,128)(2,1)S(1)}, u32[]{:S(2)}, u32[]{:S(2)}) collective-permute-start(bf16[18,8,256]{2,1,0:T(8,128)(2,1)S(1)} %get-tuple-element.15), channel_id=1, source_target_pairs={{0,8},{8,16},{16,24},{24,32},{32,40},{40,48},{48,56},{56,64},{64,7... | collective-permute-start | bytes 221192 | tf_op jit(solution)/shard_map/ppermute | solution.py:15
  129.9 7.6 %collective-permute-start.17 = (bf16[18,8,256]{2,1,0:T(8,128)(2,1)S(1)}, bf16[18,8,256]{2,1,0:T(8,128)(2,1)S(1)}, u32[]{:S(2)}, u32[]{:S(2)}) collective-permute-start(bf16[18,8,256]{2,1,0:T(8,128)(2,1)S(1)} %get-tuple-element.16), channel_id=1, source_target_pairs={{0,248},{8,0},{16,8},{24,16},{32,24},{40,32},{48,40},{56,48},{64,5... | collective-permute-start | bytes 221192 | tf_op jit(solution)/shard_map/ppermute | solution.py:15
  137.6 4.9 %collective-permute-start.18 = (f32[1,16,256]{2,1,0:T(8,128)S(1)}, f32[1,16,256]{2,1,0:T(8,128)S(1)}, u32[]{:S(2)}, u32[]{:S(2)}) collective-permute-start(f32[1,16,256]{2,1,0:T(8,128)S(1)} %get-tuple-element.13), channel_id=1, source_target_pairs={{0,1},{1,2},{2,3},{3,4},{4,5},{5,6},{6,7},{8,9},{9,10},{10,11},{11... | collective-permute-start | bytes 49160 | tf_op jit(solution)/shard_map/ppermute | solution.py:21
  141.2 3.5 %collective-permute-start.19 = (f32[1,16,256]{2,1,0:T(8,128)S(1)}, f32[1,16,256]{2,1,0:T(8,128)S(1)}, u32[]{:S(2)}, u32[]{:S(2)}) collective-permute-start(f32[1,16,256]{2,1,0:T(8,128)S(1)} %get-tuple-element.14), channel_id=1, source_target_pairs={{1,0},{2,1},{3,2},{4,3},{5,4},{6,5},{7,6},{9,8},{10,9},{11,10},{12... | collective-permute-start | bytes 49160 | tf_op jit(solution)/shard_map/ppermute | solution.py:21
  144.7 25.6 %copy-start.5 = (bf16[16,16,256]{2,1,0:T(8,128)(2,1)}, bf16[16,16,256]{2,1,0:T(8,128)(2,1)S(1)}, u32[]{:S(2)}) copy-start(bf16[16,16,256]{2,1,0:T(8,128)(2,1)S(1)} %fusion.26) | copy-start | bytes 393220
  146.0 13.1 %all-to-all-start.4 = ((bf16[8,32,2,256]{3,2,1,0:T(2,128)(2,1)}), bf16[8,32,2,256]{3,2,1,0:T(2,128)(2,1)S(1)}, u32[]{:S(2)}, u32[]{:S(2)}) async-start(bf16[8,32,2,256]{3,2,1,0:T(2,128)(2,1)} %bitcast.140), calls=%async_computation.4 | async-start | bytes 524288 | tf_op jit(solution)/shard_map/all_to_all | solution.py:94
  159.9 32.4 %all-to-all-start.5 = ((bf16[32,2,256]{2,1,0:T(2,128)(2,1)}), bf16[32,2,256]{2,1,0:T(2,128)(2,1)S(1)}, u32[]{:S(2)}, u32[]{:S(2)}) async-start(bf16[32,2,256]{2,1,0:T(2,128)(2,1)} %reduce_sum.50), calls=%async_computation.5 | async-start | bytes 65536 | tf_op jit(solution)/shard_map/all_to_all | solution.py:102
  192.3 19.5 %all-to-all-start = ((bf16[8,32,8,256]{3,2,1,0:T(8,128)(2,1)}), bf16[8,32,8,256]{3,2,1,0:T(8,128)(2,1)S(1)}, u32[]{:S(2)}, u32[]{:S(2)}) async-start(bf16[8,32,8,256]{3,2,1,0:T(8,128)(2,1)} %bitcast.139), calls=%async_computation | async-start | bytes 2097152 | tf_op jit(solution)/shard_map/all_to_all | solution.py:94
  212.5 27.1 %all-to-all-start.6 = ((bf16[32,2,256]{2,1,0:T(2,128)(2,1)}), bf16[32,2,256]{2,1,0:T(2,128)(2,1)S(1)}, u32[]{:S(2)}, u32[]{:S(2)}) async-start(bf16[32,2,256]{2,1,0:T(2,128)(2,1)} %broadcast_in_dim.22), calls=%async_computation.6 | async-start | bytes 65536 | tf_op jit(solution)/shard_map/all_to_all | solution.py:68
  273.9 50.4 %copy-start.6 = (f32[256,256]{1,0:T(8,128)S(1)}, f32[256,256]{1,0:T(8,128)}, u32[]{:S(2)}) copy-start(f32[256,256]{1,0:T(8,128)} %get-tuple-element.22) | copy-start | bytes 786436
  273.9 11.0 %all-to-all-start.7 = ((bf16[8,32,2,256]{3,2,1,0:T(2,128)(2,1)}), bf16[8,32,2,256]{3,2,1,0:T(2,128)(2,1)S(1)}, u32[]{:S(2)}, u32[]{:S(2)}) async-start(bf16[8,32,2,256]{3,2,1,0:T(2,128)(2,1)} %broadcast_in_dim.23), calls=%async_computation.7 | async-start | bytes 524288 | tf_op jit(solution)/shard_map/all_to_all | solution.py:68
  320.6 19.5 %all-to-all-start.3 = ((bf16[8,32,8,256]{3,2,1,0:T(8,128)(2,1)}), bf16[8,32,8,256]{3,2,1,0:T(8,128)(2,1)S(1)}, u32[]{:S(2)}, u32[]{:S(2)}) async-start(bf16[8,32,8,256]{3,2,1,0:T(8,128)(2,1)} %broadcast_in_dim.21), calls=%async_computation.3 | async-start | bytes 2097152 | tf_op jit(solution)/shard_map/all_to_all | solution.py:68
where the time goes:
time: 343 us; the launch traced here: 341 us
  starting transfers between devices  130 us (38%)
  waiting for transfers between devices  108 us (31%)
  blocking collectives  68.1 us (20%)
  local copies, waits for them, and re-layouts  15 us (4%)
  other arithmetic  10.1 us (3%)
  matrix products  8.67 us (3%)
    ppermute x3, starting transfers between devices, padded(): lax.ppermute(lax.slice_in_dim(block, 0, width, axis=dim), axis, backward)  53.4 us
    all_to_all x3, waiting for transfers between devices, from_everyone(): lax.all_to_all(jnp.broadcast_to(value[None], (peers, *value.shape)), axis...  42.9 us
    all_to_all x1, blocking collectives, from_everyone(): lax.all_to_all(jnp.broadcast_to(value[None], (peers, *value.shape)), axis...  34.6 us
    all_to_all x1, blocking collectives, sum_in_two_steps(): lax.all_to_all(own.astype(jnp.bfloat16), far, 0, 0, tiled=True)  33.5 us
    all_to_all x2, waiting for transfers between devices, sum_at_owner(): lax.all_to_all(tiles, axis, split_axis=0, concat_axis=0, tiled=True)  22.8 us
    all_to_all x1, waiting for transfers between devices, sum_in_two_steps(): lax.all_to_all(own.astype(jnp.bfloat16), far, 0, 0, tiled=True)  21 us
    ppermute x4, starting transfers between devices, passed_along(): return lax.ppermute(value, axis, pairs)  15.3 us
    all_to_all x3, starting transfers between devices, from_everyone(): lax.all_to_all(jnp.broadcast_to(value[None], (peers, *value.shape)), axis...  12.3 us
  transfers between devices with their start and end apart: 26, of which 19 were waited for; matrix products, arithmetic and copies ran while one was open for 3% of the time, Pallas kernels for 0%

commit v1 on v0

--- a/solution.py
+++ b/solution.py
@@ -56,58 +56,46 @@
     return value
 
 
-def rows_for(lines, peers):
-    spare = -lines.shape[0] % peers
-    if not spare:
-        return lines
-    return jnp.concatenate([lines, jnp.zeros((spare, *lines.shape[1:]), lines.dtype)])
-
-
-def from_everyone(value, axis):
-    peers = lax.axis_size(axis)
-    return lax.all_to_all(
-        jnp.broadcast_to(value[None], (peers, *value.shape)), axis, 0, 0, tiled=True
-    )
-
-
-def laid_out(tiles, dim):
-    tiles = jnp.moveaxis(tiles, 0, dim)
-    lengths = tiles.shape
-    return tiles.reshape(*lengths[:dim], lengths[dim] * lengths[dim + 1], *lengths[dim + 2 :])
-
-
-def whole_of(value, axes, dim):
-    far, near = axes
-    initial = from_everyone(value, far)
-    tiles = jnp.swapaxes(from_everyone(initial, near), 0, 1)
-    return laid_out(tiles.reshape(-1, *value.shape), dim)
-
-
-def in_blocks(value, dim, peers):
-    lengths = value.shape
-    tiles = value.reshape(*lengths[:dim], peers, lengths[dim] // peers, *lengths[dim + 1 :])
-    return jnp.moveaxis(tiles, dim, 0)
-
-
-def sum_at_owner(value, axis, dim):
-    tiles = in_blocks(value, dim, lax.axis_size(axis))
-    arrived = lax.all_to_all(tiles, axis, split_axis=0, concat_axis=0, tiled=True)
-    return arrived.astype(jnp.float32).sum(axis=0)
-
-
-def sum_in_two_steps(value, axes, dim):
-    far, near = axes
-    own = sum_at_owner(in_blocks(value, dim, lax.axis_size(far)), near, dim + 1)
-    return jnp.sum(
-        lax.all_to_all(own.astype(jnp.bfloat16), far, 0, 0, tiled=True).astype(jnp.float32), axis=0
-    )
-
-
-def sum_by_parts(value, axes):
-    lines = value.reshape(-1, value.shape[-1])
-    padded = rows_for(lines, lax.axis_size(axes[0]) * lax.axis_size(axes[1]))
-    whole = whole_of(sum_in_two_steps(padded, axes, 0).astype(jnp.bfloat16), axes, 0)
-    return lax.slice_in_dim(whole, 0, len(lines)).reshape(value.shape).astype(jnp.float32)
+def near_and_far(count, near):
+    near_groups = [[first + step for step in range(near)] for first in range(0, count, near)]
+    far_groups = [[first + near * step for step in range(count // near)] for first in range(near)]
+    return near_groups, far_groups
+
+
+def radix_of(count):
+    near = 1
+    while near * near < count:
+        near *= 2
+    return near if count % near == 0 else count
+
+
+def exchanged(tiles, axis, groups=None):
+    return lax.all_to_all(tiles, axis, 0, 0, tiled=True, axis_index_groups=groups)
+
+
+def summed(tiles):
+    return tiles.astype(jnp.float32).sum(axis=0).astype(jnp.bfloat16)
+
+
+def spread_to(value, peers, axis, groups=None):
+    tiles = exchanged(jnp.broadcast_to(value[None], (peers, *value.shape)), axis, groups)
+    return tiles.reshape(peers * value.shape[0], *value.shape[1:])
+
+
+def sum_over_cells(value):
+    lats, halves, lons = lax.axis_size("lat"), lax.axis_size("ch"), lax.axis_size("lon")
+    rows, width = value.shape
+    near = radix_of(lons)
+    far = lons // near
+    near_groups, far_groups = near_and_far(lons, near)
+    tiles = value.reshape(lats, rows // lats, halves, width // halves)
+    tiles = jnp.swapaxes(tiles, 1, 2).reshape(lats * halves, rows // lats, width // halves)
+    own = summed(exchanged(tiles, ("lat", "ch")))
+    own = summed(exchanged(own.reshape(near, -1, own.shape[-1]), "lon", near_groups))
+    own = summed(exchanged(own.reshape(far, -1, own.shape[-1]), "lon", far_groups))
+    own = spread_to(own, far, "lon", far_groups)
+    own = spread_to(own, near, "lon", near_groups)
+    return spread_to(own, lats, "lat").astype(jnp.float32)
 
 
 def add_edges(middle, to_first, to_last):
@@ -261,15 +249,12 @@
         (((0,), (0,)), ((), ())),
         preferred_element_type=jnp.float32,
     )
-    block_stack = jnp.concatenate(weight_terms, axis=0)
     own_width = channels // lax.axis_size("ch")
-    block_sum, encoder_sum = (
-        sum_by_parts(block_stack.astype(jnp.bfloat16), ("lon", ("lat", "ch"))),
-        sum_by_parts(encoder_term.astype(jnp.bfloat16), ("lon", ("lat", "ch"))),
-    )
-    first_col = lax.axis_index("ch") * own_width
-    block_sum = lax.dynamic_slice_in_dim(block_sum, first_col, own_width, 1)
-    encoder_sum = lax.dynamic_slice_in_dim(encoder_sum, first_col, own_width, 1)
+    grads = jnp.concatenate(weight_terms + [encoder_term], axis=0).astype(jnp.bfloat16)
+    grad_sum = sum_over_cells(grads)
+    block_rows = layers * basis_count * channels
+    block_sum = grad_sum[:block_rows]
+    encoder_sum = grad_sum[block_rows:]
     cells_total = cell_count * lax.axis_size("lon") * lax.axis_size(("lat", "ch"))
     normalizer = 1.0 / math.sqrt(cells_total)
     block_grads = (block_sum * normalizer).reshape(layers, basis_count * channels, own_width)

time: 343 us -> 278 us (0.81)
  waiting for transfers between devices: 108 us -> 28.3 us
  blocking collectives: 68.1 us -> 118 us
  starting transfers between devices: 130 us -> 102 us
  local copies, waits for them, and re-layouts: 15 us -> 10.4 us
    all_to_all x6 -> x1, waiting for transfers between devices: 86.7 us -> 7.99 us  [exchanged(): lax.all_to_all(tiles, axis, 0, 0, tiled=True, axis_index_groups=groups)]
    all_to_all x2 -> x5, blocking collectives: 68.1 us -> 118 us  [exchanged(): lax.all_to_all(tiles, axis, 0, 0, tiled=True, axis_index_groups=groups)]
    all_to_all x6 -> x1, starting transfers between devices: 31.6 us -> 3.57 us  [exchanged(): lax.all_to_all(tiles, axis, 0, 0, tiled=True, axis_index_groups=groups)]
  transfers between devices with their start and end apart: 26 -> 21, of which waited for: 19 -> 13; matrix products, arithmetic and copies ran while one was open for 3% -> 3% of each run, Pallas kernels for 0% -> 0%
where the time goes in v1:
time: 278 us; the launch traced here: 277 us
  blocking collectives  118 us (42%)
  starting transfers between devices  102 us (37%)
  waiting for transfers between devices  28.3 us (10%)
  local copies, waits for them, and re-layouts  10.4 us (4%)
  other arithmetic  8.88 us (3%)
  matrix products  7.86 us (3%)
    all_to_all x5, blocking collectives, exchanged(): lax.all_to_all(tiles, axis, 0, 0, tiled=True, axis_index_groups=groups)  118 us
    ppermute x3, starting transfers between devices, padded(): lax.ppermute(lax.slice_in_dim(block, 0, width, axis=dim), axis, backward)  53.4 us
    ppermute x4, starting transfers between devices, passed_along(): return lax.ppermute(value, axis, pairs)  15.2 us
    ppermute x6, starting transfers between devices, from_behind(): return lax.ppermute(block, axis, route)  11.6 us
    ppermute x3, starting transfers between devices, padded(): lax.ppermute(lax.slice_in_dim(block, block.shape[dim] - width, None, axis...  8.62 us
    ppermute x6, waiting for transfers between devices, from_behind(): return lax.ppermute(block, axis, route)  8.55 us
    all_to_all x1, waiting for transfers between devices, exchanged(): lax.all_to_all(tiles, axis, 0, 0, tiled=True, axis_index_groups=groups)  7.99 us
    ppermute x2, starting transfers between devices, with_halo(): lax.ppermute(last, axis, up)  7.29 us
  transfers between devices with their start and end apart: 21, of which 13 were waited for; matrix products, arithmetic and copies ran while one was open for 3% of the time, Pallas kernels for 0%

profile of v1, /device:TPU:40, one launch (start us, length us, event | category | flops | bytes accessed | tf_op | source)
XLA Modules:
  0.0 277.0 jit_solution(974024801128965668)
XLA Ops:
  0.6 0.9 fusion.64
  1.6 4.7 %collective-permute-start = (bf16[32,2,128]{2,1,0:T(2,128)(2,1)S(1)}, bf16[32,2,128]{2,1,0:T(2,128)(2,1)S(1)}, u32[]{:S(2)}, u32[]{:S(2)}) collective-permute-start(bf16[32,2,128]{2,1,0:T(2,128)(2,1)S(1)} %get-tuple-element.23), channel_id=1, source_target_pairs={{0,8},{8,16},{16,24},{24,32},{32,40},{40,48},{48,56},{56,64},{64,7... | collective-permute-start | bytes 49160 | tf_op jit(solution)/shard_map/ppermute | solution.py:31
  6.3 42.6 %collective-permute-start.1 = (bf16[32,2,128]{2,1,0:T(2,128)(2,1)S(1)}, bf16[32,2,128]{2,1,0:T(2,128)(2,1)S(1)}, u32[]{:S(2)}, u32[]{:S(2)}) collective-permute-start(bf16[32,2,128]{2,1,0:T(2,128)(2,1)S(1)} %get-tuple-element.24), channel_id=1, source_target_pairs={{8,0},{16,8},{24,16},{32,24},{40,32},{48,40},{56,48},{64,56},{72,6... | collective-permute-start | bytes 49160 | tf_op jit(solution)/shard_map/ppermute | solution.py:34
  48.9 0.7 convert_element_type.153
  49.6 0.7 broadcast_compare_fusion
  50.3 0.8 select_bitcast_fusion
  51.2 0.7 subtract_add_fusion
  51.8 1.8 slice.173
  54.2 1.1 pad_maximum_fusion.1
  55.3 0.5 slice.177
  55.8 0.5 slice.175
  56.3 0.4 slice.171
  56.7 0.4 slice.169
  57.2 1.0 add_convert_fusion
  58.3 0.4 reshape.156
  59.0 1.6 collective-permute-start.2
  60.5 1.3 collective-permute-start.3
  61.9 3.4 %collective-permute-done.3 = bf16[1,8192]{1,0:T(2,128)(2,1)S(1)} collective-permute-done((bf16[1,8192]{1,0:T(2,128)(2,1)S(1)}, bf16[1,8192]{1,0:T(2,128)(2,1)S(1)}, u32[]{:S(2)}, u32[]{:S(2)}) %collective-permute-start.3) | collective-permute-done | bytes 16416 | tf_op jit(solution)/shard_map/ppermute | solution.py:21
  65.8 4.6 %collective-permute-start.4 = (bf16[1,16,256]{2,1,0:T(8,128)(2,1)S(1)}, bf16[1,16,256]{2,1,0:T(8,128)(2,1)S(1)}, u32[]{:S(2)}, u32[]{:S(2)}) collective-permute-start(bf16[1,16,256]{2,1,0:T(8,128)(2,1)S(1)} %get-tuple-element.31), channel_id=1, source_target_pairs={{0,1},{1,2},{2,3},{3,4},{4,5},{5,6},{6,7},{8,9},{9,10},{10,11},{11... | collective-permute-start | bytes 24584 | tf_op jit(solution)/shard_map/ppermute | solution.py:47
  70.4 1.3 collective-permute-start.5
  71.7 0.3 convolution_convert_fusion
  72.1 1.4 collective-permute-done.5
  73.5 2.0 collective-permute-start.6
  75.5 5.2 %collective-permute-start.7 = (bf16[18,8,256]{2,1,0:T(8,128)(2,1)S(1)}, bf16[18,8,256]{2,1,0:T(8,128)(2,1)S(1)}, u32[]{:S(2)}, u32[]{:S(2)}) collective-permute-start(bf16[18,8,256]{2,1,0:T(8,128)(2,1)S(1)} %get-tuple-element.28), channel_id=1, source_target_pairs={{8,0},{16,8},{24,16},{32,24},{40,32},{48,40},{56,48},{64,56},{72,6... | collective-permute-start | bytes 221192 | tf_op jit(solution)/shard_map/ppermute | solution.py:34
  81.0 1.6 collective-permute-done.7
  83.9 0.8 copy-done.3
  84.8 1.0 fusion.37
  85.8 2.7 collective-permute-start.8
  88.5 1.3 collective-permute-start.9
  89.9 2.7 collective-permute-done.9
  92.6 2.0 collective-permute-start.10
  94.5 5.6 %collective-permute-start.11 = (bf16[18,8,256]{2,1,0:T(8,128)(2,1)S(1)}, bf16[18,8,256]{2,1,0:T(8,128)(2,1)S(1)}, u32[]{:S(2)}, u32[]{:S(2)}) collective-permute-start(bf16[18,8,256]{2,1,0:T(8,128)(2,1)S(1)} %get-tuple-element.26), channel_id=1, source_target_pairs={{8,0},{16,8},{24,16},{32,24},{40,32},{48,40},{56,48},{64,56},{72,6... | collective-permute-start | bytes 221192 | tf_op jit(solution)/shard_map/ppermute | solution.py:34
  100.2 0.4 collective-permute-done.10
  100.5 1.6 collective-permute-done.11
  103.4 0.5 copy-done.10
  103.9 1.0 fusion.35
  105.3 0.4 reshape.145
  106.8 2.1 collective-permute-start.12
  108.9 5.5 %collective-permute-start.13 = (bf16[18,8,256]{2,1,0:T(8,128)(2,1)S(1)}, bf16[18,8,256]{2,1,0:T(8,128)(2,1)S(1)}, u32[]{:S(2)}, u32[]{:S(2)}) collective-permute-start(bf16[18,8,256]{2,1,0:T(8,128)(2,1)S(1)} %get-tuple-element.20), channel_id=1, source_target_pairs={{0,248},{8,0},{16,8},{24,16},{32,24},{40,32},{48,40},{56,48},{64,5... | collective-permute-start | bytes 221192 | tf_op jit(solution)/shard_map/ppermute | solution.py:15
  114.4 0.6 collective-permute-done.12
  115.0 1.8 collective-permute-done.13
  116.8 2.3 collective-permute-start.14
  119.1 1.3 collective-permute-start.15
  120.5 3.5 %collective-permute-done.15 = f32[1,16,256]{2,1,0:T(8,128)S(1)} collective-permute-done((f32[1,16,256]{2,1,0:T(8,128)S(1)}, f32[1,16,256]{2,1,0:T(8,128)S(1)}, u32[]{:S(2)}, u32[]{:S(2)}) %collective-permute-start.15) | collective-permute-done | bytes 16416 | tf_op jit(solution)/shard_map/ppermute | solution.py:21
  124.5 0.4 reshape.146
  125.9 2.0 collective-permute-start.16
  127.9 5.6 %collective-permute-start.17 = (bf16[18,8,256]{2,1,0:T(8,128)(2,1)S(1)}, bf16[18,8,256]{2,1,0:T(8,128)(2,1)S(1)}, u32[]{:S(2)}, u32[]{:S(2)}) collective-permute-start(bf16[18,8,256]{2,1,0:T(8,128)(2,1)S(1)} %get-tuple-element.16), channel_id=1, source_target_pairs={{0,248},{8,0},{16,8},{24,16},{32,24},{40,32},{48,40},{56,48},{64,5... | collective-permute-start | bytes 221192 | tf_op jit(solution)/shard_map/ppermute | solution.py:15
  133.5 0.4 convolution_convert_fusion.1
  133.9 1.6 collective-permute-done.17
  135.5 3.6 %collective-permute-start.18 = (f32[1,16,256]{2,1,0:T(8,128)S(1)}, f32[1,16,256]{2,1,0:T(8,128)S(1)}, u32[]{:S(2)}, u32[]{:S(2)}) collective-permute-start(f32[1,16,256]{2,1,0:T(8,128)S(1)} %get-tuple-element.13), channel_id=1, source_target_pairs={{0,1},{1,2},{2,3},{3,4},{4,5},{5,6},{6,7},{8,9},{9,10},{10,11},{11... | collective-permute-start | bytes 49160 | tf_op jit(solution)/shard_map/ppermute | solution.py:21
  139.1 1.5 collective-permute-start.19
  140.6 0.4 convolution_convert_fusion.2
  140.9 1.6 collective-permute-done.19
  143.8 24.1 %all_to_all.30 = bf16[8,640,128]{2,1,0:T(8,128)(2,1)S(1)} all-to-all(bf16[8,640,128]{2,1,0:T(8,128)(2,1)S(1)} %bitcast.137), channel_id=1, replica_groups=mesh['ens'=2,'lon'=32,'lat'=4,'ch'=2] {'lat','ch'}, dimensions={0} | all-to-all | bytes 2621440 | tf_op jit(solution)/shard_map/all_to_all | solution.py:73
  168.1 15.3 %all_to_all.31 = bf16[8,80,128]{2,1,0:T(8,128)(2,1)S(1)} all-to-all(bf16[8,80,128]{2,1,0:T(8,128)(2,1)S(1)} %bitcast.149), channel_id=1, replica_groups={{0,8,16,24,32,40,48,56},{64,72,80,88,96,104,112,120},{128,136,144,152,1..., dimensions={0} | all-to-all | bytes 327680 | tf_op jit(solution)/shard_map/all_to_all | solution.py:73
  183.5 37.4 %all_to_all.32 = bf16[4,20,128]{2,1,0:T(8,128)(2,1)S(1)} all-to-all(bf16[4,20,128]{2,1,0:T(8,128)(2,1)S(1)} %reshape.150), channel_id=1, replica_groups={{0,64,128,192},{8,72,136,200},{16,80,144,208},{24,88,152,216},{32,96,16..., dimensions={0} | all-to-all | bytes 40960 | tf_op jit(solution)/shard_map/all_to_all | solution.py:73
  220.9 24.6 %all_to_all.33 = bf16[4,20,128]{2,1,0:T(8,128)(2,1)S(1)} all-to-all(bf16[4,20,128]{2,1,0:T(8,128)(2,1)S(1)} %broadcast_in_dim.22), channel_id=1, replica_groups={{0,64,128,192},{8,72,136,200},{16,80,144,208},{24,88,152,216},{32,96,16..., dimensions={0} | all-to-all | bytes 40960 | tf_op jit(solution)/shard_map/all_to_all | solution.py:73
  245.6 16.3 %all_to_all.34 = bf16[8,80,128]{2,1,0:T(8,128)(2,1)S(1)} all-to-all(bf16[8,80,128]{2,1,0:T(8,128)(2,1)S(1)} %broadcast_in_dim.24), channel_id=1, replica_groups={{0,8,16,24,32,40,48,56},{64,72,80,88,96,104,112,120},{128,136,144,152,1..., dimensions={0} | all-to-all | bytes 327680 | tf_op jit(solution)/shard_map/all_to_all | solution.py:73
  261.9 0.9 broadcast_in_dim.26
  262.8 3.6 %all-to-all-start.5 = ((bf16[4,640,128]{2,1,0:T(8,128)(2,1)}), bf16[4,640,128]{2,1,0:T(8,128)(2,1)S(1)}, u32[]{:S(2)}, u32[]{:S(2)}) async-start(bf16[4,640,128]{2,1,0:T(8,128)(2,1)} %broadcast_in_dim.26), calls=%async_computation.5 | async-start | bytes 1310720 | tf_op jit(solution)/shard_map/all_to_all | solution.py:73
  266.4 0.7 add_convert_fusion.1
  267.1 8.0 %all-to-all-done.5 = bf16[4,640,128]{2,1,0:T(8,128)(2,1)S(1)} async-done(((bf16[4,640,128]{2,1,0:T(8,128)(2,1)}), bf16[4,640,128]{2,1,0:T(8,128)(2,1)S(1)}, u32[]{:S(2)}, u32[]{:S(2)}) %all-to-all-start.5) | async-done | bytes 655392 | tf_op jit(solution)/shard_map/all_to_all | solution.py:73
  275.2 0.7 slice_multiply_fusion.1
  276.0 1.0 slice_multiply_fusion
  (100 shorter events, 8.8 us)
Async XLA Ops:
  0.6 64.9 %copy-start = (bf16[512,256]{1,0:T(8,128)(2,1)S(1)}, bf16[512,256]{1,0:T(8,128)(2,1)}, u32[]{:S(2)}) copy-start(bf16[512,256]{1,0:T(8,128)(2,1)} %param.11) | copy-start | bytes 786436
  1.6 52.5 %collective-permute-start = (bf16[32,2,128]{2,1,0:T(2,128)(2,1)S(1)}, bf16[32,2,128]{2,1,0:T(2,128)(2,1)S(1)}, u32[]{:S(2)}, u32[]{:S(2)}) collective-permute-start(bf16[32,2,128]{2,1,0:T(2,128)(2,1)S(1)} %get-tuple-element.23), channel_id=1, source_target_pairs={{0,8},{8,16},{16,24},{24,32},{32,40},{40,48},{48,56},{56,64},{64,7... | collective-permute-start | bytes 49160 | tf_op jit(solution)/shard_map/ppermute | solution.py:31
  6.3 47.8 %collective-permute-start.1 = (bf16[32,2,128]{2,1,0:T(2,128)(2,1)S(1)}, bf16[32,2,128]{2,1,0:T(2,128)(2,1)S(1)}, u32[]{:S(2)}, u32[]{:S(2)}) collective-permute-start(bf16[32,2,128]{2,1,0:T(2,128)(2,1)S(1)} %get-tuple-element.24), channel_id=1, source_target_pairs={{8,0},{16,8},{24,16},{32,24},{40,32},{48,40},{56,48},{64,56},{72,6... | collective-permute-start | bytes 49160 | tf_op jit(solution)/shard_map/ppermute | solution.py:34
  59.0 2.9 %collective-permute-start.2 = (bf16[1,8192]{1,0:T(2,128)(2,1)S(1)}, bf16[1,8192]{1,0:T(2,128)(2,1)S(1)}, u32[]{:S(2)}, u32[]{:S(2)}) collective-permute-start(bf16[1,8192]{1,0:T(2,128)(2,1)S(1)} %get-tuple-element.11), channel_id=1, source_target_pairs={{0,1},{1,2},{2,3},{3,4},{4,5},{5,6},{6,7},{8,9},{9,10},{10,11},{11... | collective-permute-start | bytes 49160 | tf_op jit(solution)/shard_map/ppermute | solution.py:21
  60.5 4.8 %collective-permute-start.3 = (bf16[1,8192]{1,0:T(2,128)(2,1)S(1)}, bf16[1,8192]{1,0:T(2,128)(2,1)S(1)}, u32[]{:S(2)}, u32[]{:S(2)}) collective-permute-start(bf16[1,8192]{1,0:T(2,128)(2,1)S(1)} %get-tuple-element.12), channel_id=1, source_target_pairs={{1,0},{2,1},{3,2},{4,3},{5,4},{6,5},{7,6},{9,8},{10,9},{11,10},{12... | collective-permute-start | bytes 49160 | tf_op jit(solution)/shard_map/ppermute | solution.py:21
  65.8 6.2 %collective-permute-start.4 = (bf16[1,16,256]{2,1,0:T(8,128)(2,1)S(1)}, bf16[1,16,256]{2,1,0:T(8,128)(2,1)S(1)}, u32[]{:S(2)}, u32[]{:S(2)}) collective-permute-start(bf16[1,16,256]{2,1,0:T(8,128)(2,1)S(1)} %get-tuple-element.31), channel_id=1, source_target_pairs={{0,1},{1,2},{2,3},{3,4},{4,5},{5,6},{6,7},{8,9},{9,10},{10,11},{11... | collective-permute-start | bytes 24584 | tf_op jit(solution)/shard_map/ppermute | solution.py:47
  70.4 3.1 %collective-permute-start.5 = (bf16[1,16,256]{2,1,0:T(8,128)(2,1)S(1)}, bf16[1,16,256]{2,1,0:T(8,128)(2,1)S(1)}, u32[]{:S(2)}, u32[]{:S(2)}) collective-permute-start(bf16[1,16,256]{2,1,0:T(8,128)(2,1)S(1)} %get-tuple-element.32), channel_id=1, source_target_pairs={{1,0},{2,1},{3,2},{4,3},{5,4},{6,5},{7,6},{9,8},{10,9},{11,10},{12... | collective-permute-start | bytes 24584 | tf_op jit(solution)/shard_map/ppermute | solution.py:48
  73.5 7.5 %collective-permute-start.6 = (bf16[18,8,256]{2,1,0:T(8,128)(2,1)S(1)}, bf16[18,8,256]{2,1,0:T(8,128)(2,1)S(1)}, u32[]{:S(2)}, u32[]{:S(2)}) collective-permute-start(bf16[18,8,256]{2,1,0:T(8,128)(2,1)S(1)} %get-tuple-element.27), channel_id=1, source_target_pairs={{0,8},{8,16},{16,24},{24,32},{32,40},{40,48},{48,56},{56,64},{64,7... | collective-permute-start | bytes 221192 | tf_op jit(solution)/shard_map/ppermute | solution.py:31
  75.5 7.1 %collective-permute-start.7 = (bf16[18,8,256]{2,1,0:T(8,128)(2,1)S(1)}, bf16[18,8,256]{2,1,0:T(8,128)(2,1)S(1)}, u32[]{:S(2)}, u32[]{:S(2)}) collective-permute-start(bf16[18,8,256]{2,1,0:T(8,128)(2,1)S(1)} %get-tuple-element.28), channel_id=1, source_target_pairs={{8,0},{16,8},{24,16},{32,24},{40,32},{48,40},{56,48},{64,56},{72,6... | collective-permute-start | bytes 221192 | tf_op jit(solution)/shard_map/ppermute | solution.py:34
  83.5 1.2 copy-start.3
  85.8 4.1 %collective-permute-start.8 = (bf16[1,16,256]{2,1,0:T(8,128)(2,1)S(1)}, bf16[1,16,256]{2,1,0:T(8,128)(2,1)S(1)}, u32[]{:S(2)}, u32[]{:S(2)}) collective-permute-start(bf16[1,16,256]{2,1,0:T(8,128)(2,1)S(1)} %get-tuple-element.29), channel_id=1, source_target_pairs={{0,1},{1,2},{2,3},{3,4},{4,5},{5,6},{6,7},{8,9},{9,10},{10,11},{11... | collective-permute-start | bytes 24584 | tf_op jit(solution)/shard_map/ppermute | solution.py:47
  88.5 4.0 %collective-permute-start.9 = (bf16[1,16,256]{2,1,0:T(8,128)(2,1)S(1)}, bf16[1,16,256]{2,1,0:T(8,128)(2,1)S(1)}, u32[]{:S(2)}, u32[]{:S(2)}) collective-permute-start(bf16[1,16,256]{2,1,0:T(8,128)(2,1)S(1)} %get-tuple-element.30), channel_id=1, source_target_pairs={{1,0},{2,1},{3,2},{4,3},{5,4},{6,5},{7,6},{9,8},{10,9},{11,10},{12... | collective-permute-start | bytes 24584 | tf_op jit(solution)/shard_map/ppermute | solution.py:48
  92.6 8.0 %collective-permute-start.10 = (bf16[18,8,256]{2,1,0:T(8,128)(2,1)S(1)}, bf16[18,8,256]{2,1,0:T(8,128)(2,1)S(1)}, u32[]{:S(2)}, u32[]{:S(2)}) collective-permute-start(bf16[18,8,256]{2,1,0:T(8,128)(2,1)S(1)} %get-tuple-element.25), channel_id=1, source_target_pairs={{0,8},{8,16},{16,24},{24,32},{32,40},{40,48},{48,56},{56,64},{64,7... | collective-permute-start | bytes 221192 | tf_op jit(solution)/shard_map/ppermute | solution.py:31
  94.5 7.6 %collective-permute-start.11 = (bf16[18,8,256]{2,1,0:T(8,128)(2,1)S(1)}, bf16[18,8,256]{2,1,0:T(8,128)(2,1)S(1)}, u32[]{:S(2)}, u32[]{:S(2)}) collective-permute-start(bf16[18,8,256]{2,1,0:T(8,128)(2,1)S(1)} %get-tuple-element.26), channel_id=1, source_target_pairs={{8,0},{16,8},{24,16},{32,24},{40,32},{48,40},{56,48},{64,56},{72,6... | collective-permute-start | bytes 221192 | tf_op jit(solution)/shard_map/ppermute | solution.py:34
  103.0 0.9 copy-start.10
  103.4 1.6 copy-start.1
  105.0 0.7 copy-start.5
  106.5 17.4 %copy-start.11 = (bf16[16,16,256]{2,1,0:T(8,128)(2,1)S(1)}, bf16[16,16,256]{2,1,0:T(8,128)(2,1)}, u32[]{:S(2)}) copy-start(bf16[16,16,256]{2,1,0:T(8,128)(2,1)} %param.15) | copy-start | bytes 393220
  106.7 17.3 %copy-start.9 = (f32[256,256]{1,0:T(8,128)S(1)}, f32[256,256]{1,0:T(8,128)}, u32[]{:S(2)}) copy-start(f32[256,256]{1,0:T(8,128)} %get-tuple-element.41) | copy-start | bytes 786436
  106.7 17.4 %copy-start.4 = (bf16[2,1024,256]{2,1,0:T(8,128)(2,1)S(1)}, bf16[2,1024,256]{2,1,0:T(8,128)(2,1)}, u32[]{:S(2)}) copy-start(bf16[2,1024,256]{2,1,0:T(8,128)(2,1)} %param.14) | copy-start | bytes 3145732
  106.8 8.2 %collective-permute-start.12 = (bf16[18,8,256]{2,1,0:T(8,128)(2,1)S(1)}, bf16[18,8,256]{2,1,0:T(8,128)(2,1)S(1)}, u32[]{:S(2)}, u32[]{:S(2)}) collective-permute-start(bf16[18,8,256]{2,1,0:T(8,128)(2,1)S(1)} %get-tuple-element.19), channel_id=1, source_target_pairs={{0,8},{8,16},{16,24},{24,32},{32,40},{40,48},{48,56},{56,64},{64,7... | collective-permute-start | bytes 221192 | tf_op jit(solution)/shard_map/ppermute | solution.py:15
  108.9 7.9 %collective-permute-start.13 = (bf16[18,8,256]{2,1,0:T(8,128)(2,1)S(1)}, bf16[18,8,256]{2,1,0:T(8,128)(2,1)S(1)}, u32[]{:S(2)}, u32[]{:S(2)}) collective-permute-start(bf16[18,8,256]{2,1,0:T(8,128)(2,1)S(1)} %get-tuple-element.20), channel_id=1, source_target_pairs={{0,248},{8,0},{16,8},{24,16},{32,24},{40,32},{48,40},{56,48},{64,5... | collective-permute-start | bytes 221192 | tf_op jit(solution)/shard_map/ppermute | solution.py:15
  116.8 3.7 %collective-permute-start.14 = (f32[1,16,256]{2,1,0:T(8,128)S(1)}, f32[1,16,256]{2,1,0:T(8,128)S(1)}, u32[]{:S(2)}, u32[]{:S(2)}) collective-permute-start(f32[1,16,256]{2,1,0:T(8,128)S(1)} %get-tuple-element.17), channel_id=1, source_target_pairs={{0,1},{1,2},{2,3},{3,4},{4,5},{5,6},{6,7},{8,9},{9,10},{10,11},{11... | collective-permute-start | bytes 49160 | tf_op jit(solution)/shard_map/ppermute | solution.py:21
  119.1 4.8 %collective-permute-start.15 = (f32[1,16,256]{2,1,0:T(8,128)S(1)}, f32[1,16,256]{2,1,0:T(8,128)S(1)}, u32[]{:S(2)}, u32[]{:S(2)}) collective-permute-start(f32[1,16,256]{2,1,0:T(8,128)S(1)} %get-tuple-element.18), channel_id=1, source_target_pairs={{1,0},{2,1},{3,2},{4,3},{5,4},{6,5},{7,6},{9,8},{10,9},{11,10},{12... | collective-permute-start | bytes 49160 | tf_op jit(solution)/shard_map/ppermute | solution.py:21
  125.7 7.8 %copy-start.2 = (bf16[32,8,4,256]{3,1,2,0:T(8,128)(2,1)S(1)}, bf16[32,8,4,256]{3,1,2,0:T(8,128)(2,1)}, u32[]{:S(2)}) copy-start(bf16[32,8,4,256]{3,1,2,0:T(8,128)(2,1)} %copy-done.1) | copy-start | bytes 1572868
  125.7 7.8 %copy-start.6 = (bf16[256,256]{1,0:T(8,128)(2,1)S(1)}, bf16[256,256]{1,0:T(8,128)(2,1)}, u32[]{:S(2)}) copy-start(bf16[256,256]{1,0:T(8,128)(2,1)} %copy-done.5) | copy-start | bytes 393220
  125.9 8.0 %collective-permute-start.16 = (bf16[18,8,256]{2,1,0:T(8,128)(2,1)S(1)}, bf16[18,8,256]{2,1,0:T(8,128)(2,1)S(1)}, u32[]{:S(2)}, u32[]{:S(2)}) collective-permute-start(bf16[18,8,256]{2,1,0:T(8,128)(2,1)S(1)} %get-tuple-element.15), channel_id=1, source_target_pairs={{0,8},{8,16},{16,24},{24,32},{32,40},{40,48},{48,56},{56,64},{64,7... | collective-permute-start | bytes 221192 | tf_op jit(solution)/shard_map/ppermute | solution.py:15
  127.9 7.6 %collective-permute-start.17 = (bf16[18,8,256]{2,1,0:T(8,128)(2,1)S(1)}, bf16[18,8,256]{2,1,0:T(8,128)(2,1)S(1)}, u32[]{:S(2)}, u32[]{:S(2)}) collective-permute-start(bf16[18,8,256]{2,1,0:T(8,128)(2,1)S(1)} %get-tuple-element.16), channel_id=1, source_target_pairs={{0,248},{8,0},{16,8},{24,16},{32,24},{40,32},{48,40},{56,48},{64,5... | collective-permute-start | bytes 221192 | tf_op jit(solution)/shard_map/ppermute | solution.py:15
  135.5 5.4 %collective-permute-start.18 = (f32[1,16,256]{2,1,0:T(8,128)S(1)}, f32[1,16,256]{2,1,0:T(8,128)S(1)}, u32[]{:S(2)}, u32[]{:S(2)}) collective-permute-start(f32[1,16,256]{2,1,0:T(8,128)S(1)} %get-tuple-element.13), channel_id=1, source_target_pairs={{0,1},{1,2},{2,3},{3,4},{4,5},{5,6},{6,7},{8,9},{9,10},{10,11},{11... | collective-permute-start | bytes 49160 | tf_op jit(solution)/shard_map/ppermute | solution.py:21
  139.1 3.5 %collective-permute-start.19 = (f32[1,16,256]{2,1,0:T(8,128)S(1)}, f32[1,16,256]{2,1,0:T(8,128)S(1)}, u32[]{:S(2)}, u32[]{:S(2)}) collective-permute-start(f32[1,16,256]{2,1,0:T(8,128)S(1)} %get-tuple-element.14), channel_id=1, source_target_pairs={{1,0},{2,1},{3,2},{4,3},{5,4},{6,5},{7,6},{9,8},{10,9},{11,10},{12... | collective-permute-start | bytes 49160 | tf_op jit(solution)/shard_map/ppermute | solution.py:21
  142.6 0.7 copy-start.7
  245.5 20.9 %copy-start.8 = (f32[256,256]{1,0:T(8,128)S(1)}, f32[256,256]{1,0:T(8,128)}, u32[]{:S(2)}) copy-start(f32[256,256]{1,0:T(8,128)} %get-tuple-element.22) | copy-start | bytes 786436
  262.8 12.3 %all-to-all-start.5 = ((bf16[4,640,128]{2,1,0:T(8,128)(2,1)}), bf16[4,640,128]{2,1,0:T(8,128)(2,1)S(1)}, u32[]{:S(2)}, u32[]{:S(2)}) async-start(bf16[4,640,128]{2,1,0:T(8,128)(2,1)} %broadcast_in_dim.26), calls=%async_computation.5 | async-start | bytes 1310720 | tf_op jit(solution)/shard_map/all_to_all | solution.py:73

commit v2 on v1

v2 whole, which is shorter than its diff:
```python
import math

import jax
import jax.numpy as jnp
import numpy as np
from jax import lax
from jax.experimental import pallas as pl
from jax.experimental.pallas import tpu as pltpu
from jax.sharding import PartitionSpec as P

REACH = 8
TAP_REACH = 2
LANES = 128
BAND = ("lat", "ch")


def ring_permute(value, axis, steps):
    count = lax.axis_size(axis)
    return lax.ppermute(value, axis, [(i, (i + steps) % count) for i in range(count)])


def line_permute(value, axis, steps):
    count = lax.axis_size(axis)
    pairs = [(i, i + steps) for i in range(count) if 0 <= i + steps < count]
    return lax.ppermute(value, axis, pairs)


def near_and_far(count, near):
    near_groups = [[first + step for step in range(near)] for first in range(0, count, near)]
    far_groups = [[first + near * step for step in range(count // near)] for first in range(near)]
    return near_groups, far_groups


def radix_of(count):
    near = 1
    while near * near < count:
        near *= 2
    return near if count % near == 0 else count


def exchanged(tiles, axis, groups=None):
    return lax.all_to_all(tiles, axis, 0, 0, tiled=True, axis_index_groups=groups)


def summed(tiles):
    return tiles.astype(jnp.float32).sum(axis=0).astype(jnp.bfloat16)


def copies_to(value, peers, axis, groups=None):
    return exchanged(jnp.broadcast_to(value[None], (peers, *value.shape)), axis, groups)


def sum_over_cells(value):
    lats, lons = lax.axis_size("lat"), lax.axis_size("lon")
    rows, width = value.shape
    half = width // lax.axis_size("ch")
    core = lax.axis_index("ch")
    given = lax.dynamic_slice_in_dim(value, (1 - core) * half, half, 1)
    kept = lax.dynamic_slice_in_dim(value, core * half, half, 1)
    taken = ring_permute(given, "ch", 1)
    own = (kept.astype(jnp.float32) + taken.astype(jnp.float32)).astype(jnp.bfloat16)
    near = radix_of(lons)
    far = lons // near
    near_groups, far_groups = near_and_far(lons, near)
    own = summed(exchanged(own.reshape(lats, rows // lats, half), "lat"))
    own = summed(exchanged(own.reshape(near, -1, half), "lon", near_groups))
    own = summed(copies_to(own, far, "lon", far_groups))
    own = copies_to(own, near, "lon", near_groups).reshape(-1, half)
    return copies_to(own, lats, "lat").reshape(rows, half).astype(jnp.float32)


def placement(basis_count, span):
    taps = span - 1
    blocks = []

    def source(k, r, t):
        return (k * 3 + r) * span + t

    for k in range(basis_count):
        wide = np.zeros((basis_count * 3 * span, 2 * LANES), np.float32)
        for r in range(3):
            for t in range(span):
                wide[source(k, r, t), r * 64 + t] = 1
        blocks.append(wide)
    for k in range(basis_count):
        thin = np.zeros((basis_count * 3 * span, LANES), np.float32)
        for r in range(3):
            for t in range(span):
                thin[source(k, r, t), r * 32 + t] = 1
        blocks.append(thin)
    for r in range(3):
        wide = np.zeros((basis_count * 3 * span, 2 * LANES), np.float32)
        for k in range(basis_count):
            for t in range(span):
                wide[source(k, r, t), k * 64 + taps - t] = 1
        blocks.append(wide)
    for r in range(3):
        thin = np.zeros((basis_count * 3 * span, LANES), np.float32)
        for k in range(basis_count):
            for t in range(span):
                thin[source(k, r, t), k * 32 + taps - t] = 1
        blocks.append(thin)
    return np.concatenate(blocks, axis=1)


FORWARD_WIDE, FORWARD_THIN, BACKWARD_WIDE, BACKWARD_THIN = 0, 8, 12, 18


def slanted(vecs, row, block, height):
    vector = vecs[row : row + 1, block * LANES : (block + 1) * LANES]
    spread = jnp.broadcast_to(vector, (height, LANES))
    return pltpu.roll(spread, 0, 1, stride=1, stride_axis=0).astype(jnp.bfloat16)


def dot(left, right):
    return jnp.dot(left, right, preferred_element_type=jnp.float32)


def dot_nt(left, right):
    return lax.dot_general(
        left, right, (((1,), (1,)), ((), ())), preferred_element_type=jnp.float32
    )


def forward_kernel(
    vecs, own, west, east, weights, cot, feat0, pre0, feat1, state2, act1, s0, wide, s1
):
    rows, cols = cot.shape[0], cot.shape[1]
    channels = cot.shape[2]
    basis_count = weights.shape[1] // channels
    mid = cols + 2 * REACH
    for i in range(rows + 4):
        s0[i * 64 : i * 64 + cols] = west[i * cols : (i + 1) * cols]
        s0[i * 64 + cols : i * 64 + 2 * cols] = own[i]
        s0[i * 64 + 2 * cols : i * 64 + 3 * cols] = east[i * cols : (i + 1) * cols]
        s0[i * 64 + 3 * cols : (i + 1) * 64] = jnp.zeros((64 - 3 * cols, channels), jnp.bfloat16)
    s0[(rows + 4) * 64 :] = jnp.zeros((64, channels), jnp.bfloat16)
    for i in range(rows + 2):
        band = jnp.concatenate(
            [
                jnp.concatenate(
                    [slanted(vecs, i + 1, FORWARD_WIDE + 2 * k + h, mid) for h in range(2)],
                    axis=1,
                )
                for k in range(basis_count)
            ],
            axis=0,
        )
        out = dot(band, s0[i * 64 : (i + 4) * 64])
        for k in range(basis_count):
            part = out[k * mid : (k + 1) * mid]
            wide[i * mid : (i + 1) * mid, k * channels : (k + 1) * channels] = part.astype(
                jnp.bfloat16
            )
            if 1 <= i <= rows:
                feat0[(i - 1) * cols : i * cols, k * channels : (k + 1) * channels] = part[
                    REACH : REACH + cols
                ].astype(jnp.bfloat16)
    pre0[...] = dot(wide[...], weights[0])
    for i in range(rows + 2):
        pre = pre0[i * mid : (i + 1) * mid]
        before = s0[(i + 1) * 64 : (i + 1) * 64 + 3 * cols].astype(jnp.float32)
        before = before[REACH : REACH + mid]
        s1[i * mid : (i + 1) * mid] = (before + pre * jax.nn.sigmoid(pre)).astype(jnp.bfloat16)
    s1[(rows + 2) * mid :] = jnp.zeros((mid, channels), jnp.bfloat16)
    for i in range(rows):
        band = jnp.concatenate(
            [slanted(vecs, i + 2, FORWARD_THIN + k, cols) for k in range(basis_count)], axis=0
        )
        out = dot(band, s1[i * mid : (i + 4) * mid])
        for k in range(basis_count):
            feat1[i * cols : (i + 1) * cols, k * channels : (k + 1) * channels] = out[
                k * cols : (k + 1) * cols
            ].astype(jnp.bfloat16)
    pre1 = dot(feat1[...], weights[1])
    for i in range(rows):
        pre = pre1[i * cols : (i + 1) * cols]
        sigma = jax.nn.sigmoid(pre)
        before = s1[(i + 1) * mid : (i + 2) * mid].astype(jnp.float32)[REACH : REACH + cols]
        state2[i] = (before + pre * sigma).astype(jnp.bfloat16)
        upstream = cot[i].astype(jnp.float32)
        act1[i] = (upstream * sigma * (1.0 + pre * (1.0 - sigma))).astype(jnp.bfloat16)


def backward_kernel(
    vecs, own, west, east, weights, pre0, cot, west_cot, east_cot, act0, grad0, a1, e1, g1, a0, e0
):
    rows, cols, channels = grad0.shape
    basis_count = weights.shape[1] // channels
    mid = cols + 2 * REACH
    full = 3 * cols
    skip = (rows + 4) * cols
    for i in range(rows + 4):
        a1[i * full : i * full + cols] = west[i]
        a1[i * full + cols : i * full + 2 * cols] = own[i]
        a1[i * full + 2 * cols : (i + 1) * full] = east[i]
    for k in range(basis_count):
        errors = dot_nt(a1[...], weights[1, k * channels : (k + 1) * channels])
        errors = errors.astype(jnp.bfloat16)
        for i in range(rows + 4):
            first = (i * basis_count + k) * 64
            e1[first : first + full] = errors[i * full : (i + 1) * full]
            e1[first + full : first + 64] = jnp.zeros((64 - full, channels), jnp.bfloat16)
    for i in range(rows + 2):
        band = jnp.concatenate(
            [
                slanted(vecs, i + s, BACKWARD_WIDE + (2 - s) * 2 + h, mid)
                for s in range(3)
                for h in range(2)
            ],
            axis=1,
        )
        spread = dot(band, e1[i * basis_count * 64 : (i + 3) * basis_count * 64])
        upstream = jnp.concatenate(
            [
                west_cot[skip + i * REACH : skip + (i + 1) * REACH].astype(jnp.float32),
                cot[i].astype(jnp.float32),
                east_cot[skip + i * REACH : skip + (i + 1) * REACH].astype(jnp.float32),
            ],
            axis=0,
        )
        grad = (upstream + spread).astype(jnp.bfloat16).astype(jnp.float32)
        g1[i * mid : (i + 1) * mid] = grad
        pre = pre0[i * mid : (i + 1) * mid]
        sigma = jax.nn.sigmoid(pre)
        act = grad * sigma * (1.0 + pre * (1.0 - sigma))
        a0[i * mid : (i + 1) * mid] = act.astype(jnp.bfloat16)
        if 1 <= i <= rows:
            act0[(i - 1) * cols : i * cols] = act[REACH : REACH + cols].astype(jnp.bfloat16)
    for k in range(basis_count):
        errors = dot_nt(a0[...], weights[0, k * channels : (k + 1) * channels])
        errors = errors.astype(jnp.bfloat16)
        for i in range(rows + 2):
            first = (i * basis_count + k) * mid
            e0[first : first + mid] = errors[i * mid : (i + 1) * mid]
    for i in range(rows):
        band = jnp.concatenate(
            [slanted(vecs, i + s + 1, BACKWARD_THIN + 2 - s, cols) for s in range(3)], axis=1
        )
        spread = dot(band, e0[i * basis_count * mid : (i + 3) * basis_count * mid])
        before = g1[(i + 1) * mid + REACH : (i + 1) * mid + REACH + cols]
        grad0[i] = (before + spread).astype(jnp.bfloat16)


def in_vmem(count):
    return [pl.BlockSpec(memory_space=pltpu.VMEM)] * count


def run_forward(vecs, own, west, east, weights, cot):
    rows, cols, channels = cot.shape
    depth = weights.shape[1]
    mid = cols + 2 * REACH
    bf16, f32 = jnp.bfloat16, jnp.float32
    return pl.pallas_call(
        forward_kernel,
        out_shape=(
            jax.ShapeDtypeStruct((rows * cols, depth), bf16),
            jax.ShapeDtypeStruct(((rows + 2) * mid, channels), f32),
            jax.ShapeDtypeStruct((rows * cols, depth), bf16),
            jax.ShapeDtypeStruct((rows, cols, channels), bf16),
            jax.ShapeDtypeStruct((rows, cols, channels), bf16),
        ),
        in_specs=in_vmem(6),
        out_specs=tuple(in_vmem(5)),
        scratch_shapes=[
            pltpu.VMEM(((rows + 5) * 64, channels), bf16),
            pltpu.VMEM(((rows + 2) * mid, depth), bf16),
            pltpu.VMEM(((rows + 3) * mid, channels), bf16),
        ],
        name="forward",
    )(vecs, own, west, east, weights, cot)


def run_backward(vecs, own, west, east, weights, pre0, cot, west_cot, east_cot):
    rows, cols, channels = own.shape
    rows -= 4
    basis_count = weights.shape[1] // channels
    mid = cols + 2 * REACH
    bf16, f32 = jnp.bfloat16, jnp.float32
    return pl.pallas_call(
        backward_kernel,
        out_shape=(
            jax.ShapeDtypeStruct((rows * cols, channels), bf16),
            jax.ShapeDtypeStruct((rows, cols, channels), bf16),
        ),
        in_specs=in_vmem(9),
        out_specs=tuple(in_vmem(2)),
        scratch_shapes=[
            pltpu.VMEM(((rows + 4) * 3 * cols, channels), bf16),
            pltpu.VMEM(((rows + 4) * basis_count * 64, channels), bf16),
            pltpu.VMEM(((rows + 2) * mid, channels), f32),
            pltpu.VMEM(((rows + 2) * mid, channels), bf16),
            pltpu.VMEM(((rows + 2) * basis_count * mid, channels), bf16),
        ],
        name="backward",
    )(vecs, own, west, east, weights, pre0, cot, west_cot, east_cot)


def per_device(
    input_field,
    encoder_filter,
    row_owner,
    encoder_weight,
    disco_basis,
    row_widths,
    block_weights,
    cotangent,
):
    rows_in, cols_in, in_width = input_field.shape
    rows_dev, cols_dev, channels = cotangent.shape
    basis_count, tap_count = encoder_filter.shape[1:]
    layers = block_weights.shape[0]
    span = disco_basis.shape[3]
    cell_count = rows_dev * cols_dev
    latent_width = basis_count * in_width
    f32, bf16 = jnp.float32, jnp.bfloat16

    from_west = ring_permute(input_field[:, cols_in - TAP_REACH :], "lon", 1)
    from_east = ring_permute(input_field[:, :TAP_REACH], "lon", -1)
    offsets = jnp.abs(jnp.arange(span, dtype=jnp.int32) - REACH)
    keep = offsets[None, :] <= row_widths[:, None]
    masked = jnp.where(keep[:, None, None, :], disco_basis, jnp.zeros_like(disco_basis))
    masked = masked.reshape(rows_dev, -1)
    taps_at = (
        np.arange(cols_in + 2 * TAP_REACH)[None, :, None] - 2 * np.arange(cols_dev)[:, None, None]
        == np.arange(tap_count)[None, None, :]
    )
    filters = jnp.einsum(
        "pkt,jqt->pjkq", encoder_filter, jnp.asarray(taps_at, bf16), preferred_element_type=f32
    ).astype(bf16)
    extended_in = jnp.concatenate([from_west, input_field, from_east], axis=1)
    filtered = jnp.einsum("pjkq,pqc->pjkc", filters, extended_in, preferred_element_type=f32)
    filtered = filtered.astype(bf16).reshape(rows_in, cols_dev * latent_width)
    first_row = lax.axis_index(BAND) * rows_dev
    relative = row_owner - first_row + 1
    selector = (relative[None, :] == jnp.arange(rows_dev + 2, dtype=jnp.int32)[:, None]).astype(bf16)
    partial = jnp.dot(selector, filtered, preferred_element_type=f32)
    partial = partial.reshape(rows_dev + 2, cols_dev, latent_width)

    def edge_message(latent_rows, cot_row, basis_rows):
        basis_rows = jnp.pad(basis_rows, ((0, 6), (0, latent_width - basis_rows.shape[1])))
        return jnp.concatenate(
            [
                latent_rows.astype(bf16).reshape(-1, latent_width),
                cot_row.reshape(-1, latent_width),
                basis_rows,
            ]
        )

    above = line_permute(edge_message(partial[-3:], cotangent[-1:], masked[-2:]), BAND, 1)
    below = line_permute(edge_message(partial[:3], cotangent[:1], masked[:2]), BAND, -1)
    lat_rows = 3 * cols_dev
    cot_rows = cols_dev * channels // latent_width

    def opened(message):
        latent = message[:lat_rows].reshape(3, cols_dev, latent_width).astype(f32)
        cot = message[lat_rows : lat_rows + cot_rows].reshape(1, cols_dev, channels)
        return latent, cot, message[lat_rows + cot_rows :][:2, : masked.shape[1]]

    above_latent, above_cot, above_basis = opened(above)
    below_latent, below_cot, below_basis = opened(below)
    tail = rows_dev + 1
    latent = (
        jnp.pad(partial, ((1, 1), (0, 0), (0, 0)))
        + jnp.pad(above_latent, ((0, tail), (0, 0), (0, 0)))
        + jnp.pad(below_latent, ((tail, 0), (0, 0), (0, 0)))
    ).astype(bf16)
    state0 = jnp.dot(
        latent.reshape(-1, latent_width), encoder_weight, preferred_element_type=f32
    ).astype(bf16)
    cot_rows_ext = jnp.concatenate([above_cot, cotangent, below_cot])
    to_east = jnp.concatenate([state0, cot_rows_ext[:, -REACH:].reshape(-1, channels)])
    to_west = jnp.concatenate([state0, cot_rows_ext[:, :REACH].reshape(-1, channels)])
    west = ring_permute(to_east, "lon", 1)
    east = ring_permute(to_west, "lon", -1)
    basis_ext = jnp.concatenate([above_basis, masked, below_basis])
    vecs = jnp.dot(
        basis_ext, jnp.asarray(placement(basis_count, span), bf16), preferred_element_type=f32
    )
    state0 = state0.reshape(rows_dev + 4, cols_dev, channels)
    feat0, pre0, feat1, state_out, act1 = run_forward(
        vecs, state0, west, east, block_weights, cotangent
    )

    act_above = line_permute(act1[-2:], BAND, 1)
    act_below = line_permute(act1[:2], BAND, -1)
    act_rows = jnp.concatenate([act_above, act1, act_below])
    act_west = ring_permute(act_rows, "lon", 1)
    act_east = ring_permute(act_rows, "lon", -1)
    weight1 = lax.dot_general(
        feat1, act1.reshape(cell_count, channels), (((0,), (0,)), ((), ())),
        preferred_element_type=f32,
    )
    act0, gradient = run_backward(
        vecs, act_rows, act_west, act_east, block_weights, pre0, cot_rows_ext, west, east
    )
    weight0 = lax.dot_general(
        feat0, act0, (((0,), (0,)), ((), ())), preferred_element_type=f32
    )
    encoder_term = lax.dot_general(
        latent[2 : rows_dev + 2].reshape(cell_count, latent_width),
        gradient.reshape(cell_count, channels),
        (((0,), (0,)), ((), ())),
        preferred_element_type=f32,
    )
    grads = jnp.concatenate([weight0, weight1, encoder_term], axis=0).astype(bf16)
    grad_sum = sum_over_cells(grads)
    block_rows = layers * basis_count * channels
    cells_total = cell_count * lax.axis_size("lon") * lax.axis_size(BAND)
    normalizer = 1.0 / math.sqrt(cells_total)
    block_grads = (grad_sum[:block_rows] * normalizer).reshape(
        layers, basis_count * channels, grad_sum.shape[1]
    )
    return (state_out, gradient, block_grads, grad_sum[block_rows:] * normalizer)


def solution(mesh):
    placed = (
        P(("ens", "lat", "ch"), "lon", None),
        P(("lat", "ch"), None, None),
        P(("ens", "lat", "ch")),
        P(),
        P(("lat", "ch"), None, None, None),
        P(("lat", "ch")),
        P(),
        P(("ens", "lat", "ch"), "lon", None),
    )
    return jax.shard_map(
        per_device,
        mesh=mesh,
        in_specs=placed,
        out_specs=(
            P(("ens", "lat", "ch"), "lon", None),
            P(("ens", "lat", "ch"), "lon", None),
            P("ens", None, "ch"),
            P("ens", "ch"),
        ),
        check_vma=False,
    )
```

time: 278 us -> 210 us (0.76)
  starting transfers between devices: 102 us -> 73.4 us
  blocking collectives: 118 us -> 94 us
  waiting for transfers between devices: 28.3 us -> 11.9 us
  Pallas kernels: 0 us -> 9.23 us
  other arithmetic: 8.88 us -> 4.65 us
  local copies, waits for them, and re-layouts: 10.4 us -> 7.24 us
    ppermute x20 -> x11, starting transfers between devices: 98.6 us -> 73.4 us  [the longest x7 65.5 us: ring_permute(): lax.ppermute(value, axis, [(i, (i + steps) % count) for i in range(count)])]
    all_to_all x5, blocking collectives: 118 us -> 94 us  [exchanged(): lax.all_to_all(tiles, axis, 0, 0, tiled=True, axis_index_groups=groups)]
    pallas_call x0 -> x2, Pallas kernels: none -> 9.23 us  [the longest x1 5.15 us: run_backward(): pl.pallas_call(backward_kernel, out_shape=(jax.ShapeDtypeStruct((rows * c...]
    ppermute x20 -> x11, waiting for transfers between devices: 20.3 us -> 11.9 us  [the longest x7 6.77 us: ring_permute(): lax.ppermute(value, axis, [(i, (i + steps) % count) for i in range(count)])]
    all_to_all x1 -> x0, waiting for transfers between devices: 7.99 us -> none  [exchanged(): lax.all_to_all(tiles, axis, 0, 0, tiled=True, axis_index_groups=groups)]
    all_to_all x1 -> x0, starting transfers between devices: 3.57 us -> none  [exchanged(): lax.all_to_all(tiles, axis, 0, 0, tiled=True, axis_index_groups=groups)]
    dot_general x22 -> x8, matrix products: 7.86 us -> 7.03 us  [the longest x1 1.45 us: per_device(): jnp.einsum('pjkq,pqc->pjkc', filters, extended_in, preferred_element_type...]
  transfers between devices with their start and end apart: 21 -> 11, of which waited for: 13 -> 6; matrix products, arithmetic and copies ran while one was open for 3% -> 4% of each run, Pallas kernels for 0% -> 0%
where the time goes in v2:
time: 210 us; the launch traced here: 209 us
  blocking collectives  94 us (45%)
  starting transfers between devices  73.4 us (35%)
  waiting for transfers between devices  11.9 us (6%)
  Pallas kernels  9.23 us (4%)
  local copies, waits for them, and re-layouts  7.24 us (3%)
  matrix products  7.03 us (3%)
  other arithmetic  4.65 us (2%)
    all_to_all x5, blocking collectives, exchanged(): lax.all_to_all(tiles, axis, 0, 0, tiled=True, axis_index_groups=groups)  94 us
    ppermute x7, starting transfers between devices, ring_permute(): lax.ppermute(value, axis, [(i, (i + steps) % count) for i in range(count)])  65.5 us
    ppermute x4, starting transfers between devices, line_permute(): return lax.ppermute(value, axis, pairs)  7.89 us
    ppermute x7, waiting for transfers between devices, ring_permute(): lax.ppermute(value, axis, [(i, (i + steps) % count) for i in range(count)])  6.77 us
    ppermute x4, waiting for transfers between devices, line_permute(): return lax.ppermute(value, axis, pairs)  5.17 us
    pallas_call x1, Pallas kernels, run_backward(): pl.pallas_call(backward_kernel, out_shape=(jax.ShapeDtypeStruct((rows * c...  5.15 us
  transfers between devices with their start and end apart: 11, of which 6 were waited for; matrix products, arithmetic and copies ran while one was open for 4% of the time, Pallas kernels for 0%

profile of v2, /device:TPU:40, one launch (start us, length us, event | category | flops | bytes accessed | tf_op | source)
XLA Modules:
  0.0 208.7 jit_solution(10070161339261964990)
XLA Ops:
  0.6 0.0 copy-start
  0.6 0.9 fusion.19
  1.6 4.7 %collective-permute-start = (bf16[32,2,128]{2,1,0:T(2,128)(2,1)S(1)}, bf16[32,2,128]{2,1,0:T(2,128)(2,1)S(1)}, u32[]{:S(2)}, u32[]{:S(2)}) collective-permute-start(bf16[32,2,128]{2,1,0:T(2,128)(2,1)S(1)} %get-tuple-element.20), channel_id=1, source_target_pairs={{0,8},{8,16},{16,24},{24,32},{32,40},{40,48},{48,56},{56,64},{64,7... | collective-permute-start | bytes 49160 | tf_op jit(solution)/shard_map/ppermute | solution.py:19
  6.3 42.6 %collective-permute-start.1 = (bf16[32,2,128]{2,1,0:T(2,128)(2,1)S(1)}, bf16[32,2,128]{2,1,0:T(2,128)(2,1)S(1)}, u32[]{:S(2)}, u32[]{:S(2)}) collective-permute-start(bf16[32,2,128]{2,1,0:T(2,128)(2,1)S(1)} %get-tuple-element.21), channel_id=1, source_target_pairs={{0,248},{8,0},{16,8},{24,16},{32,24},{40,32},{48,40},{56,48},{64,5... | collective-permute-start | bytes 49160 | tf_op jit(solution)/shard_map/ppermute | solution.py:19
  48.9 0.7 broadcast_compare_fusion
  49.6 0.8 broadcast_select_fusion
  50.5 0.7 fusion.21
  51.2 1.1 fusion
  52.3 0.7 subtract_add_fusion
  53.0 0.1 slice.82
  53.2 0.1 slice.87
  53.3 0.1 reshape.108
  53.4 1.4 convolution_convert_fusion.2
  54.9 0.3 copy.20
  55.1 0.4 reshape.106
  55.5 0.3 fusion.23
  55.8 0.1 fusion.18
  55.9 0.1 convert_element_type.68
  56.0 1.5 collective-permute-start.2
  57.5 0.1 convert_element_type.69
  57.6 1.3 collective-permute-start.3
  58.9 0.0 copy-start.6
  58.9 0.5 copy.26
  59.5 0.3 copy-done.6
  59.8 2.6 %collective-permute-done.3 = bf16[64,512]{1,0:T(8,128)(2,1)S(1)} collective-permute-done((bf16[64,512]{1,0:T(8,128)(2,1)S(1)}, bf16[64,512]{1,0:T(8,128)(2,1)S(1)}, u32[]{:S(2)}, u32[]{:S(2)}) %collective-permute-start.3) | collective-permute-done | bytes 65568 | tf_op jit(solution)/shard_map/ppermute | solution.py:25
  62.5 0.0 copy-start.2
  62.5 0.1 add_convert_fusion.1
  62.6 0.2 convolution_convert_fusion.4
  62.9 0.2 copy-done.5
  63.1 1.9 collective-permute-start.4
  65.0 5.2 %collective-permute-start.5 = (bf16[464,256]{1,0:T(8,128)(2,1)S(1)}, bf16[464,256]{1,0:T(8,128)(2,1)S(1)}, u32[]{:S(2)}, u32[]{:S(2)}) collective-permute-start(bf16[464,256]{1,0:T(8,128)(2,1)S(1)} %get-tuple-element.22), channel_id=1, source_target_pairs={{0,248},{8,0},{16,8},{24,16},{32,24},{40,32},{48,40},{56,48},{64,5... | collective-permute-start | bytes 712712 | tf_op jit(solution)/shard_map/ppermute | solution.py:19
  70.2 1.0 fusion.12.vecs
  71.2 1.7 collective-permute-done.4.west.west_cot
  72.9 1.8 collective-permute-done.5.east.east_cot
  74.7 0.7 copy-done.4
  75.4 4.1 %forward.1 = (bf16[256,1024]{1,0:T(8,128)(2,1)}, f32[576,256]{1,0:T(8,128)}, bf16[256,1024]{1,0:T(8,128)(2,1)}, bf16[16,16,256]{2,1,0:T(8,128)(2,1)}, bf16[16,16,256]{2,1,0:T(8,128)(2,1)}) custom-call(f32[20,2688]{1,0:T(8,128)} %fusion.12.vecs, bf16[20,16,256]{2,1,0:T(8,128)(2,1)} %bitcast.50, bf16[464,256]{1,0:T(8,128)(2,1)} %copy-done.3, ...), custom_call_target="tpu_custom_call" | custom-call | tf_op jit(solution)/shard_map/forward/pallas_call | solution.py:254
  79.4 0.7 fusion.20
  80.2 3.7 %collective-permute-start.6 = (bf16[2,16,256]{2,1,0:T(8,128)(2,1)S(1)}, bf16[2,16,256]{2,1,0:T(8,128)(2,1)S(1)}, u32[]{:S(2)}, u32[]{:S(2)}) collective-permute-start(bf16[2,16,256]{2,1,0:T(8,128)(2,1)S(1)} %get-tuple-element.27), channel_id=1, source_target_pairs={{0,1},{1,2},{2,3},{3,4},{4,5},{5,6},{6,7},{8,9},{9,10},{10,11},{11... | collective-permute-start | bytes 49160 | tf_op jit(solution)/shard_map/ppermute | solution.py:25
  83.9 1.3 collective-permute-start.7
  85.3 0.9 constant_dynamic-update-slice_fusion.4
  86.2 2.6 %collective-permute-done.7 = bf16[2,16,256]{2,1,0:T(8,128)(2,1)S(1)} collective-permute-done((bf16[2,16,256]{2,1,0:T(8,128)(2,1)S(1)}, bf16[2,16,256]{2,1,0:T(8,128)(2,1)S(1)}, u32[]{:S(2)}, u32[]{:S(2)}) %collective-permute-start.7) | collective-permute-done | bytes 16416 | tf_op jit(solution)/shard_map/ppermute | solution.py:25
  88.8 1.9 collective-permute-start.8
  90.7 5.6 %collective-permute-start.9 = (bf16[20,16,256]{2,1,0:T(8,128)(2,1)S(1)}, bf16[20,16,256]{2,1,0:T(8,128)(2,1)S(1)}, u32[]{:S(2)}, u32[]{:S(2)}) collective-permute-start(bf16[20,16,256]{2,1,0:T(8,128)(2,1)S(1)} %constant_dynamic-update-slice_fusion.3.own), channel_id=1, source_target_pairs={{0,248},{8,0},{16,8},{24,16},{32,24},{40,32},{48,40},{56,48},{64,5... | collective-permute-start | bytes 491528 | tf_op jit(solution)/shard_map/ppermute | solution.py:19
  96.4 1.4 convolution_convert_fusion
  97.8 1.6 collective-permute-done.9.east
  99.4 0.7 copy-done.10
  100.1 5.2 %backward.1 = (bf16[256,256]{1,0:T(8,128)(2,1)}, bf16[16,16,256]{2,1,0:T(8,128)(2,1)}) custom-call(f32[20,2688]{1,0:T(8,128)} %fusion.12.vecs, bf16[20,16,256]{2,1,0:T(8,128)(2,1)} %copy-done.8, bf16[20,16,256]{2,1,0:T(8,128)(2,1)} %copy-done.9, bf16[20,16,256]{2,1,0:T(8,128)(2,1)} %copy-done.10, bf16[2,1024,256]{2,1,0:T(8,128)(2,1)} %weights.3, ...), custom_call_target="tpu_custom_call" | custom-call | tf_op jit(solution)/shard_map/backward/pallas_call | solution.py:280
  105.3 1.2 fusion.1
  106.5 0.4 convolution_convert_fusion.1
  106.9 0.1 pad_maximum_fusion
  107.0 0.1 constant_dynamic-slice_fusion
  107.0 3.6 %collective-permute-start.10 = (bf16[2560,128]{1,0:T(8,128)(2,1)S(1)}, bf16[2560,128]{1,0:T(8,128)(2,1)S(1)}, u32[]{:S(2)}, u32[]{:S(2)}) collective-permute-start(bf16[2560,128]{1,0:T(8,128)(2,1)S(1)} %constant_dynamic-slice_fusion), channel_id=1, source_target_pairs={{0,1},{1,0},{2,3},{3,2},{4,5},{5,4},{6,7},{7,6},{8,9},{9,8},{10,11... | collective-permute-start | bytes 1966088 | tf_op jit(solution)/shard_map/ppermute | solution.py:19
  110.6 1.7 collective-permute-done.10
  112.3 0.2 add_convert_fusion
  112.5 16.0 %all_to_all.25 = bf16[4,640,128]{2,1,0:T(8,128)(2,1)S(1)} all-to-all(bf16[4,640,128]{2,1,0:T(8,128)(2,1)S(1)} %bitcast.48), channel_id=1, replica_groups=mesh['ens'=2,'lon'=32,'lat'=4,'ch'=2] {'lat'}, dimensions={0} | all-to-all | bytes 1310720 | tf_op jit(solution)/shard_map/all_to_all | solution.py:42
  128.5 0.1 reduce_sum.36
  128.6 14.5 %all_to_all.26 = bf16[8,80,128]{2,1,0:T(8,128)(2,1)S(1)} all-to-all(bf16[8,80,128]{2,1,0:T(8,128)(2,1)S(1)} %bitcast.54), channel_id=1, replica_groups={{0,8,16,24,32,40,48,56},{64,72,80,88,96,104,112,120},{128,136,144,152,1..., dimensions={0} | all-to-all | bytes 327680 | tf_op jit(solution)/shard_map/all_to_all | solution.py:42
  143.2 35.2 %all_to_all.27 = bf16[4,80,128]{2,1,0:T(8,128)(2,1)S(1)} all-to-all(bf16[4,80,128]{2,1,0:T(8,128)(2,1)S(1)} %broadcast_in_dim.20), channel_id=1, replica_groups={{0,64,128,192},{8,72,136,200},{16,80,144,208},{24,88,152,216},{32,96,16..., dimensions={0} | all-to-all | bytes 163840 | tf_op jit(solution)/shard_map/all_to_all | solution.py:42
  178.4 17.1 %all_to_all.28 = bf16[8,80,128]{2,1,0:T(8,128)(2,1)S(1)} all-to-all(bf16[8,80,128]{2,1,0:T(8,128)(2,1)S(1)} %broadcast_in_dim.21), channel_id=1, replica_groups={{0,8,16,24,32,40,48,56},{64,72,80,88,96,104,112,120},{128,136,144,152,1..., dimensions={0} | all-to-all | bytes 327680 | tf_op jit(solution)/shard_map/all_to_all | solution.py:42
  195.5 0.1 broadcast_in_dim.40
  195.6 11.2 %all_to_all.29 = bf16[4,640,128]{2,1,0:T(8,128)(2,1)S(1)} all-to-all(bf16[4,640,128]{2,1,0:T(8,128)(2,1)S(1)} %broadcast_in_dim.40), channel_id=1, replica_groups=mesh['ens'=2,'lon'=32,'lat'=4,'ch'=2] {'lat'}, dimensions={0} | all-to-all | bytes 1310720 | tf_op jit(solution)/shard_map/all_to_all | solution.py:42
  206.8 0.1 bitcast_convert_fusion
  207.0 1.0 slice_multiply_fusion
  208.0 0.7 slice_multiply_fusion.1
  (51 shorter events, 0.4 us)
Async XLA Ops:
  0.6 61.9 %copy-start = (bf16[512,256]{1,0:T(8,128)(2,1)S(1)}, bf16[512,256]{1,0:T(8,128)(2,1)}, u32[]{:S(2)}) copy-start(bf16[512,256]{1,0:T(8,128)(2,1)} %param.13) | copy-start | bytes 786436
  1.6 51.8 %collective-permute-start = (bf16[32,2,128]{2,1,0:T(2,128)(2,1)S(1)}, bf16[32,2,128]{2,1,0:T(2,128)(2,1)S(1)}, u32[]{:S(2)}, u32[]{:S(2)}) collective-permute-start(bf16[32,2,128]{2,1,0:T(2,128)(2,1)S(1)} %get-tuple-element.20), channel_id=1, source_target_pairs={{0,8},{8,16},{16,24},{24,32},{32,40},{40,48},{48,56},{56,64},{64,7... | collective-permute-start | bytes 49160 | tf_op jit(solution)/shard_map/ppermute | solution.py:19
  6.3 47.1 %collective-permute-start.1 = (bf16[32,2,128]{2,1,0:T(2,128)(2,1)S(1)}, bf16[32,2,128]{2,1,0:T(2,128)(2,1)S(1)}, u32[]{:S(2)}, u32[]{:S(2)}) collective-permute-start(bf16[32,2,128]{2,1,0:T(2,128)(2,1)S(1)} %get-tuple-element.21), channel_id=1, source_target_pairs={{0,248},{8,0},{16,8},{24,16},{32,24},{40,32},{48,40},{56,48},{64,5... | collective-permute-start | bytes 49160 | tf_op jit(solution)/shard_map/ppermute | solution.py:19
  56.0 3.5 %collective-permute-start.2 = (bf16[64,512]{1,0:T(8,128)(2,1)S(1)}, bf16[64,512]{1,0:T(8,128)(2,1)S(1)}, u32[]{:S(2)}, u32[]{:S(2)}) collective-permute-start(bf16[64,512]{1,0:T(8,128)(2,1)S(1)} %fusion.9), channel_id=1, source_target_pairs={{0,1},{1,2},{2,3},{3,4},{4,5},{5,6},{6,7},{8,9},{9,10},{10,11},{11... | collective-permute-start | bytes 196616 | tf_op jit(solution)/shard_map/ppermute | solution.py:25
  57.6 4.8 %collective-permute-start.3 = (bf16[64,512]{1,0:T(8,128)(2,1)S(1)}, bf16[64,512]{1,0:T(8,128)(2,1)S(1)}, u32[]{:S(2)}, u32[]{:S(2)}) collective-permute-start(bf16[64,512]{1,0:T(8,128)(2,1)S(1)} %fusion.10), channel_id=1, source_target_pairs={{1,0},{2,1},{3,2},{4,3},{5,4},{6,5},{7,6},{9,8},{10,9},{11,10},{12... | collective-permute-start | bytes 196616 | tf_op jit(solution)/shard_map/ppermute | solution.py:25
  58.9 0.9 copy-start.6
  62.4 0.7 copy-start.5
  62.5 7.8 %copy-start.2 = (bf16[204,2688]{1,0:T(8,128)(2,1)S(1)}, bf16[204,2688]{1,0:T(8,128)(2,1)}, u32[]{:S(2)}) copy-start(bf16[204,2688]{1,0:T(8,128)(2,1)} %constant.42.clone) | copy-start | bytes 3290116
  62.8 11.9 %copy-start.1 = (bf16[320,256]{1,0:T(8,128)(2,1)}, bf16[320,256]{1,0:T(8,128)(2,1)S(1)}, u32[]{:S(2)}) copy-start(bf16[320,256]{1,0:T(8,128)(2,1)S(1)} %convolution_convert_fusion.4) | copy-start | bytes 491524
  63.1 9.8 %collective-permute-start.4 = (bf16[464,256]{1,0:T(8,128)(2,1)S(1)}, bf16[464,256]{1,0:T(8,128)(2,1)S(1)}, u32[]{:S(2)}, u32[]{:S(2)}) collective-permute-start(bf16[464,256]{1,0:T(8,128)(2,1)S(1)} %get-tuple-element.23), channel_id=1, source_target_pairs={{0,8},{8,16},{16,24},{24,32},{32,40},{40,48},{48,56},{56,64},{64,7... | collective-permute-start | bytes 712712 | tf_op jit(solution)/shard_map/ppermute | solution.py:19
  65.0 9.6 %collective-permute-start.5 = (bf16[464,256]{1,0:T(8,128)(2,1)S(1)}, bf16[464,256]{1,0:T(8,128)(2,1)S(1)}, u32[]{:S(2)}, u32[]{:S(2)}) collective-permute-start(bf16[464,256]{1,0:T(8,128)(2,1)S(1)} %get-tuple-element.22), channel_id=1, source_target_pairs={{0,248},{8,0},{16,8},{24,16},{32,24},{40,32},{48,40},{56,48},{64,5... | collective-permute-start | bytes 712712 | tf_op jit(solution)/shard_map/ppermute | solution.py:19
  72.9 1.8 copy-start.3
  74.7 0.7 copy-start.4
  80.2 5.1 %collective-permute-start.6 = (bf16[2,16,256]{2,1,0:T(8,128)(2,1)S(1)}, bf16[2,16,256]{2,1,0:T(8,128)(2,1)S(1)}, u32[]{:S(2)}, u32[]{:S(2)}) collective-permute-start(bf16[2,16,256]{2,1,0:T(8,128)(2,1)S(1)} %get-tuple-element.27), channel_id=1, source_target_pairs={{0,1},{1,2},{2,3},{3,4},{4,5},{5,6},{6,7},{8,9},{9,10},{10,11},{11... | collective-permute-start | bytes 49160 | tf_op jit(solution)/shard_map/ppermute | solution.py:25
  83.9 4.9 %collective-permute-start.7 = (bf16[2,16,256]{2,1,0:T(8,128)(2,1)S(1)}, bf16[2,16,256]{2,1,0:T(8,128)(2,1)S(1)}, u32[]{:S(2)}, u32[]{:S(2)}) collective-permute-start(bf16[2,16,256]{2,1,0:T(8,128)(2,1)S(1)} %get-tuple-element.26), channel_id=1, source_target_pairs={{1,0},{2,1},{3,2},{4,3},{5,4},{6,5},{7,6},{9,8},{10,9},{11,10},{12... | collective-permute-start | bytes 49160 | tf_op jit(solution)/shard_map/ppermute | solution.py:25
  88.8 10.7 %copy-start.8 = (bf16[20,16,256]{2,1,0:T(8,128)(2,1)}, bf16[20,16,256]{2,1,0:T(8,128)(2,1)S(1)}, u32[]{:S(2)}) copy-start(bf16[20,16,256]{2,1,0:T(8,128)(2,1)S(1)} %constant_dynamic-update-slice_fusion.3.own) | copy-start | bytes 491524
  88.8 9.0 %collective-permute-start.8 = (bf16[20,16,256]{2,1,0:T(8,128)(2,1)S(1)}, bf16[20,16,256]{2,1,0:T(8,128)(2,1)S(1)}, u32[]{:S(2)}, u32[]{:S(2)}) collective-permute-start(bf16[20,16,256]{2,1,0:T(8,128)(2,1)S(1)} %constant_dynamic-update-slice_fusion.3.own), channel_id=1, source_target_pairs={{0,8},{8,16},{16,24},{24,32},{32,40},{40,48},{48,56},{56,64},{64,7... | collective-permute-start | bytes 491528 | tf_op jit(solution)/shard_map/ppermute | solution.py:19
  90.7 8.7 %collective-permute-start.9 = (bf16[20,16,256]{2,1,0:T(8,128)(2,1)S(1)}, bf16[20,16,256]{2,1,0:T(8,128)(2,1)S(1)}, u32[]{:S(2)}, u32[]{:S(2)}) collective-permute-start(bf16[20,16,256]{2,1,0:T(8,128)(2,1)S(1)} %constant_dynamic-update-slice_fusion.3.own), channel_id=1, source_target_pairs={{0,248},{8,0},{16,8},{24,16},{32,24},{40,32},{48,40},{56,48},{64,5... | collective-permute-start | bytes 491528 | tf_op jit(solution)/shard_map/ppermute | solution.py:19
  97.8 1.6 copy-start.9
  99.4 0.7 copy-start.10
  105.2 1.2 copy-start.7
  105.3 1.3 copy-start.11
  107.0 5.3 %collective-permute-start.10 = (bf16[2560,128]{1,0:T(8,128)(2,1)S(1)}, bf16[2560,128]{1,0:T(8,128)(2,1)S(1)}, u32[]{:S(2)}, u32[]{:S(2)}) collective-permute-start(bf16[2560,128]{1,0:T(8,128)(2,1)S(1)} %constant_dynamic-slice_fusion), channel_id=1, source_target_pairs={{0,1},{1,0},{2,3},{3,2},{4,5},{5,4},{6,7},{7,6},{8,9},{9,8},{10,11... | collective-permute-start | bytes 1966088 | tf_op jit(solution)/shard_map/ppermute | solution.py:19

commit v3 on v2

--- a/solution.py
+++ b/solution.py
@@ -125,22 +125,20 @@
 def forward_kernel(
     vecs, own, west, east, weights, cot, feat0, pre0, feat1, state2, act1, s0, wide, s1
 ):
-    rows, cols = cot.shape[0], cot.shape[1]
-    channels = cot.shape[2]
+    rows, cols, channels = state2.shape
     basis_count = weights.shape[1] // channels
     mid = cols + 2 * REACH
-    for i in range(rows + 4):
-        s0[i * 64 : i * 64 + cols] = west[i * cols : (i + 1) * cols]
+    for i in range(rows + 8):
+        s0[i * 64 : i * 64 + cols] = west[i]
         s0[i * 64 + cols : i * 64 + 2 * cols] = own[i]
-        s0[i * 64 + 2 * cols : i * 64 + 3 * cols] = east[i * cols : (i + 1) * cols]
+        s0[i * 64 + 2 * cols : i * 64 + 3 * cols] = east[i]
         s0[i * 64 + 3 * cols : (i + 1) * 64] = jnp.zeros((64 - 3 * cols, channels), jnp.bfloat16)
-    s0[(rows + 4) * 64 :] = jnp.zeros((64, channels), jnp.bfloat16)
-    for i in range(rows + 2):
+    s0[(rows + 8) * 64 :] = jnp.zeros((64, channels), jnp.bfloat16)
+    for i in range(rows + 6):
         band = jnp.concatenate(
             [
                 jnp.concatenate(
-                    [slanted(vecs, i + 1, FORWARD_WIDE + 2 * k + h, mid) for h in range(2)],
-                    axis=1,
+                    [slanted(vecs, i, FORWARD_WIDE + 2 * k + h, mid) for h in range(2)], axis=1
                 )
                 for k in range(basis_count)
             ],
@@ -152,20 +150,20 @@
             wide[i * mid : (i + 1) * mid, k * channels : (k + 1) * channels] = part.astype(
                 jnp.bfloat16
             )
-            if 1 <= i <= rows:
-                feat0[(i - 1) * cols : i * cols, k * channels : (k + 1) * channels] = part[
+            if 3 <= i < rows + 3:
+                feat0[(i - 3) * cols : (i - 2) * cols, k * channels : (k + 1) * channels] = part[
                     REACH : REACH + cols
                 ].astype(jnp.bfloat16)
     pre0[...] = dot(wide[...], weights[0])
-    for i in range(rows + 2):
+    for i in range(rows + 6):
         pre = pre0[i * mid : (i + 1) * mid]
         before = s0[(i + 1) * 64 : (i + 1) * 64 + 3 * cols].astype(jnp.float32)
         before = before[REACH : REACH + mid]
         s1[i * mid : (i + 1) * mid] = (before + pre * jax.nn.sigmoid(pre)).astype(jnp.bfloat16)
-    s1[(rows + 2) * mid :] = jnp.zeros((mid, channels), jnp.bfloat16)
-    for i in range(rows):
+    s1[(rows + 6) * mid :] = jnp.zeros((mid, channels), jnp.bfloat16)
+    for i in range(rows + 4):
         band = jnp.concatenate(
-            [slanted(vecs, i + 2, FORWARD_THIN + k, cols) for k in range(basis_count)], axis=0
+            [slanted(vecs, i + 1, FORWARD_THIN + k, cols) for k in range(basis_count)], axis=0
         )
         out = dot(band, s1[i * mid : (i + 4) * mid])
         for k in range(basis_count):
@@ -173,23 +171,21 @@
                 k * cols : (k + 1) * cols
             ].astype(jnp.bfloat16)
     pre1 = dot(feat1[...], weights[1])
-    for i in range(rows):
+    for i in range(rows + 4):
         pre = pre1[i * cols : (i + 1) * cols]
         sigma = jax.nn.sigmoid(pre)
-        before = s1[(i + 1) * mid : (i + 2) * mid].astype(jnp.float32)[REACH : REACH + cols]
-        state2[i] = (before + pre * sigma).astype(jnp.bfloat16)
-        upstream = cot[i].astype(jnp.float32)
+        if 2 <= i < rows + 2:
+            before = s1[(i + 1) * mid : (i + 2) * mid].astype(jnp.float32)[REACH : REACH + cols]
+            state2[i - 2] = (before + pre * sigma).astype(jnp.bfloat16)
+        upstream = cot[i].astype(jnp.float32)[REACH : REACH + cols]
         act1[i] = (upstream * sigma * (1.0 + pre * (1.0 - sigma))).astype(jnp.bfloat16)
 
 
-def backward_kernel(
-    vecs, own, west, east, weights, pre0, cot, west_cot, east_cot, act0, grad0, a1, e1, g1, a0, e0
-):
+def backward_kernel(vecs, own, west, east, weights, pre0, cot, act0, grad0, a1, e1, g1, a0, e0):
     rows, cols, channels = grad0.shape
     basis_count = weights.shape[1] // channels
     mid = cols + 2 * REACH
     full = 3 * cols
-    skip = (rows + 4) * cols
     for i in range(rows + 4):
         a1[i * full : i * full + cols] = west[i]
         a1[i * full + cols : i * full + 2 * cols] = own[i]
@@ -201,27 +197,28 @@
             first = (i * basis_count + k) * 64
             e1[first : first + full] = errors[i * full : (i + 1) * full]
             e1[first + full : first + 64] = jnp.zeros((64 - full, channels), jnp.bfloat16)
-    for i in range(rows + 2):
+    parts = []
+    for i in range(-2, rows + 2):
+        row = i + 2
         band = jnp.concatenate(
             [
-                slanted(vecs, i + s, BACKWARD_WIDE + (2 - s) * 2 + h, mid)
-                for s in range(3)
-                for h in range(2)
-            ],
-            axis=1,
-        )
-        spread = dot(band, e1[i * basis_count * 64 : (i + 3) * basis_count * 64])
-        upstream = jnp.concatenate(
-            [
-                west_cot[skip + i * REACH : skip + (i + 1) * REACH].astype(jnp.float32),
-                cot[i].astype(jnp.float32),
-                east_cot[skip + i * REACH : skip + (i + 1) * REACH].astype(jnp.float32),
+                jnp.concatenate(
+                    [slanted(vecs, row + 1, BACKWARD_WIDE + 2 * r + h, mid) for h in range(2)],
+                    axis=1,
+                )
+                for r in range(3)
             ],
             axis=0,
         )
-        grad = (upstream + spread).astype(jnp.bfloat16).astype(jnp.float32)
+        parts.append(dot(band, e1[row * basis_count * 64 : (row + 1) * basis_count * 64]))
+        if i < 0:
+            continue
+        spread = (
+            parts[i][2 * mid :] + parts[i + 1][mid : 2 * mid] + parts[i + 2][:mid]
+        )
+        grad = (cot[i + 1].astype(jnp.float32) + spread).astype(jnp.bfloat16).astype(jnp.float32)
         g1[i * mid : (i + 1) * mid] = grad
-        pre = pre0[i * mid : (i + 1) * mid]
+        pre = pre0[(i + 2) * mid : (i + 3) * mid]
         sigma = jax.nn.sigmoid(pre)
         act = grad * sigma * (1.0 + pre * (1.0 - sigma))
         a0[i * mid : (i + 1) * mid] = act.astype(jnp.bfloat16)
@@ -233,21 +230,103 @@
         for i in range(rows + 2):
             first = (i * basis_count + k) * mid
             e0[first : first + mid] = errors[i * mid : (i + 1) * mid]
-    for i in range(rows):
+    parts = []
+    for i in range(-2, rows):
+        row = i + 2
         band = jnp.concatenate(
-            [slanted(vecs, i + s + 1, BACKWARD_THIN + 2 - s, cols) for s in range(3)], axis=1
+            [slanted(vecs, row + 2, BACKWARD_THIN + r, cols) for r in range(3)], axis=0
         )
-        spread = dot(band, e0[i * basis_count * mid : (i + 3) * basis_count * mid])
+        parts.append(dot(band, e0[row * basis_count * mid : (row + 1) * basis_count * mid]))
+        if i < 0:
+            continue
+        spread = parts[i][2 * cols :] + parts[i + 1][cols : 2 * cols] + parts[i + 2][:cols]
         before = g1[(i + 1) * mid + REACH : (i + 1) * mid + REACH + cols]
         grad0[i] = (before + spread).astype(jnp.bfloat16)
 
 
+def encoder_kernel(
+    first, owner, taps, field, west, east, cot, masked, partial, down, up, acc
+):
+    rows_in, cols_in, width = field.shape
+    rows, cols, channels = cot.shape
+    basis_count = taps.shape[1]
+    depth = cols_in + 16
+    steps = lax.broadcasted_iota(jnp.int32, (16, width), 0)
+    acc[...] = jnp.zeros_like(acc)
+    for p in range(rows_in):
+        pieces = []
+        for k in range(basis_count):
+            vector = jnp.broadcast_to(taps[p, k : k + 1], (cols, LANES))
+            pieces.append(pltpu.roll(vector, 0, 1, stride=2, stride_axis=0))
+        band = jnp.concatenate(pieces, axis=0).astype(jnp.bfloat16)[:, :depth]
+        edges = jnp.zeros((16, width), jnp.float32)
+        for t in range(TAP_REACH):
+            column = slice(t * width, (t + 1) * width)
+            edges = jnp.where(steps == t, east[p : p + 1, column].astype(jnp.float32), edges)
+            edges = jnp.where(
+                steps == 16 - TAP_REACH + t, west[p : p + 1, column].astype(jnp.float32), edges
+            )
+        out = dot(band, jnp.concatenate([field[p], edges.astype(jnp.bfloat16)], axis=0))
+        target = owner[p] - first[0]
+        acc[target] += out.astype(jnp.bfloat16).astype(jnp.float32)
+    for i in range(rows + 2):
+        for k in range(basis_count):
+            part = acc[i, k * cols : (k + 1) * cols]
+            columns = slice(k * width, (k + 1) * width)
+            partial[i, :, columns] = part
+            if i < 5:
+                up[i * cols : (i + 1) * cols, columns] = part.astype(jnp.bfloat16)
+            if i >= rows - 3:
+                n = i - rows + 3
+                down[n * cols : (n + 1) * cols, columns] = part.astype(jnp.bfloat16)
+    mid = cols + 2 * REACH
+    for message, where, kept in ((down, rows - 2, rows - 8), (up, 0, 0)):
+        for n in range(2):
+            at = rows_in + (where + n) * REACH
+            wide = jnp.concatenate(
+                [
+                    west[at : at + REACH].astype(jnp.float32),
+                    cot[where + n].astype(jnp.float32),
+                    east[at : at + REACH].astype(jnp.float32),
+                ],
+                axis=0,
+            )
+            message[5 * cols : 5 * cols + mid, n * channels : (n + 1) * channels] = wide.astype(
+                jnp.bfloat16
+            )
+        message[5 * cols + mid :] = jnp.zeros((8, 2 * channels), jnp.bfloat16)
+        message[5 * cols + mid :, : masked.shape[1]] = masked[kept : kept + 8]
+
+
 def in_vmem(count):
     return [pl.BlockSpec(memory_space=pltpu.VMEM)] * count
 
 
+GRANT = pltpu.CompilerParams(vmem_limit_bytes=26 * 2**20)
+
+
+def run_encoder(first, owner, taps, field, west, east, cot, masked):
+    rows, cols, channels = cot.shape
+    basis_count, width = taps.shape[1], field.shape[2]
+    message = jax.ShapeDtypeStruct((5 * cols + cols + 2 * REACH + 8, 2 * channels), jnp.bfloat16)
+    return pl.pallas_call(
+        encoder_kernel,
+        out_shape=(
+            jax.ShapeDtypeStruct((rows + 2, cols, basis_count * width), jnp.float32),
+            message,
+            message,
+        ),
+        in_specs=[pl.BlockSpec(memory_space=pltpu.SMEM)] * 2 + in_vmem(6),
+        out_specs=tuple(in_vmem(3)),
+        scratch_shapes=[pltpu.VMEM((rows + 2, basis_count * cols, width), jnp.float32)],
+        compiler_params=GRANT,
+        name="encoder",
+    )(first, owner, taps, field, west, east, cot, masked)
+
+
 def run_forward(vecs, own, west, east, weights, cot):
-    rows, cols, channels = cot.shape
+    rows, cols, channels = own.shape
+    rows -= 8
     depth = weights.shape[1]
     mid = cols + 2 * REACH
     bf16, f32 = jnp.bfloat16, jnp.float32
@@ -255,23 +334,24 @@
         forward_kernel,
         out_shape=(
             jax.ShapeDtypeStruct((rows * cols, depth), bf16),
-            jax.ShapeDtypeStruct(((rows + 2) * mid, channels), f32),
-            jax.ShapeDtypeStruct((rows * cols, depth), bf16),
+            jax.ShapeDtypeStruct(((rows + 6) * mid, channels), f32),
+            jax.ShapeDtypeStruct(((rows + 4) * cols, depth), bf16),
             jax.ShapeDtypeStruct((rows, cols, channels), bf16),
-            jax.ShapeDtypeStruct((rows, cols, channels), bf16),
+            jax.ShapeDtypeStruct((rows + 4, cols, channels), bf16),
         ),
         in_specs=in_vmem(6),
         out_specs=tuple(in_vmem(5)),
         scratch_shapes=[
-            pltpu.VMEM(((rows + 5) * 64, channels), bf16),
-            pltpu.VMEM(((rows + 2) * mid, depth), bf16),
-            pltpu.VMEM(((rows + 3) * mid, channels), bf16),
+            pltpu.VMEM(((rows + 9) * 64, channels), bf16),
+            pltpu.VMEM(((rows + 6) * mid, depth), bf16),
+            pltpu.VMEM(((rows + 7) * mid, channels), bf16),
         ],
+        compiler_params=GRANT,
         name="forward",
     )(vecs, own, west, east, weights, cot)
 
 
-def run_backward(vecs, own, west, east, weights, pre0, cot, west_cot, east_cot):
+def run_backward(vecs, own, west, east, weights, pre0, cot):
     rows, cols, channels = own.shape
     rows -= 4
     basis_count = weights.shape[1] // channels
@@ -283,7 +363,7 @@
             jax.ShapeDtypeStruct((rows * cols, channels), bf16),
             jax.ShapeDtypeStruct((rows, cols, channels), bf16),
         ),
-        in_specs=in_vmem(9),
+        in_specs=in_vmem(7),
         out_specs=tuple(in_vmem(2)),
         scratch_shapes=[
             pltpu.VMEM(((rows + 4) * 3 * cols, channels), bf16),
@@ -292,8 +372,9 @@
             pltpu.VMEM(((rows + 2) * mid, channels), bf16),
             pltpu.VMEM(((rows + 2) * basis_count * mid, channels), bf16),
         ],
+        compiler_params=GRANT,
         name="backward",
-    )(vecs, own, west, east, weights, pre0, cot, west_cot, east_cot)
+    )(vecs, own, west, east, weights, pre0, cot)
 
 
 def per_device(
@@ -315,90 +396,93 @@
     latent_width = basis_count * in_width
     f32, bf16 = jnp.float32, jnp.bfloat16
 
-    from_west = ring_permute(input_field[:, cols_in - TAP_REACH :], "lon", 1)
-    from_east = ring_permute(input_field[:, :TAP_REACH], "lon", -1)
+    def side_message(columns, cot_columns):
+        return jnp.concatenate(
+            [columns.reshape(rows_in, -1), cot_columns.reshape(-1, channels)]
+        )
+
+    west_side = ring_permute(
+        side_message(input_field[:, cols_in - TAP_REACH :], cotangent[:, cols_dev - REACH :]),
+        "lon",
+        1,
+    )
+    east_side = ring_permute(
+        side_message(input_field[:, :TAP_REACH], cotangent[:, :REACH]), "lon", -1
+    )
+    cot_mid = jnp.concatenate(
+        [
+            west_side[rows_in:].reshape(rows_dev, REACH, channels),
+            cotangent,
+            east_side[rows_in:].reshape(rows_dev, REACH, channels),
+        ],
+        axis=1,
+    )
     offsets = jnp.abs(jnp.arange(span, dtype=jnp.int32) - REACH)
     keep = offsets[None, :] <= row_widths[:, None]
     masked = jnp.where(keep[:, None, None, :], disco_basis, jnp.zeros_like(disco_basis))
     masked = masked.reshape(rows_dev, -1)
-    taps_at = (
-        np.arange(cols_in + 2 * TAP_REACH)[None, :, None] - 2 * np.arange(cols_dev)[:, None, None]
-        == np.arange(tap_count)[None, None, :]
-    )
-    filters = jnp.einsum(
-        "pkt,jqt->pjkq", encoder_filter, jnp.asarray(taps_at, bf16), preferred_element_type=f32
-    ).astype(bf16)
-    extended_in = jnp.concatenate([from_west, input_field, from_east], axis=1)
-    filtered = jnp.einsum("pjkq,pqc->pjkc", filters, extended_in, preferred_element_type=f32)
-    filtered = filtered.astype(bf16).reshape(rows_in, cols_dev * latent_width)
-    first_row = lax.axis_index(BAND) * rows_dev
-    relative = row_owner - first_row + 1
-    selector = (relative[None, :] == jnp.arange(rows_dev + 2, dtype=jnp.int32)[:, None]).astype(bf16)
-    partial = jnp.dot(selector, filtered, preferred_element_type=f32)
-    partial = partial.reshape(rows_dev + 2, cols_dev, latent_width)
-
-    def edge_message(latent_rows, cot_row, basis_rows):
-        basis_rows = jnp.pad(basis_rows, ((0, 6), (0, latent_width - basis_rows.shape[1])))
-        return jnp.concatenate(
-            [
-                latent_rows.astype(bf16).reshape(-1, latent_width),
-                cot_row.reshape(-1, latent_width),
-                basis_rows,
-            ]
-        )
-
-    above = line_permute(edge_message(partial[-3:], cotangent[-1:], masked[-2:]), BAND, 1)
-    below = line_permute(edge_message(partial[:3], cotangent[:1], masked[:2]), BAND, -1)
-    lat_rows = 3 * cols_dev
-    cot_rows = cols_dev * channels // latent_width
-
-    def opened(message):
-        latent = message[:lat_rows].reshape(3, cols_dev, latent_width).astype(f32)
-        cot = message[lat_rows : lat_rows + cot_rows].reshape(1, cols_dev, channels)
-        return latent, cot, message[lat_rows + cot_rows :][:2, : masked.shape[1]]
-
-    above_latent, above_cot, above_basis = opened(above)
-    below_latent, below_cot, below_basis = opened(below)
-    tail = rows_dev + 1
+    first_row = lax.axis_index(BAND) * rows_dev - 1
+    tap_lanes = np.zeros((tap_count, LANES), np.float32)
+    for t in range(tap_count):
+        tap_lanes[t, (t - TAP_REACH) % LANES] = 1
+        if t < TAP_REACH:
+            tap_lanes[t, cols_in + 16 - TAP_REACH + t] = 1
+    taps = jnp.einsum(
+        "pkt,tl->pkl", encoder_filter, jnp.asarray(tap_lanes, bf16), preferred_element_type=f32
+    )
+    partial, down, up = run_encoder(
+        first_row.reshape(1), row_owner, taps, input_field, west_side, east_side, cotangent, masked
+    )
+    above = line_permute(down, BAND, 1)
+    below = line_permute(up, BAND, -1)
+    lat_rows = 5 * cols_dev
+
+    def opened(message, kept):
+        latent = message[:lat_rows].reshape(5, cols_dev, latent_width).astype(f32)
+        cot = message[lat_rows:-8]
+        cot = jnp.stack([cot[:, :channels], cot[:, channels:]])
+        return latent, cot, message[-8:][kept, : masked.shape[1]]
+
+    above_latent, above_cot, above_basis = opened(above, slice(5, 8))
+    below_latent, below_cot, below_basis = opened(below, slice(0, 3))
+    tail = rows_dev + 3
     latent = (
-        jnp.pad(partial, ((1, 1), (0, 0), (0, 0)))
+        jnp.pad(partial, ((3, 3), (0, 0), (0, 0)))
         + jnp.pad(above_latent, ((0, tail), (0, 0), (0, 0)))
         + jnp.pad(below_latent, ((tail, 0), (0, 0), (0, 0)))
     ).astype(bf16)
     state0 = jnp.dot(
         latent.reshape(-1, latent_width), encoder_weight, preferred_element_type=f32
     ).astype(bf16)
-    cot_rows_ext = jnp.concatenate([above_cot, cotangent, below_cot])
-    to_east = jnp.concatenate([state0, cot_rows_ext[:, -REACH:].reshape(-1, channels)])
-    to_west = jnp.concatenate([state0, cot_rows_ext[:, :REACH].reshape(-1, channels)])
-    west = ring_permute(to_east, "lon", 1)
-    east = ring_permute(to_west, "lon", -1)
+    state0 = state0.reshape(rows_dev + 8, cols_dev, channels)
+    west = ring_permute(state0, "lon", 1)
+    east = ring_permute(state0, "lon", -1)
+    cot_ext = jnp.concatenate([above_cot, cot_mid, below_cot])
     basis_ext = jnp.concatenate([above_basis, masked, below_basis])
     vecs = jnp.dot(
         basis_ext, jnp.asarray(placement(basis_count, span), bf16), preferred_element_type=f32
     )
-    state0 = state0.reshape(rows_dev + 4, cols_dev, channels)
     feat0, pre0, feat1, state_out, act1 = run_forward(
-        vecs, state0, west, east, block_weights, cotangent
-    )
-
-    act_above = line_permute(act1[-2:], BAND, 1)
-    act_below = line_permute(act1[:2], BAND, -1)
-    act_rows = jnp.concatenate([act_above, act1, act_below])
-    act_west = ring_permute(act_rows, "lon", 1)
-    act_east = ring_permute(act_rows, "lon", -1)
+        vecs, state0, west, east, block_weights, cot_ext
+    )
+
+    act_west = ring_permute(act1, "lon", 1)
+    act_east = ring_permute(act1, "lon", -1)
+    inner = slice(2 * cols_dev, 2 * cols_dev + cell_count)
     weight1 = lax.dot_general(
-        feat1, act1.reshape(cell_count, channels), (((0,), (0,)), ((), ())),
+        feat1[inner],
+        act1.reshape(-1, channels)[inner],
+        (((0,), (0,)), ((), ())),
         preferred_element_type=f32,
     )
     act0, gradient = run_backward(
-        vecs, act_rows, act_west, act_east, block_weights, pre0, cot_rows_ext, west, east
+        vecs, act1, act_west, act_east, block_weights, pre0, cot_ext
     )
     weight0 = lax.dot_general(
         feat0, act0, (((0,), (0,)), ((), ())), preferred_element_type=f32
     )
     encoder_term = lax.dot_general(
-        latent[2 : rows_dev + 2].reshape(cell_count, latent_width),
+        latent[4 : rows_dev + 4].reshape(cell_count, latent_width),
         gradient.reshape(cell_count, channels),
         (((0,), (0,)), ((), ())),
         preferred_element_type=f32,

time: 210 us -> 195 us (0.929)
  starting transfers between devices: 73.4 us -> 68.1 us
  local copies, waits for them, and re-layouts: 7.24 us -> 2.96 us
  matrix products: 7.03 us -> 3.31 us
  blocking collectives: 94 us -> 97.1 us
  Pallas kernels: 9.23 us -> 6.82 us
    ppermute x4 -> x2, starting transfers between devices: 7.89 us -> 2.87 us  [line_permute(): return lax.ppermute(value, axis, pairs)]
    all_to_all x5, blocking collectives: 94 us -> 97.1 us  [exchanged(): lax.all_to_all(tiles, axis, 0, 0, tiled=True, axis_index_groups=groups)]
    dot_general x5 -> x3, matrix products: 5.45 us -> 2.42 us  [the longest x1 1.16 us: per_device(): lax.dot_general(latent[4:rows_dev + 4].reshape(cell_count, latent_width),...]
    unnamed x29 -> x17, local copies, waits for them, and re-layouts: 3.33 us -> 0.7 us
    ppermute x4 -> x2, waiting for transfers between devices: 5.17 us -> 3.51 us  [line_permute(): return lax.ppermute(value, axis, pairs)]
  transfers between devices with their start and end apart: 11 -> 9, of which waited for: 6 -> 6; matrix products, arithmetic and copies ran while one was open for 4% -> 2% of each run, Pallas kernels for 0% -> 0%
where the time goes in v3:
time: 195 us; the launch traced here: 194 us
  blocking collectives  97.1 us (50%)
  starting transfers between devices  68.1 us (35%)
  waiting for transfers between devices  11.1 us (6%)
  Pallas kernels  6.82 us (3%)
  other arithmetic  3.98 us (2%)
  matrix products  3.31 us (2%)
  local copies, waits for them, and re-layouts  2.96 us (2%)
    all_to_all x5, blocking collectives, exchanged(): lax.all_to_all(tiles, axis, 0, 0, tiled=True, axis_index_groups=groups)  97.1 us
    ppermute x7, starting transfers between devices, ring_permute(): lax.ppermute(value, axis, [(i, (i + steps) % count) for i in range(count)])  65.2 us
    ppermute x7, waiting for transfers between devices, ring_permute(): lax.ppermute(value, axis, [(i, (i + steps) % count) for i in range(count)])  7.63 us
  transfers between devices with their start and end apart: 9, of which 6 were waited for; matrix products, arithmetic and copies ran while one was open for 2% of the time, Pallas kernels for 0%

profile of v3, /device:TPU:40, one launch (start us, length us, event | category | flops | bytes accessed | tf_op | source)
XLA Modules:
  0.0 194.5 jit_solution(10257457672927667431)
XLA Ops:
  0.6 0.0 copy-start
  0.6 0.0 copy-start.2
  0.7 0.0 copy-start.3
  0.7 0.9 slice_bitcast_fusion.2
  1.6 0.9 fusion.10
  2.5 4.7 %collective-permute-start = (bf16[160,256]{1,0:T(8,128)(2,1)S(1)}, bf16[160,256]{1,0:T(8,128)(2,1)S(1)}, u32[]{:S(2)}, u32[]{:S(2)}) collective-permute-start(bf16[160,256]{1,0:T(8,128)(2,1)S(1)} %pad_maximum_fusion.1), channel_id=1, source_target_pairs={{0,8},{8,16},{16,24},{24,32},{32,40},{40,48},{48,56},{56,64},{64,7... | collective-permute-start | bytes 245768 | tf_op jit(solution)/shard_map/ppermute | solution.py:19
  7.3 42.6 %collective-permute-start.1 = (bf16[160,256]{1,0:T(8,128)(2,1)S(1)}, bf16[160,256]{1,0:T(8,128)(2,1)S(1)}, u32[]{:S(2)}, u32[]{:S(2)}) collective-permute-start(bf16[160,256]{1,0:T(8,128)(2,1)S(1)} %pad_maximum_fusion.2), channel_id=1, source_target_pairs={{0,248},{8,0},{16,8},{24,16},{32,24},{40,32},{48,40},{56,48},{64,5... | collective-permute-start | bytes 245768 | tf_op jit(solution)/shard_map/ppermute | solution.py:19
  49.9 0.7 broadcast_compare_fusion
  50.6 0.8 broadcast_select_fusion
  51.5 0.9 fusion.7
  52.4 0.1 reshape.96.masked
  52.6 0.0 collective-permute-done.west
  52.6 0.0 collective-permute-done.1.east
  52.6 0.0 copy-done.2
  52.6 0.0 copy-done.3
  52.6 0.0 copy-start.4
  52.6 0.6 copy-done.4
  53.3 1.1 encoder.1
  54.3 1.6 collective-permute-start.2
  55.9 1.3 collective-permute-start.3
  57.3 0.0 collective-permute-done.2
  57.3 3.5 %collective-permute-done.3 = bf16[120,512]{1,0:T(8,128)(2,1)S(1)} collective-permute-done((bf16[120,512]{1,0:T(8,128)(2,1)S(1)}, bf16[120,512]{1,0:T(8,128)(2,1)S(1)}, u32[]{:S(2)}, u32[]{:S(2)}) %collective-permute-start.3) | collective-permute-done | bytes 122912 | tf_op jit(solution)/shard_map/ppermute | solution.py:25
  60.8 0.0 copy-start.5
  60.8 0.1 add_convert_fusion.1
  60.9 0.0 copy-done
  60.9 0.0 copy-start.1
  60.9 0.3 convolution_convert_fusion.2
  61.2 2.1 %collective-permute-start.4 = (bf16[24,16,256]{2,1,0:T(8,128)(2,1)S(1)}, bf16[24,16,256]{2,1,0:T(8,128)(2,1)S(1)}, u32[]{:S(2)}, u32[]{:S(2)}) collective-permute-start(bf16[24,16,256]{2,1,0:T(8,128)(2,1)S(1)} %bitcast.62), channel_id=1, source_target_pairs={{0,8},{8,16},{16,24},{24,32},{32,40},{40,48},{48,56},{56,64},{64,7... | collective-permute-start | bytes 589832 | tf_op jit(solution)/shard_map/ppermute | solution.py:19
  63.2 5.2 %collective-permute-start.5 = (bf16[24,16,256]{2,1,0:T(8,128)(2,1)S(1)}, bf16[24,16,256]{2,1,0:T(8,128)(2,1)S(1)}, u32[]{:S(2)}, u32[]{:S(2)}) collective-permute-start(bf16[24,16,256]{2,1,0:T(8,128)(2,1)S(1)} %bitcast.63), channel_id=1, source_target_pairs={{0,248},{8,0},{16,8},{24,16},{32,24},{40,32},{48,40},{56,48},{64,5... | collective-permute-start | bytes 589832 | tf_op jit(solution)/shard_map/ppermute | solution.py:19
  68.5 0.0 copy-done.5
  68.5 0.3 fusion.6.vecs
  68.8 1.3 collective-permute-done.4.west
  70.1 1.5 collective-permute-done.5.east
  71.6 0.0 copy-done.1
  71.6 2.7 %forward.1 = (bf16[256,1024]{1,0:T(8,128)(2,1)S(1)}, f32[704,256]{1,0:T(8,128)S(1)}, bf16[320,1024]{1,0:T(8,128)(2,1)S(1)}, bf16[16,16,256]{2,1,0:T(8,128)(2,1)}, bf16[20,16,256]{2,1,0:T(8,128)(2,1)S(1)}) custom-call(f32[22,2688]{1,0:T(8,128)S(1)} %fusion.6.vecs, bf16[24,16,256]{2,1,0:T(8,128)(2,1)S(1)} %bitcast.64, ...), custom_call_target="tpu_custom_call" | custom-call | tf_op jit(solution)/shard_map/forward/pallas_call | solution.py:333
  74.3 1.9 collective-permute-start.6
  76.2 5.6 %collective-permute-start.7 = (bf16[20,16,256]{2,1,0:T(8,128)(2,1)S(1)}, bf16[20,16,256]{2,1,0:T(8,128)(2,1)S(1)}, u32[]{:S(2)}, u32[]{:S(2)}) collective-permute-start(bf16[20,16,256]{2,1,0:T(8,128)(2,1)S(1)} %get-tuple-element.18.own), channel_id=1, source_target_pairs={{0,248},{8,0},{16,8},{24,16},{32,24},{40,32},{48,40},{56,48},{64,5... | collective-permute-start | bytes 491528 | tf_op jit(solution)/shard_map/ppermute | solution.py:19
  81.9 0.3 convolution_convert_fusion
  82.3 1.4 collective-permute-done.6.west
  83.6 1.8 collective-permute-done.7.east
  85.4 3.1 %backward.1 = (bf16[256,256]{1,0:T(8,128)(2,1)S(1)}, bf16[16,16,256]{2,1,0:T(8,128)(2,1)}) custom-call(f32[22,2688]{1,0:T(8,128)S(1)} %fusion.6.vecs, bf16[20,16,256]{2,1,0:T(8,128)(2,1)S(1)} %get-tuple-element.18.own, bf16[20,16,256]{2,1,0:T(8,128)(2,1)S(1)} %collective-permute-done.6.west, bf16[20,16,256]{2,1,0:T(8,128)(2,1)S(1)} %collective-permute-done.7.east, ...), custom_call_target="tpu_custom_call" | custom-call | tf_op jit(solution)/shard_map/backward/pallas_call | solution.py:360
  88.4 1.2 fusion
  89.6 0.4 convolution_convert_fusion.1
  90.0 0.1 pad_maximum_fusion
  90.1 0.1 constant_dynamic-slice_fusion
  90.1 3.1 %collective-permute-start.8 = (bf16[2560,128]{1,0:T(8,128)(2,1)S(1)}, bf16[2560,128]{1,0:T(8,128)(2,1)S(1)}, u32[]{:S(2)}, u32[]{:S(2)}) collective-permute-start(bf16[2560,128]{1,0:T(8,128)(2,1)S(1)} %constant_dynamic-slice_fusion), channel_id=1, source_target_pairs={{0,1},{1,0},{2,3},{3,2},{4,5},{5,4},{6,7},{7,6},{8,9},{9,8},{10,11... | collective-permute-start | bytes 1966088 | tf_op jit(solution)/shard_map/ppermute | solution.py:19
  93.3 1.7 collective-permute-done.8
  95.0 0.2 add_convert_fusion
  95.1 18.4 %all_to_all.25 = bf16[4,640,128]{2,1,0:T(8,128)(2,1)S(1)} all-to-all(bf16[4,640,128]{2,1,0:T(8,128)(2,1)S(1)} %bitcast.66), channel_id=1, replica_groups=mesh['ens'=2,'lon'=32,'lat'=4,'ch'=2] {'lat'}, dimensions={0} | all-to-all | bytes 1310720 | tf_op jit(solution)/shard_map/all_to_all | solution.py:42
  113.5 0.1 reduce_sum.36
  113.7 14.5 %all_to_all.26 = bf16[8,80,128]{2,1,0:T(8,128)(2,1)S(1)} all-to-all(bf16[8,80,128]{2,1,0:T(8,128)(2,1)S(1)} %bitcast.69), channel_id=1, replica_groups={{0,8,16,24,32,40,48,56},{64,72,80,88,96,104,112,120},{128,136,144,152,1..., dimensions={0} | all-to-all | bytes 327680 | tf_op jit(solution)/shard_map/all_to_all | solution.py:42
  128.2 35.9 %all_to_all.27 = bf16[4,80,128]{2,1,0:T(8,128)(2,1)S(1)} all-to-all(bf16[4,80,128]{2,1,0:T(8,128)(2,1)S(1)} %broadcast_in_dim.20), channel_id=1, replica_groups={{0,64,128,192},{8,72,136,200},{16,80,144,208},{24,88,152,216},{32,96,16..., dimensions={0} | all-to-all | bytes 163840 | tf_op jit(solution)/shard_map/all_to_all | solution.py:42
  164.1 17.1 %all_to_all.28 = bf16[8,80,128]{2,1,0:T(8,128)(2,1)S(1)} all-to-all(bf16[8,80,128]{2,1,0:T(8,128)(2,1)S(1)} %broadcast_in_dim.36), channel_id=1, replica_groups={{0,8,16,24,32,40,48,56},{64,72,80,88,96,104,112,120},{128,136,144,152,1..., dimensions={0} | all-to-all | bytes 327680 | tf_op jit(solution)/shard_map/all_to_all | solution.py:42
  181.3 0.1 broadcast_in_dim.38
  181.4 11.2 %all_to_all.29 = bf16[4,640,128]{2,1,0:T(8,128)(2,1)S(1)} all-to-all(bf16[4,640,128]{2,1,0:T(8,128)(2,1)S(1)} %broadcast_in_dim.38), channel_id=1, replica_groups=mesh['ens'=2,'lon'=32,'lat'=4,'ch'=2] {'lat'}, dimensions={0} | all-to-all | bytes 1310720 | tf_op jit(solution)/shard_map/all_to_all | solution.py:42
  192.6 0.1 bitcast_convert_fusion
  192.7 1.0 slice_multiply_fusion
  193.8 0.7 slice_multiply_fusion.1
  (23 shorter events, 0.3 us)
Async XLA Ops:
  0.6 60.2 %copy-start = (bf16[512,256]{1,0:T(8,128)(2,1)S(1)}, bf16[512,256]{1,0:T(8,128)(2,1)}, u32[]{:S(2)}) copy-start(bf16[512,256]{1,0:T(8,128)(2,1)} %param.13) | copy-start | bytes 786436
  0.6 52.0 %copy-start.2 = (bf16[16,16,256]{2,1,0:T(8,128)(2,1)S(1)}, bf16[16,16,256]{2,1,0:T(8,128)(2,1)}, u32[]{:S(2)}) copy-start(bf16[16,16,256]{2,1,0:T(8,128)(2,1)} %cot.1) | copy-start | bytes 393220
  0.7 52.0 %copy-start.3 = (bf16[32,32,128]{2,1,0:T(8,128)(2,1)S(1)}, bf16[32,32,128]{2,1,0:T(8,128)(2,1)}, u32[]{:S(2)}) copy-start(bf16[32,32,128]{2,1,0:T(8,128)(2,1)} %field.1) | copy-start | bytes 786436
  2.5 50.0 %collective-permute-start = (bf16[160,256]{1,0:T(8,128)(2,1)S(1)}, bf16[160,256]{1,0:T(8,128)(2,1)S(1)}, u32[]{:S(2)}, u32[]{:S(2)}) collective-permute-start(bf16[160,256]{1,0:T(8,128)(2,1)S(1)} %pad_maximum_fusion.1), channel_id=1, source_target_pairs={{0,8},{8,16},{16,24},{24,32},{32,40},{40,48},{48,56},{56,64},{64,7... | collective-permute-start | bytes 245768 | tf_op jit(solution)/shard_map/ppermute | solution.py:19
  7.3 45.3 %collective-permute-start.1 = (bf16[160,256]{1,0:T(8,128)(2,1)S(1)}, bf16[160,256]{1,0:T(8,128)(2,1)S(1)}, u32[]{:S(2)}, u32[]{:S(2)}) collective-permute-start(bf16[160,256]{1,0:T(8,128)(2,1)S(1)} %pad_maximum_fusion.2), channel_id=1, source_target_pairs={{0,248},{8,0},{16,8},{24,16},{32,24},{40,32},{48,40},{56,48},{64,5... | collective-permute-start | bytes 245768 | tf_op jit(solution)/shard_map/ppermute | solution.py:19
  52.6 0.7 copy-start.4
  54.3 2.9 %collective-permute-start.2 = (bf16[120,512]{1,0:T(8,128)(2,1)S(1)}, bf16[120,512]{1,0:T(8,128)(2,1)S(1)}, u32[]{:S(2)}, u32[]{:S(2)}) collective-permute-start(bf16[120,512]{1,0:T(8,128)(2,1)S(1)} %get-tuple-element.14), channel_id=1, source_target_pairs={{0,1},{1,2},{2,3},{3,4},{4,5},{5,6},{6,7},{8,9},{9,10},{10,11},{11... | collective-permute-start | bytes 368648 | tf_op jit(solution)/shard_map/ppermute | solution.py:25
  55.9 4.9 %collective-permute-start.3 = (bf16[120,512]{1,0:T(8,128)(2,1)S(1)}, bf16[120,512]{1,0:T(8,128)(2,1)S(1)}, u32[]{:S(2)}, u32[]{:S(2)}) collective-permute-start(bf16[120,512]{1,0:T(8,128)(2,1)S(1)} %get-tuple-element.15), channel_id=1, source_target_pairs={{1,0},{2,1},{3,2},{4,3},{5,4},{6,5},{7,6},{9,8},{10,9},{11,10},{12... | collective-permute-start | bytes 368648 | tf_op jit(solution)/shard_map/ppermute | solution.py:25
  60.8 7.7 %copy-start.5 = (bf16[204,2688]{1,0:T(8,128)(2,1)S(1)}, bf16[204,2688]{1,0:T(8,128)(2,1)}, u32[]{:S(2)}) copy-start(bf16[204,2688]{1,0:T(8,128)(2,1)} %constant.42.clone) | copy-start | bytes 3290116
  60.9 10.7 %copy-start.1 = (bf16[2,1024,256]{2,1,0:T(8,128)(2,1)S(1)}, bf16[2,1024,256]{2,1,0:T(8,128)(2,1)}, u32[]{:S(2)}) copy-start(bf16[2,1024,256]{2,1,0:T(8,128)(2,1)} %weights.3) | copy-start | bytes 3145732
  61.2 8.9 %collective-permute-start.4 = (bf16[24,16,256]{2,1,0:T(8,128)(2,1)S(1)}, bf16[24,16,256]{2,1,0:T(8,128)(2,1)S(1)}, u32[]{:S(2)}, u32[]{:S(2)}) collective-permute-start(bf16[24,16,256]{2,1,0:T(8,128)(2,1)S(1)} %bitcast.62), channel_id=1, source_target_pairs={{0,8},{8,16},{16,24},{24,32},{32,40},{40,48},{48,56},{56,64},{64,7... | collective-permute-start | bytes 589832 | tf_op jit(solution)/shard_map/ppermute | solution.py:19
  63.2 8.3 %collective-permute-start.5 = (bf16[24,16,256]{2,1,0:T(8,128)(2,1)S(1)}, bf16[24,16,256]{2,1,0:T(8,128)(2,1)S(1)}, u32[]{:S(2)}, u32[]{:S(2)}) collective-permute-start(bf16[24,16,256]{2,1,0:T(8,128)(2,1)S(1)} %bitcast.63), channel_id=1, source_target_pairs={{0,248},{8,0},{16,8},{24,16},{32,24},{40,32},{48,40},{56,48},{64,5... | collective-permute-start | bytes 589832 | tf_op jit(solution)/shard_map/ppermute | solution.py:19
  74.3 9.3 %collective-permute-start.6 = (bf16[20,16,256]{2,1,0:T(8,128)(2,1)S(1)}, bf16[20,16,256]{2,1,0:T(8,128)(2,1)S(1)}, u32[]{:S(2)}, u32[]{:S(2)}) collective-permute-start(bf16[20,16,256]{2,1,0:T(8,128)(2,1)S(1)} %get-tuple-element.18.own), channel_id=1, source_target_pairs={{0,8},{8,16},{16,24},{24,32},{32,40},{40,48},{48,56},{56,64},{64,7... | collective-permute-start | bytes 491528 | tf_op jit(solution)/shard_map/ppermute | solution.py:19
  76.2 9.1 %collective-permute-start.7 = (bf16[20,16,256]{2,1,0:T(8,128)(2,1)S(1)}, bf16[20,16,256]{2,1,0:T(8,128)(2,1)S(1)}, u32[]{:S(2)}, u32[]{:S(2)}) collective-permute-start(bf16[20,16,256]{2,1,0:T(8,128)(2,1)S(1)} %get-tuple-element.18.own), channel_id=1, source_target_pairs={{0,248},{8,0},{16,8},{24,16},{32,24},{40,32},{48,40},{56,48},{64,5... | collective-permute-start | bytes 491528 | tf_op jit(solution)/shard_map/ppermute | solution.py:19
  90.1 4.8 %collective-permute-start.8 = (bf16[2560,128]{1,0:T(8,128)(2,1)S(1)}, bf16[2560,128]{1,0:T(8,128)(2,1)S(1)}, u32[]{:S(2)}, u32[]{:S(2)}) collective-permute-start(bf16[2560,128]{1,0:T(8,128)(2,1)S(1)} %constant_dynamic-slice_fusion), channel_id=1, source_target_pairs={{0,1},{1,0},{2,3},{3,2},{4,5},{5,4},{6,7},{7,6},{8,9},{9,8},{10,11... | collective-permute-start | bytes 1966088 | tf_op jit(solution)/shard_map/ppermute | solution.py:19

commit v4 on v3

--- a/solution.py
+++ b/solution.py
@@ -25,10 +25,10 @@
     return lax.ppermute(value, axis, pairs)
 
 
-def near_and_far(count, near):
-    near_groups = [[first + step for step in range(near)] for first in range(0, count, near)]
-    far_groups = [[first + near * step for step in range(count // near)] for first in range(near)]
-    return near_groups, far_groups
+def ring_groups(count, near):
+    places = [(place - near // 2) % count for place in range(count)]
+    runs = [places[first : first + near] for first in range(0, count, near)]
+    return runs
 
 
 def radix_of(count):
@@ -48,6 +48,35 @@
 
 def copies_to(value, peers, axis, groups=None):
     return exchanged(jnp.broadcast_to(value[None], (peers, *value.shape)), axis, groups)
+
+
+def sum_of_runs(value, axis, runs):
+    if len(runs) != 4:
+        peers = [list(group) for group in zip(*runs)]
+        return summed(copies_to(value, len(runs), axis, peers))
+    near = len(runs[0])
+    count = len(runs) * near
+    run = ((lax.axis_index(axis) + near // 2) % count) // near
+
+    def sent(block, moves):
+        pairs = [pair for source, target in moves for pair in zip(runs[source], runs[target])]
+        return lax.ppermute(block, axis, pairs).astype(jnp.float32)
+
+    own = value.astype(jnp.float32)
+    middle = (run == 1) | (run == 2)
+    by_middle = sent(value, [(1, 2), (2, 1)])
+    pair = own + by_middle
+    by_side = sent(jnp.where(middle, pair, own), [(0, 1), (1, 0), (2, 3), (3, 2)])
+    by_seam = sent(value, [(0, 3), (3, 0)])
+    by_far = sent(value, [(0, 2), (3, 1)])
+    one_and_two = jnp.where(middle, pair, by_side)
+    three = jnp.where(
+        run == 3, own, jnp.where(run == 0, by_seam, jnp.where(run == 1, by_far, by_side))
+    )
+    zero = jnp.where(
+        run == 0, own, jnp.where(run == 1, by_side, jnp.where(run == 2, by_far, by_seam))
+    )
+    return (one_and_two + three + zero).astype(jnp.bfloat16)
 
 
 def sum_over_cells(value):
@@ -60,12 +89,11 @@
     taken = ring_permute(given, "ch", 1)
     own = (kept.astype(jnp.float32) + taken.astype(jnp.float32)).astype(jnp.bfloat16)
     near = radix_of(lons)
-    far = lons // near
-    near_groups, far_groups = near_and_far(lons, near)
+    runs = ring_groups(lons, near)
     own = summed(exchanged(own.reshape(lats, rows // lats, half), "lat"))
-    own = summed(exchanged(own.reshape(near, -1, half), "lon", near_groups))
-    own = summed(copies_to(own, far, "lon", far_groups))
-    own = copies_to(own, near, "lon", near_groups).reshape(-1, half)
+    own = summed(exchanged(own.reshape(near, -1, half), "lon", runs))
+    own = sum_of_runs(own, "lon", runs)
+    own = copies_to(own, near, "lon", runs).reshape(-1, half)
     return copies_to(own, lats, "lat").reshape(rows, half).astype(jnp.float32)
 
 

time: 195 us -> 188 us (0.964)
  blocking collectives: 97.1 us -> 60.7 us
  starting transfers between devices: 68.1 us -> 95.3 us
    all_to_all x5 -> x4, blocking collectives: 97.1 us -> 60.7 us  [exchanged(): lax.all_to_all(tiles, axis, 0, 0, tiled=True, axis_index_groups=groups)]
    ppermute x0 -> x4, starting transfers between devices: none -> 27.2 us  [sent(): return lax.ppermute(block, axis, pairs).astype(jnp.float32)]
  transfers between devices with their start and end apart: 9 -> 13, of which waited for: 6 -> 8; matrix products, arithmetic and copies ran while one was open for 2% -> 2% of each run, Pallas kernels for 0% -> 0%
where the time goes in v4:
time: 188 us; the launch traced here: 187 us
  starting transfers between devices  95.3 us (51%)
  blocking collectives  60.7 us (32%)
  waiting for transfers between devices  12.9 us (7%)
  Pallas kernels  6.83 us (4%)
  other arithmetic  4 us (2%)
  matrix products  3.31 us (2%)
  local copies, waits for them, and re-layouts  2.95 us (2%)
    ppermute x7, starting transfers between devices, ring_permute(): lax.ppermute(value, axis, [(i, (i + steps) % count) for i in range(count)])  65.2 us
    all_to_all x4, blocking collectives, exchanged(): lax.all_to_all(tiles, axis, 0, 0, tiled=True, axis_index_groups=groups)  60.7 us
    ppermute x4, starting transfers between devices, sent(): return lax.ppermute(block, axis, pairs).astype(jnp.float32)  27.2 us
    ppermute x7, waiting for transfers between devices, ring_permute(): lax.ppermute(value, axis, [(i, (i + steps) % count) for i in range(count)])  7.62 us
  transfers between devices with their start and end apart: 13, of which 8 were waited for; matrix products, arithmetic and copies ran while one was open for 2% of the time, Pallas kernels for 0%

profile of v4, /device:TPU:40, one launch (start us, length us, event | category | flops | bytes accessed | tf_op | source)
XLA Modules:
  0.0 187.0 jit_solution(3159084744135464920)
XLA Ops:
  0.6 0.0 copy-start
  0.6 0.0 copy-start.2
  0.7 0.0 copy-start.3
  0.7 0.9 slice_bitcast_fusion.2
  1.6 0.9 fusion.14
  2.5 4.7 %collective-permute-start = (bf16[160,256]{1,0:T(8,128)(2,1)S(1)}, bf16[160,256]{1,0:T(8,128)(2,1)S(1)}, u32[]{:S(2)}, u32[]{:S(2)}) collective-permute-start(bf16[160,256]{1,0:T(8,128)(2,1)S(1)} %pad_maximum_fusion.1), channel_id=1, source_target_pairs={{0,8},{8,16},{16,24},{24,32},{32,40},{40,48},{48,56},{56,64},{64,7... | collective-permute-start | bytes 245768 | tf_op jit(solution)/shard_map/ppermute | solution.py:19
  7.3 42.6 %collective-permute-start.1 = (bf16[160,256]{1,0:T(8,128)(2,1)S(1)}, bf16[160,256]{1,0:T(8,128)(2,1)S(1)}, u32[]{:S(2)}, u32[]{:S(2)}) collective-permute-start(bf16[160,256]{1,0:T(8,128)(2,1)S(1)} %pad_maximum_fusion.2), channel_id=1, source_target_pairs={{0,248},{8,0},{16,8},{24,16},{32,24},{40,32},{48,40},{56,48},{64,5... | collective-permute-start | bytes 245768 | tf_op jit(solution)/shard_map/ppermute | solution.py:19
  49.9 0.7 broadcast_compare_fusion
  50.6 0.8 broadcast_select_fusion
  51.5 0.9 fusion.11
  52.4 0.1 reshape.95.masked
  52.6 0.0 collective-permute-done.west
  52.6 0.0 collective-permute-done.1.east
  52.6 0.0 copy-done.2
  52.6 0.0 copy-done.3
  52.6 0.0 copy-start.4
  52.6 0.6 copy-done.4
  53.3 1.1 encoder.1
  54.3 1.6 collective-permute-start.2
  55.9 1.3 collective-permute-start.3
  57.3 0.0 collective-permute-done.2
  57.3 3.5 %collective-permute-done.3 = bf16[120,512]{1,0:T(8,128)(2,1)S(1)} collective-permute-done((bf16[120,512]{1,0:T(8,128)(2,1)S(1)}, bf16[120,512]{1,0:T(8,128)(2,1)S(1)}, u32[]{:S(2)}, u32[]{:S(2)}) %collective-permute-start.3) | collective-permute-done | bytes 122912 | tf_op jit(solution)/shard_map/ppermute | solution.py:25
  60.8 0.1 add_convert_fusion.1
  60.9 0.0 copy-done
  60.9 0.0 copy-start.1
  60.9 0.3 convolution_convert_fusion.2
  61.2 2.1 %collective-permute-start.4 = (bf16[24,16,256]{2,1,0:T(8,128)(2,1)S(1)}, bf16[24,16,256]{2,1,0:T(8,128)(2,1)S(1)}, u32[]{:S(2)}, u32[]{:S(2)}) collective-permute-start(bf16[24,16,256]{2,1,0:T(8,128)(2,1)S(1)} %bitcast.62), channel_id=1, source_target_pairs={{0,8},{8,16},{16,24},{24,32},{32,40},{40,48},{48,56},{56,64},{64,7... | collective-permute-start | bytes 589832 | tf_op jit(solution)/shard_map/ppermute | solution.py:19
  63.3 5.2 %collective-permute-start.5 = (bf16[24,16,256]{2,1,0:T(8,128)(2,1)S(1)}, bf16[24,16,256]{2,1,0:T(8,128)(2,1)S(1)}, u32[]{:S(2)}, u32[]{:S(2)}) collective-permute-start(bf16[24,16,256]{2,1,0:T(8,128)(2,1)S(1)} %bitcast.63), channel_id=1, source_target_pairs={{0,248},{8,0},{16,8},{24,16},{32,24},{40,32},{48,40},{56,48},{64,5... | collective-permute-start | bytes 589832 | tf_op jit(solution)/shard_map/ppermute | solution.py:19
  68.5 0.0 copy-done.5
  68.5 0.3 fusion.10.vecs
  68.8 1.3 collective-permute-done.4.west
  70.1 1.5 collective-permute-done.5.east
  71.6 0.0 copy-done.1
  71.6 2.7 %forward.1 = (bf16[256,1024]{1,0:T(8,128)(2,1)S(1)}, f32[704,256]{1,0:T(8,128)S(1)}, bf16[320,1024]{1,0:T(8,128)(2,1)S(1)}, bf16[16,16,256]{2,1,0:T(8,128)(2,1)}, bf16[20,16,256]{2,1,0:T(8,128)(2,1)S(1)}) custom-call(f32[22,2688]{1,0:T(8,128)S(1)} %fusion.10.vecs, bf16[24,16,256]{2,1,0:T(8,128)(2,1)S(1)} %bitcast.64, ...), custom_call_target="tpu_custom_call" | custom-call | tf_op jit(solution)/shard_map/forward/pallas_call | solution.py:361
  74.3 1.9 %collective-permute-start.6 = (bf16[20,16,256]{2,1,0:T(8,128)(2,1)S(1)}, bf16[20,16,256]{2,1,0:T(8,128)(2,1)S(1)}, u32[]{:S(2)}, u32[]{:S(2)}) collective-permute-start(bf16[20,16,256]{2,1,0:T(8,128)(2,1)S(1)} %get-tuple-element.18.own), channel_id=1, source_target_pairs={{0,8},{8,16},{16,24},{24,32},{32,40},{40,48},{48,56},{56,64},{64,7... | collective-permute-start | bytes 491528 | tf_op jit(solution)/shard_map/ppermute | solution.py:19
  76.2 5.6 %collective-permute-start.7 = (bf16[20,16,256]{2,1,0:T(8,128)(2,1)S(1)}, bf16[20,16,256]{2,1,0:T(8,128)(2,1)S(1)}, u32[]{:S(2)}, u32[]{:S(2)}) collective-permute-start(bf16[20,16,256]{2,1,0:T(8,128)(2,1)S(1)} %get-tuple-element.18.own), channel_id=1, source_target_pairs={{0,248},{8,0},{16,8},{24,16},{32,24},{40,32},{48,40},{56,48},{64,5... | collective-permute-start | bytes 491528 | tf_op jit(solution)/shard_map/ppermute | solution.py:19
  81.9 0.4 convolution_convert_fusion
  82.3 1.3 collective-permute-done.6.west
  83.6 1.8 collective-permute-done.7.east
  85.4 3.1 %backward.1 = (bf16[256,256]{1,0:T(8,128)(2,1)S(1)}, bf16[16,16,256]{2,1,0:T(8,128)(2,1)}) custom-call(f32[22,2688]{1,0:T(8,128)S(1)} %fusion.10.vecs, bf16[20,16,256]{2,1,0:T(8,128)(2,1)S(1)} %get-tuple-element.18.own, bf16[20,16,256]{2,1,0:T(8,128)(2,1)S(1)} %collective-permute-done.6.west, bf16[20,16,256]{2,1,0:T(8,128)(2,1)S(1)} %collective-permute-done.7.east, ...), custom_call_target="tpu_custom_call" | custom-call | tf_op jit(solution)/shard_map/backward/pallas_call | solution.py:388
  88.4 1.2 fusion
  89.6 0.4 convolution_convert_fusion.1
  90.0 0.1 pad_maximum_fusion
  90.1 0.1 constant_dynamic-slice_fusion
  90.1 3.1 %collective-permute-start.8 = (bf16[2560,128]{1,0:T(8,128)(2,1)S(1)}, bf16[2560,128]{1,0:T(8,128)(2,1)S(1)}, u32[]{:S(2)}, u32[]{:S(2)}) collective-permute-start(bf16[2560,128]{1,0:T(8,128)(2,1)S(1)} %constant_dynamic-slice_fusion), channel_id=1, source_target_pairs={{0,1},{1,0},{2,3},{3,2},{4,5},{5,4},{6,7},{7,6},{8,9},{9,8},{10,11... | collective-permute-start | bytes 1966088 | tf_op jit(solution)/shard_map/ppermute | solution.py:19
  93.3 1.7 collective-permute-done.8
  95.0 0.2 add_convert_fusion
  95.2 18.4 %all_to_all.20 = bf16[4,640,128]{2,1,0:T(8,128)(2,1)S(1)} all-to-all(bf16[4,640,128]{2,1,0:T(8,128)(2,1)S(1)} %bitcast.66), channel_id=1, replica_groups=mesh['ens'=2,'lon'=32,'lat'=4,'ch'=2] {'lat'}, dimensions={0} | all-to-all | bytes 1310720 | tf_op jit(solution)/shard_map/all_to_all | solution.py:42
  113.5 0.1 reduce_sum.24
  113.7 14.4 %all_to_all.21 = bf16[8,80,128]{2,1,0:T(8,128)(2,1)S(1)} all-to-all(bf16[8,80,128]{2,1,0:T(8,128)(2,1)S(1)} %bitcast.69), channel_id=1, replica_groups={{224,232,240,248,0,8,16,24},{32,40,48,56,64,72,80,88},{96,104,112,120,1..., dimensions={0} | all-to-all | bytes 327680 | tf_op jit(solution)/shard_map/all_to_all | solution.py:42
  128.1 0.7 collective-permute-start.9
  128.8 0.0 collective-permute-done.9
  128.8 12.1 %collective-permute-start.10 = (f32[80,128]{1,0:T(8,128)S(1)}, f32[80,128]{1,0:T(8,128)S(1)}, u32[]{:S(2)}, u32[]{:S(2)}) collective-permute-start(f32[80,128]{1,0:T(8,128)S(1)} %convert_select_fusion.2), channel_id=1, source_target_pairs={{224,32},{232,40},{240,48},{248,56},{0,64},{8,72},{16,80},{24,88},... | collective-permute-start | bytes 122888 | tf_op jit(solution)/shard_map/ppermute | solution.py:63
  140.9 13.1 %collective-permute-start.11 = (bf16[80,128]{1,0:T(8,128)(2,1)S(1)}, bf16[80,128]{1,0:T(8,128)(2,1)S(1)}, u32[]{:S(2)}, u32[]{:S(2)}) collective-permute-start(bf16[80,128]{1,0:T(8,128)(2,1)S(1)} %reduce_sum.25), channel_id=1, source_target_pairs={{224,160},{232,168},{240,176},{248,184},{0,192},{8,200},{16,208},{... | collective-permute-start | bytes 61448 | tf_op jit(solution)/shard_map/ppermute | solution.py:63
  154.0 1.3 collective-permute-start.12
  155.3 0.7 collective-permute-done.11
  156.0 1.0 collective-permute-done.12
  157.0 0.0 collective-permute-done.10
  157.1 16.7 %all_to_all.22 = bf16[8,80,128]{2,1,0:T(8,128)(2,1)S(1)} all-to-all(bf16[8,80,128]{2,1,0:T(8,128)(2,1)S(1)} %broadcast_in_dim.29), channel_id=1, replica_groups={{224,232,240,248,0,8,16,24},{32,40,48,56,64,72,80,88},{96,104,112,120,1..., dimensions={0} | all-to-all | bytes 327680 | tf_op jit(solution)/shard_map/all_to_all | solution.py:42
  173.8 0.1 broadcast_in_dim.31
  173.9 11.2 %all_to_all.23 = bf16[4,640,128]{2,1,0:T(8,128)(2,1)S(1)} all-to-all(bf16[4,640,128]{2,1,0:T(8,128)(2,1)S(1)} %broadcast_in_dim.31), channel_id=1, replica_groups=mesh['ens'=2,'lon'=32,'lat'=4,'ch'=2] {'lat'}, dimensions={0} | all-to-all | bytes 1310720 | tf_op jit(solution)/shard_map/all_to_all | solution.py:42
  185.1 0.1 bitcast_convert_fusion
  185.3 1.0 slice_multiply_fusion
  186.3 0.7 slice_multiply_fusion.1
  (24 shorter events, 0.3 us)
Async XLA Ops:
  0.6 60.2 %copy-start = (bf16[512,256]{1,0:T(8,128)(2,1)S(1)}, bf16[512,256]{1,0:T(8,128)(2,1)}, u32[]{:S(2)}) copy-start(bf16[512,256]{1,0:T(8,128)(2,1)} %param.13) | copy-start | bytes 786436
  0.6 52.0 %copy-start.2 = (bf16[16,16,256]{2,1,0:T(8,128)(2,1)S(1)}, bf16[16,16,256]{2,1,0:T(8,128)(2,1)}, u32[]{:S(2)}) copy-start(bf16[16,16,256]{2,1,0:T(8,128)(2,1)} %cot.1) | copy-start | bytes 393220
  0.7 52.0 %copy-start.3 = (bf16[32,32,128]{2,1,0:T(8,128)(2,1)S(1)}, bf16[32,32,128]{2,1,0:T(8,128)(2,1)}, u32[]{:S(2)}) copy-start(bf16[32,32,128]{2,1,0:T(8,128)(2,1)} %field.1) | copy-start | bytes 786436
  2.5 50.0 %collective-permute-start = (bf16[160,256]{1,0:T(8,128)(2,1)S(1)}, bf16[160,256]{1,0:T(8,128)(2,1)S(1)}, u32[]{:S(2)}, u32[]{:S(2)}) collective-permute-start(bf16[160,256]{1,0:T(8,128)(2,1)S(1)} %pad_maximum_fusion.1), channel_id=1, source_target_pairs={{0,8},{8,16},{16,24},{24,32},{32,40},{40,48},{48,56},{56,64},{64,7... | collective-permute-start | bytes 245768 | tf_op jit(solution)/shard_map/ppermute | solution.py:19
  7.3 45.3 %collective-permute-start.1 = (bf16[160,256]{1,0:T(8,128)(2,1)S(1)}, bf16[160,256]{1,0:T(8,128)(2,1)S(1)}, u32[]{:S(2)}, u32[]{:S(2)}) collective-permute-start(bf16[160,256]{1,0:T(8,128)(2,1)S(1)} %pad_maximum_fusion.2), channel_id=1, source_target_pairs={{0,248},{8,0},{16,8},{24,16},{32,24},{40,32},{48,40},{56,48},{64,5... | collective-permute-start | bytes 245768 | tf_op jit(solution)/shard_map/ppermute | solution.py:19
  52.6 0.7 copy-start.4
  54.3 2.9 %collective-permute-start.2 = (bf16[120,512]{1,0:T(8,128)(2,1)S(1)}, bf16[120,512]{1,0:T(8,128)(2,1)S(1)}, u32[]{:S(2)}, u32[]{:S(2)}) collective-permute-start(bf16[120,512]{1,0:T(8,128)(2,1)S(1)} %get-tuple-element.14), channel_id=1, source_target_pairs={{0,1},{1,2},{2,3},{3,4},{4,5},{5,6},{6,7},{8,9},{9,10},{10,11},{11... | collective-permute-start | bytes 368648 | tf_op jit(solution)/shard_map/ppermute | solution.py:25
  55.9 4.9 %collective-permute-start.3 = (bf16[120,512]{1,0:T(8,128)(2,1)S(1)}, bf16[120,512]{1,0:T(8,128)(2,1)S(1)}, u32[]{:S(2)}, u32[]{:S(2)}) collective-permute-start(bf16[120,512]{1,0:T(8,128)(2,1)S(1)} %get-tuple-element.15), channel_id=1, source_target_pairs={{1,0},{2,1},{3,2},{4,3},{5,4},{6,5},{7,6},{9,8},{10,9},{11,10},{12... | collective-permute-start | bytes 368648 | tf_op jit(solution)/shard_map/ppermute | solution.py:25
  60.8 7.7 %copy-start.5 = (bf16[204,2688]{1,0:T(8,128)(2,1)S(1)}, bf16[204,2688]{1,0:T(8,128)(2,1)}, u32[]{:S(2)}) copy-start(bf16[204,2688]{1,0:T(8,128)(2,1)} %constant.74.clone) | copy-start | bytes 3290116
  60.9 10.7 %copy-start.1 = (bf16[2,1024,256]{2,1,0:T(8,128)(2,1)S(1)}, bf16[2,1024,256]{2,1,0:T(8,128)(2,1)}, u32[]{:S(2)}) copy-start(bf16[2,1024,256]{2,1,0:T(8,128)(2,1)} %weights.3) | copy-start | bytes 3145732
  61.2 8.9 %collective-permute-start.4 = (bf16[24,16,256]{2,1,0:T(8,128)(2,1)S(1)}, bf16[24,16,256]{2,1,0:T(8,128)(2,1)S(1)}, u32[]{:S(2)}, u32[]{:S(2)}) collective-permute-start(bf16[24,16,256]{2,1,0:T(8,128)(2,1)S(1)} %bitcast.62), channel_id=1, source_target_pairs={{0,8},{8,16},{16,24},{24,32},{32,40},{40,48},{48,56},{56,64},{64,7... | collective-permute-start | bytes 589832 | tf_op jit(solution)/shard_map/ppermute | solution.py:19
  63.3 8.3 %collective-permute-start.5 = (bf16[24,16,256]{2,1,0:T(8,128)(2,1)S(1)}, bf16[24,16,256]{2,1,0:T(8,128)(2,1)S(1)}, u32[]{:S(2)}, u32[]{:S(2)}) collective-permute-start(bf16[24,16,256]{2,1,0:T(8,128)(2,1)S(1)} %bitcast.63), channel_id=1, source_target_pairs={{0,248},{8,0},{16,8},{24,16},{32,24},{40,32},{48,40},{56,48},{64,5... | collective-permute-start | bytes 589832 | tf_op jit(solution)/shard_map/ppermute | solution.py:19
  74.3 9.3 %collective-permute-start.6 = (bf16[20,16,256]{2,1,0:T(8,128)(2,1)S(1)}, bf16[20,16,256]{2,1,0:T(8,128)(2,1)S(1)}, u32[]{:S(2)}, u32[]{:S(2)}) collective-permute-start(bf16[20,16,256]{2,1,0:T(8,128)(2,1)S(1)} %get-tuple-element.18.own), channel_id=1, source_target_pairs={{0,8},{8,16},{16,24},{24,32},{32,40},{40,48},{48,56},{56,64},{64,7... | collective-permute-start | bytes 491528 | tf_op jit(solution)/shard_map/ppermute | solution.py:19
  76.2 9.1 %collective-permute-start.7 = (bf16[20,16,256]{2,1,0:T(8,128)(2,1)S(1)}, bf16[20,16,256]{2,1,0:T(8,128)(2,1)S(1)}, u32[]{:S(2)}, u32[]{:S(2)}) collective-permute-start(bf16[20,16,256]{2,1,0:T(8,128)(2,1)S(1)} %get-tuple-element.18.own), channel_id=1, source_target_pairs={{0,248},{8,0},{16,8},{24,16},{32,24},{40,32},{48,40},{56,48},{64,5... | collective-permute-start | bytes 491528 | tf_op jit(solution)/shard_map/ppermute | solution.py:19
  90.1 4.8 %collective-permute-start.8 = (bf16[2560,128]{1,0:T(8,128)(2,1)S(1)}, bf16[2560,128]{1,0:T(8,128)(2,1)S(1)}, u32[]{:S(2)}, u32[]{:S(2)}) collective-permute-start(bf16[2560,128]{1,0:T(8,128)(2,1)S(1)} %constant_dynamic-slice_fusion), channel_id=1, source_target_pairs={{0,1},{1,0},{2,3},{3,2},{4,5},{5,4},{6,7},{7,6},{8,9},{9,8},{10,11... | collective-permute-start | bytes 1966088 | tf_op jit(solution)/shard_map/ppermute | solution.py:19
  128.1 0.7 collective-permute-start.9
  128.8 28.2 %collective-permute-start.10 = (f32[80,128]{1,0:T(8,128)S(1)}, f32[80,128]{1,0:T(8,128)S(1)}, u32[]{:S(2)}, u32[]{:S(2)}) collective-permute-start(f32[80,128]{1,0:T(8,128)S(1)} %convert_select_fusion.2), channel_id=1, source_target_pairs={{224,32},{232,40},{240,48},{248,56},{0,64},{8,72},{16,80},{24,88},... | collective-permute-start | bytes 122888 | tf_op jit(solution)/shard_map/ppermute | solution.py:63
  140.9 15.1 %collective-permute-start.11 = (bf16[80,128]{1,0:T(8,128)(2,1)S(1)}, bf16[80,128]{1,0:T(8,128)(2,1)S(1)}, u32[]{:S(2)}, u32[]{:S(2)}) collective-permute-start(bf16[80,128]{1,0:T(8,128)(2,1)S(1)} %reduce_sum.25), channel_id=1, source_target_pairs={{224,160},{232,168},{240,176},{248,184},{0,192},{8,200},{16,208},{... | collective-permute-start | bytes 61448 | tf_op jit(solution)/shard_map/ppermute | solution.py:63
  154.0 3.0 %collective-permute-start.12 = (bf16[80,128]{1,0:T(8,128)(2,1)S(1)}, bf16[80,128]{1,0:T(8,128)(2,1)S(1)}, u32[]{:S(2)}, u32[]{:S(2)}) collective-permute-start(bf16[80,128]{1,0:T(8,128)(2,1)S(1)} %reduce_sum.25), channel_id=1, source_target_pairs={{224,96},{232,104},{240,112},{248,120},{0,128},{8,136},{16,144},{2... | collective-permute-start | bytes 61448 | tf_op jit(solution)/shard_map/ppermute | solution.py:63

commit v5 on v3

--- a/solution.py
+++ b/solution.py
@@ -25,10 +25,10 @@
     return lax.ppermute(value, axis, pairs)
 
 
-def near_and_far(count, near):
-    near_groups = [[first + step for step in range(near)] for first in range(0, count, near)]
-    far_groups = [[first + near * step for step in range(count // near)] for first in range(near)]
-    return near_groups, far_groups
+def ring_groups(count, near):
+    places = [(place - near // 2) % count for place in range(count)]
+    runs = [places[first : first + near] for first in range(0, count, near)]
+    return runs
 
 
 def radix_of(count):
@@ -60,12 +60,11 @@
     taken = ring_permute(given, "ch", 1)
     own = (kept.astype(jnp.float32) + taken.astype(jnp.float32)).astype(jnp.bfloat16)
     near = radix_of(lons)
-    far = lons // near
-    near_groups, far_groups = near_and_far(lons, near)
+    runs = ring_groups(lons, near)
     own = summed(exchanged(own.reshape(lats, rows // lats, half), "lat"))
-    own = summed(exchanged(own.reshape(near, -1, half), "lon", near_groups))
-    own = summed(copies_to(own, far, "lon", far_groups))
-    own = copies_to(own, near, "lon", near_groups).reshape(-1, half)
+    own = summed(exchanged(own.reshape(near, -1, half), "lon", runs))
+    own = summed(copies_to(own, len(runs), "lon", [list(peers) for peers in zip(*runs)]))
+    own = copies_to(own, near, "lon", runs).reshape(-1, half)
     return copies_to(own, lats, "lat").reshape(rows, half).astype(jnp.float32)
 
 
@@ -181,7 +180,9 @@
         act1[i] = (upstream * sigma * (1.0 + pre * (1.0 - sigma))).astype(jnp.bfloat16)
 
 
-def backward_kernel(vecs, own, west, east, weights, pre0, cot, act0, grad0, a1, e1, g1, a0, e0):
+def backward_kernel(
+    vecs, own, west, east, weights, pre0, cot, act0, grad0, kept, a1, e1, g1, a0, e0
+):
     rows, cols, channels = grad0.shape
     basis_count = weights.shape[1] // channels
     mid = cols + 2 * REACH
@@ -241,11 +242,13 @@
             continue
         spread = parts[i][2 * cols :] + parts[i + 1][cols : 2 * cols] + parts[i + 2][:cols]
         before = g1[(i + 1) * mid + REACH : (i + 1) * mid + REACH + cols]
-        grad0[i] = (before + spread).astype(jnp.bfloat16)
+        total = (before + spread).astype(jnp.bfloat16)
+        grad0[i] = total
+        kept[i * cols : (i + 1) * cols] = total
 
 
 def encoder_kernel(
-    first, owner, taps, field, west, east, cot, masked, partial, down, up, acc
+    owner, taps, field, west, east, cot, masked, partial, down, up, acc
 ):
     rows_in, cols_in, width = field.shape
     rows, cols, channels = cot.shape
@@ -267,8 +270,7 @@
                 steps == 16 - TAP_REACH + t, west[p : p + 1, column].astype(jnp.float32), edges
             )
         out = dot(band, jnp.concatenate([field[p], edges.astype(jnp.bfloat16)], axis=0))
-        target = owner[p] - first[0]
-        acc[target] += out.astype(jnp.bfloat16).astype(jnp.float32)
+        acc[owner[p]] += out.astype(jnp.bfloat16).astype(jnp.float32)
     for i in range(rows + 2):
         for k in range(basis_count):
             part = acc[i, k * cols : (k + 1) * cols]
@@ -305,7 +307,7 @@
 GRANT = pltpu.CompilerParams(vmem_limit_bytes=26 * 2**20)
 
 
-def run_encoder(first, owner, taps, field, west, east, cot, masked):
+def run_encoder(owner, taps, field, west, east, cot, masked):
     rows, cols, channels = cot.shape
     basis_count, width = taps.shape[1], field.shape[2]
     message = jax.ShapeDtypeStruct((5 * cols + cols + 2 * REACH + 8, 2 * channels), jnp.bfloat16)
@@ -316,12 +318,12 @@
             message,
             message,
         ),
-        in_specs=[pl.BlockSpec(memory_space=pltpu.SMEM)] * 2 + in_vmem(6),
+        in_specs=[pl.BlockSpec(memory_space=pltpu.SMEM)] + in_vmem(6),
         out_specs=tuple(in_vmem(3)),
         scratch_shapes=[pltpu.VMEM((rows + 2, basis_count * cols, width), jnp.float32)],
         compiler_params=GRANT,
         name="encoder",
-    )(first, owner, taps, field, west, east, cot, masked)
+    )(owner, taps, field, west, east, cot, masked)
 
 
 def run_forward(vecs, own, west, east, weights, cot):
@@ -362,9 +364,10 @@
         out_shape=(
             jax.ShapeDtypeStruct((rows * cols, channels), bf16),
             jax.ShapeDtypeStruct((rows, cols, channels), bf16),
+            jax.ShapeDtypeStruct((rows * cols, channels), bf16),
         ),
         in_specs=in_vmem(7),
-        out_specs=tuple(in_vmem(2)),
+        out_specs=tuple(in_vmem(3)),
         scratch_shapes=[
             pltpu.VMEM(((rows + 4) * 3 * cols, channels), bf16),
             pltpu.VMEM(((rows + 4) * basis_count * 64, channels), bf16),
@@ -431,7 +434,7 @@
         "pkt,tl->pkl", encoder_filter, jnp.asarray(tap_lanes, bf16), preferred_element_type=f32
     )
     partial, down, up = run_encoder(
-        first_row.reshape(1), row_owner, taps, input_field, west_side, east_side, cotangent, masked
+        row_owner - first_row, taps, input_field, west_side, east_side, cotangent, masked
     )
     above = line_permute(down, BAND, 1)
     below = line_permute(up, BAND, -1)
@@ -475,7 +478,7 @@
         (((0,), (0,)), ((), ())),
         preferred_element_type=f32,
     )
-    act0, gradient = run_backward(
+    act0, gradient, gradient_rows = run_backward(
         vecs, act1, act_west, act_east, block_weights, pre0, cot_ext
     )
     weight0 = lax.dot_general(
@@ -483,7 +486,7 @@
     )
     encoder_term = lax.dot_general(
         latent[4 : rows_dev + 4].reshape(cell_count, latent_width),
-        gradient.reshape(cell_count, channels),
+        gradient_rows,
         (((0,), (0,)), ((), ())),
         preferred_element_type=f32,
     )

time: 195 us -> 188 us (0.964)
  blocking collectives: 97.1 us -> 88 us
  waiting for transfers between devices: 11.1 us -> 16.5 us
  starting transfers between devices: 68.1 us -> 65.2 us
    all_to_all x5, blocking collectives: 97.1 us -> 88 us  [exchanged(): lax.all_to_all(tiles, axis, 0, 0, tiled=True, axis_index_groups=groups)]
    ppermute x7, waiting for transfers between devices: 7.63 us -> 13 us  [ring_permute(): lax.ppermute(value, axis, [(i, (i + steps) % count) for i in range(count)])]
    ppermute x7, starting transfers between devices: 65.2 us -> 62.3 us  [ring_permute(): lax.ppermute(value, axis, [(i, (i + steps) % count) for i in range(count)])]
where the time goes in v5:
time: 188 us; the launch traced here: 187 us
  blocking collectives  88 us (47%)
  starting transfers between devices  65.2 us (35%)
  waiting for transfers between devices  16.5 us (9%)
  Pallas kernels  6.82 us (4%)
  other arithmetic  4.66 us (2%)
  matrix products  2.4 us (1%)
  local copies, waits for them, and re-layouts  2.33 us (1%)
    all_to_all x5, blocking collectives, exchanged(): lax.all_to_all(tiles, axis, 0, 0, tiled=True, axis_index_groups=groups)  88 us
    ppermute x7, starting transfers between devices, ring_permute(): lax.ppermute(value, axis, [(i, (i + steps) % count) for i in range(count)])  62.3 us
    ppermute x7, waiting for transfers between devices, ring_permute(): lax.ppermute(value, axis, [(i, (i + steps) % count) for i in range(count)])  13 us
  transfers between devices with their start and end apart: 9, of which 6 were waited for; matrix products, arithmetic and copies ran while one was open for 2% of the time, Pallas kernels for 0%

profile of v5, /device:TPU:40, one launch (start us, length us, event | category | flops | bytes accessed | tf_op | source)
XLA Modules:
  0.0 186.9 jit_solution(16787337123613630852)
XLA Ops:
  0.6 0.0 copy-start
  0.6 0.0 copy-start.3
  0.7 0.0 copy-start.2
  0.7 1.0 fusion.9
  1.6 0.9 slice_bitcast_fusion.2
  2.5 4.7 %collective-permute-start = (bf16[160,256]{1,0:T(8,128)(2,1)S(1)}, bf16[160,256]{1,0:T(8,128)(2,1)S(1)}, u32[]{:S(2)}, u32[]{:S(2)}) collective-permute-start(bf16[160,256]{1,0:T(8,128)(2,1)S(1)} %pad_maximum_fusion.1), channel_id=1, source_target_pairs={{0,8},{8,16},{16,24},{24,32},{32,40},{40,48},{48,56},{56,64},{64,7... | collective-permute-start | bytes 245768 | tf_op jit(solution)/shard_map/ppermute | solution.py:19
  7.3 42.6 %collective-permute-start.1 = (bf16[160,256]{1,0:T(8,128)(2,1)S(1)}, bf16[160,256]{1,0:T(8,128)(2,1)S(1)}, u32[]{:S(2)}, u32[]{:S(2)}) collective-permute-start(bf16[160,256]{1,0:T(8,128)(2,1)S(1)} %pad_maximum_fusion.2), channel_id=1, source_target_pairs={{0,248},{8,0},{16,8},{24,16},{32,24},{40,32},{48,40},{56,48},{64,5... | collective-permute-start | bytes 245768 | tf_op jit(solution)/shard_map/ppermute | solution.py:19
  49.9 0.7 broadcast_compare_fusion
  50.6 0.8 broadcast_select_fusion
  51.5 0.9 fusion.6
  52.4 0.7 broadcast_subtract_fusion.owner
  53.1 0.1 reshape.93.masked
  53.2 0.0 collective-permute-done.west
  53.3 0.0 collective-permute-done.1.east
  53.3 0.0 copy-done.3
  53.3 0.0 copy-done.2
  53.3 1.1 encoder.1
  54.3 1.6 collective-permute-start.2
  55.9 1.3 collective-permute-start.3
  57.3 0.0 collective-permute-done.2
  57.3 3.5 %collective-permute-done.3 = bf16[120,512]{1,0:T(8,128)(2,1)S(1)} collective-permute-done((bf16[120,512]{1,0:T(8,128)(2,1)S(1)}, bf16[120,512]{1,0:T(8,128)(2,1)S(1)}, u32[]{:S(2)}, u32[]{:S(2)}) %collective-permute-start.3) | collective-permute-done | bytes 122912 | tf_op jit(solution)/shard_map/ppermute | solution.py:25
  60.8 0.0 copy-start.4
  60.8 0.1 add_convert_fusion.1
  60.9 0.0 copy-done
  60.9 0.3 convolution_convert_fusion.3
  61.2 0.0 copy-start.1
  61.2 4.3 %collective-permute-start.5 = (bf16[24,16,256]{2,1,0:T(8,128)(2,1)S(1)}, bf16[24,16,256]{2,1,0:T(8,128)(2,1)S(1)}, u32[]{:S(2)}, u32[]{:S(2)}) collective-permute-start(bf16[24,16,256]{2,1,0:T(8,128)(2,1)S(1)} %bitcast.58), channel_id=1, source_target_pairs={{0,248},{8,0},{16,8},{24,16},{32,24},{40,32},{48,40},{56,48},{64,5... | collective-permute-start | bytes 589832 | tf_op jit(solution)/shard_map/ppermute | solution.py:19
  65.5 2.0 %collective-permute-start.4 = (bf16[24,16,256]{2,1,0:T(8,128)(2,1)S(1)}, bf16[24,16,256]{2,1,0:T(8,128)(2,1)S(1)}, u32[]{:S(2)}, u32[]{:S(2)}) collective-permute-start(bf16[24,16,256]{2,1,0:T(8,128)(2,1)S(1)} %bitcast.59), channel_id=1, source_target_pairs={{0,8},{8,16},{16,24},{24,32},{32,40},{40,48},{48,56},{56,64},{64,7... | collective-permute-start | bytes 589832 | tf_op jit(solution)/shard_map/ppermute | solution.py:19
  67.5 0.0 copy-done.4
  67.5 0.3 fusion.5.vecs
  67.8 1.1 collective-permute-done.5.east
  68.9 5.4 %collective-permute-done.4.west = bf16[24,16,256]{2,1,0:T(8,128)(2,1)S(1)} collective-permute-done((bf16[24,16,256]{2,1,0:T(8,128)(2,1)S(1)}, bf16[24,16,256]{2,1,0:T(8,128)(2,1)S(1)}, u32[]{:S(2)}, u32[]{:S(2)}) %collective-permute-start.4) | collective-permute-done | bytes 196640 | tf_op jit(solution)/shard_map/ppermute | solution.py:19
  74.3 0.0 copy-done.1
  74.3 2.7 %forward.1 = (bf16[256,1024]{1,0:T(8,128)(2,1)S(1)}, f32[704,256]{1,0:T(8,128)S(1)}, bf16[320,1024]{1,0:T(8,128)(2,1)S(1)}, bf16[16,16,256]{2,1,0:T(8,128)(2,1)}, bf16[20,16,256]{2,1,0:T(8,128)(2,1)S(1)}) custom-call(f32[22,2688]{1,0:T(8,128)S(1)} %fusion.5.vecs, bf16[24,16,256]{2,1,0:T(8,128)(2,1)S(1)} %bitcast.60, ...), custom_call_target="tpu_custom_call" | custom-call | tf_op jit(solution)/shard_map/forward/pallas_call | solution.py:335
  77.0 2.0 %collective-permute-start.7 = (bf16[20,16,256]{2,1,0:T(8,128)(2,1)S(1)}, bf16[20,16,256]{2,1,0:T(8,128)(2,1)S(1)}, u32[]{:S(2)}, u32[]{:S(2)}) collective-permute-start(bf16[20,16,256]{2,1,0:T(8,128)(2,1)S(1)} %get-tuple-element.19.own), channel_id=1, source_target_pairs={{0,248},{8,0},{16,8},{24,16},{32,24},{40,32},{48,40},{56,48},{64,5... | collective-permute-start | bytes 491528 | tf_op jit(solution)/shard_map/ppermute | solution.py:19
  79.0 4.0 %collective-permute-start.6 = (bf16[20,16,256]{2,1,0:T(8,128)(2,1)S(1)}, bf16[20,16,256]{2,1,0:T(8,128)(2,1)S(1)}, u32[]{:S(2)}, u32[]{:S(2)}) collective-permute-start(bf16[20,16,256]{2,1,0:T(8,128)(2,1)S(1)} %get-tuple-element.19.own), channel_id=1, source_target_pairs={{0,8},{8,16},{16,24},{24,32},{32,40},{40,48},{48,56},{56,64},{64,7... | collective-permute-start | bytes 491528 | tf_op jit(solution)/shard_map/ppermute | solution.py:19
  82.9 0.3 convolution_convert_fusion
  83.3 1.7 collective-permute-done.7.east
  84.9 3.2 %collective-permute-done.6.west = bf16[20,16,256]{2,1,0:T(8,128)(2,1)S(1)} collective-permute-done((bf16[20,16,256]{2,1,0:T(8,128)(2,1)S(1)}, bf16[20,16,256]{2,1,0:T(8,128)(2,1)S(1)}, u32[]{:S(2)}, u32[]{:S(2)}) %collective-permute-start.6) | collective-permute-done | bytes 163872 | tf_op jit(solution)/shard_map/ppermute | solution.py:19
  88.1 3.1 %backward.1 = (bf16[256,256]{1,0:T(8,128)(2,1)S(1)}, bf16[16,16,256]{2,1,0:T(8,128)(2,1)}, bf16[256,256]{1,0:T(8,128)(2,1)S(1)}) custom-call(f32[22,2688]{1,0:T(8,128)S(1)} %fusion.5.vecs, bf16[20,16,256]{2,1,0:T(8,128)(2,1)S(1)} %get-tuple-element.19.own, bf16[20,16,256]{2,1,0:T(8,128)(2,1)S(1)} %collective-permute-done.6.west, ...), custom_call_target="tpu_custom_call" | custom-call | tf_op jit(solution)/shard_map/backward/pallas_call | solution.py:362
  91.2 0.3 convolution_convert_fusion.2
  91.4 0.4 convolution_convert_fusion.1
  91.8 0.1 pad_maximum_fusion
  91.9 0.1 constant_dynamic-slice_fusion
  92.0 2.8 %collective-permute-start.8 = (bf16[2560,128]{1,0:T(8,128)(2,1)S(1)}, bf16[2560,128]{1,0:T(8,128)(2,1)S(1)}, u32[]{:S(2)}, u32[]{:S(2)}) collective-permute-start(bf16[2560,128]{1,0:T(8,128)(2,1)S(1)} %constant_dynamic-slice_fusion), channel_id=1, source_target_pairs={{0,1},{1,0},{2,3},{3,2},{4,5},{5,4},{6,7},{7,6},{8,9},{9,8},{10,11... | collective-permute-start | bytes 1966088 | tf_op jit(solution)/shard_map/ppermute | solution.py:19
  94.8 1.7 collective-permute-done.8
  96.5 0.2 add_convert_fusion
  96.7 18.7 %all_to_all.25 = bf16[4,640,128]{2,1,0:T(8,128)(2,1)S(1)} all-to-all(bf16[4,640,128]{2,1,0:T(8,128)(2,1)S(1)} %bitcast.63), channel_id=1, replica_groups=mesh['ens'=2,'lon'=32,'lat'=4,'ch'=2] {'lat'}, dimensions={0} | all-to-all | bytes 1310720 | tf_op jit(solution)/shard_map/all_to_all | solution.py:42
  115.4 0.1 reduce_sum.36
  115.5 13.4 %all_to_all.26 = bf16[8,80,128]{2,1,0:T(8,128)(2,1)S(1)} all-to-all(bf16[8,80,128]{2,1,0:T(8,128)(2,1)S(1)} %bitcast.66), channel_id=1, replica_groups={{224,232,240,248,0,8,16,24},{32,40,48,56,64,72,80,88},{96,104,112,120,1..., dimensions={0} | all-to-all | bytes 327680 | tf_op jit(solution)/shard_map/all_to_all | solution.py:42
  128.9 29.0 %all_to_all.27 = bf16[4,80,128]{2,1,0:T(8,128)(2,1)S(1)} all-to-all(bf16[4,80,128]{2,1,0:T(8,128)(2,1)S(1)} %broadcast_in_dim.20), channel_id=1, replica_groups={{224,32,96,160},{232,40,104,168},{240,48,112,176},{248,56,120,184},{0,6..., dimensions={0} | all-to-all | bytes 163840 | tf_op jit(solution)/shard_map/all_to_all | solution.py:42
  157.9 15.7 %all_to_all.28 = bf16[8,80,128]{2,1,0:T(8,128)(2,1)S(1)} all-to-all(bf16[8,80,128]{2,1,0:T(8,128)(2,1)S(1)} %broadcast_in_dim.36), channel_id=1, replica_groups={{224,232,240,248,0,8,16,24},{32,40,48,56,64,72,80,88},{96,104,112,120,1..., dimensions={0} | all-to-all | bytes 327680 | tf_op jit(solution)/shard_map/all_to_all | solution.py:42
  173.7 0.1 broadcast_in_dim.38
  173.8 11.2 %all_to_all.29 = bf16[4,640,128]{2,1,0:T(8,128)(2,1)S(1)} all-to-all(bf16[4,640,128]{2,1,0:T(8,128)(2,1)S(1)} %broadcast_in_dim.38), channel_id=1, replica_groups=mesh['ens'=2,'lon'=32,'lat'=4,'ch'=2] {'lat'}, dimensions={0} | all-to-all | bytes 1310720 | tf_op jit(solution)/shard_map/all_to_all | solution.py:42
  185.0 0.1 bitcast_convert_fusion
  185.1 0.7 slice_multiply_fusion.1
  185.8 1.0 slice_multiply_fusion
  (24 shorter events, 0.3 us)
Async XLA Ops:
  0.6 60.3 %copy-start = (bf16[512,256]{1,0:T(8,128)(2,1)S(1)}, bf16[512,256]{1,0:T(8,128)(2,1)}, u32[]{:S(2)}) copy-start(bf16[512,256]{1,0:T(8,128)(2,1)} %param.13) | copy-start | bytes 786436
  0.6 52.6 %copy-start.3 = (bf16[32,32,128]{2,1,0:T(8,128)(2,1)S(1)}, bf16[32,32,128]{2,1,0:T(8,128)(2,1)}, u32[]{:S(2)}) copy-start(bf16[32,32,128]{2,1,0:T(8,128)(2,1)} %field.1) | copy-start | bytes 786436
  0.7 52.6 %copy-start.2 = (bf16[16,16,256]{2,1,0:T(8,128)(2,1)S(1)}, bf16[16,16,256]{2,1,0:T(8,128)(2,1)}, u32[]{:S(2)}) copy-start(bf16[16,16,256]{2,1,0:T(8,128)(2,1)} %cot.1) | copy-start | bytes 393220
  2.5 50.7 %collective-permute-start = (bf16[160,256]{1,0:T(8,128)(2,1)S(1)}, bf16[160,256]{1,0:T(8,128)(2,1)S(1)}, u32[]{:S(2)}, u32[]{:S(2)}) collective-permute-start(bf16[160,256]{1,0:T(8,128)(2,1)S(1)} %pad_maximum_fusion.1), channel_id=1, source_target_pairs={{0,8},{8,16},{16,24},{24,32},{32,40},{40,48},{48,56},{56,64},{64,7... | collective-permute-start | bytes 245768 | tf_op jit(solution)/shard_map/ppermute | solution.py:19
  7.3 46.0 %collective-permute-start.1 = (bf16[160,256]{1,0:T(8,128)(2,1)S(1)}, bf16[160,256]{1,0:T(8,128)(2,1)S(1)}, u32[]{:S(2)}, u32[]{:S(2)}) collective-permute-start(bf16[160,256]{1,0:T(8,128)(2,1)S(1)} %pad_maximum_fusion.2), channel_id=1, source_target_pairs={{0,248},{8,0},{16,8},{24,16},{32,24},{40,32},{48,40},{56,48},{64,5... | collective-permute-start | bytes 245768 | tf_op jit(solution)/shard_map/ppermute | solution.py:19
  54.3 2.9 %collective-permute-start.2 = (bf16[120,512]{1,0:T(8,128)(2,1)S(1)}, bf16[120,512]{1,0:T(8,128)(2,1)S(1)}, u32[]{:S(2)}, u32[]{:S(2)}) collective-permute-start(bf16[120,512]{1,0:T(8,128)(2,1)S(1)} %get-tuple-element.15), channel_id=1, source_target_pairs={{0,1},{1,2},{2,3},{3,4},{4,5},{5,6},{6,7},{8,9},{9,10},{10,11},{11... | collective-permute-start | bytes 368648 | tf_op jit(solution)/shard_map/ppermute | solution.py:25
  55.9 4.9 %collective-permute-start.3 = (bf16[120,512]{1,0:T(8,128)(2,1)S(1)}, bf16[120,512]{1,0:T(8,128)(2,1)S(1)}, u32[]{:S(2)}, u32[]{:S(2)}) collective-permute-start(bf16[120,512]{1,0:T(8,128)(2,1)S(1)} %get-tuple-element.16), channel_id=1, source_target_pairs={{1,0},{2,1},{3,2},{4,3},{5,4},{6,5},{7,6},{9,8},{10,9},{11,10},{12... | collective-permute-start | bytes 368648 | tf_op jit(solution)/shard_map/ppermute | solution.py:25
  60.8 6.7 %copy-start.4 = (bf16[204,2688]{1,0:T(8,128)(2,1)S(1)}, bf16[204,2688]{1,0:T(8,128)(2,1)}, u32[]{:S(2)}) copy-start(bf16[204,2688]{1,0:T(8,128)(2,1)} %constant.42.clone) | copy-start | bytes 3290116
  61.2 13.1 %copy-start.1 = (bf16[2,1024,256]{2,1,0:T(8,128)(2,1)S(1)}, bf16[2,1024,256]{2,1,0:T(8,128)(2,1)}, u32[]{:S(2)}) copy-start(bf16[2,1024,256]{2,1,0:T(8,128)(2,1)} %weights.3) | copy-start | bytes 3145732
  61.2 7.7 %collective-permute-start.5 = (bf16[24,16,256]{2,1,0:T(8,128)(2,1)S(1)}, bf16[24,16,256]{2,1,0:T(8,128)(2,1)S(1)}, u32[]{:S(2)}, u32[]{:S(2)}) collective-permute-start(bf16[24,16,256]{2,1,0:T(8,128)(2,1)S(1)} %bitcast.58), channel_id=1, source_target_pairs={{0,248},{8,0},{16,8},{24,16},{32,24},{40,32},{48,40},{56,48},{64,5... | collective-permute-start | bytes 589832 | tf_op jit(solution)/shard_map/ppermute | solution.py:19
  65.5 8.8 %collective-permute-start.4 = (bf16[24,16,256]{2,1,0:T(8,128)(2,1)S(1)}, bf16[24,16,256]{2,1,0:T(8,128)(2,1)S(1)}, u32[]{:S(2)}, u32[]{:S(2)}) collective-permute-start(bf16[24,16,256]{2,1,0:T(8,128)(2,1)S(1)} %bitcast.59), channel_id=1, source_target_pairs={{0,8},{8,16},{16,24},{24,32},{32,40},{40,48},{48,56},{56,64},{64,7... | collective-permute-start | bytes 589832 | tf_op jit(solution)/shard_map/ppermute | solution.py:19
  77.0 7.9 %collective-permute-start.7 = (bf16[20,16,256]{2,1,0:T(8,128)(2,1)S(1)}, bf16[20,16,256]{2,1,0:T(8,128)(2,1)S(1)}, u32[]{:S(2)}, u32[]{:S(2)}) collective-permute-start(bf16[20,16,256]{2,1,0:T(8,128)(2,1)S(1)} %get-tuple-element.19.own), channel_id=1, source_target_pairs={{0,248},{8,0},{16,8},{24,16},{32,24},{40,32},{48,40},{56,48},{64,5... | collective-permute-start | bytes 491528 | tf_op jit(solution)/shard_map/ppermute | solution.py:19
  79.0 9.1 %collective-permute-start.6 = (bf16[20,16,256]{2,1,0:T(8,128)(2,1)S(1)}, bf16[20,16,256]{2,1,0:T(8,128)(2,1)S(1)}, u32[]{:S(2)}, u32[]{:S(2)}) collective-permute-start(bf16[20,16,256]{2,1,0:T(8,128)(2,1)S(1)} %get-tuple-element.19.own), channel_id=1, source_target_pairs={{0,8},{8,16},{16,24},{24,32},{32,40},{40,48},{48,56},{56,64},{64,7... | collective-permute-start | bytes 491528 | tf_op jit(solution)/shard_map/ppermute | solution.py:19
  92.0 4.5 %collective-permute-start.8 = (bf16[2560,128]{1,0:T(8,128)(2,1)S(1)}, bf16[2560,128]{1,0:T(8,128)(2,1)S(1)}, u32[]{:S(2)}, u32[]{:S(2)}) collective-permute-start(bf16[2560,128]{1,0:T(8,128)(2,1)S(1)} %constant_dynamic-slice_fusion), channel_id=1, source_target_pairs={{0,1},{1,0},{2,3},{3,2},{4,5},{5,4},{6,7},{7,6},{8,9},{9,8},{10,11... | collective-permute-start | bytes 1966088 | tf_op jit(solution)/shard_map/ppermute | solution.py:19
